TPU v7x, 32 devices: a whole 2x2x4 slice. The times are simulated.
32 devices in a mesh: group: 2 (over core), blk: 16 (over z, y, x).
Axes of the slice: x: 2, y: 2, z: 4, core: 2. Of those that a mesh axis runs over, the one named last changes fastest.
Arguments:
- field: float32 [2, 16, 5, 32, 512], P('group', 'blk'), may hold values from -6 to 6
- source: float32 [2, 16, 5, 32, 512], P('group', 'blk'), may hold values from -6 to 6
- block_inverse: float32 [2, 16, 5, 5, 32, 512], P('group', 'blk'), may hold values from -0.05 to 0.14, as said below
- coupling: float32 [2, 16, 4, 32, 512], P('group', 'blk'), may hold values from 0.3 to 1.2
- donor_base: int32 [2, 16, 16, 256], P('group', 'blk'), may hold values from 0 to 15870
- donor_weight: float32 [2, 16, 4, 16, 256], P('group', 'blk'), may hold values from 0 to 1, as said below
- receiver_cell: int32 [2, 16, 16, 256], P('group', 'blk'), may hold values from 0 to 16384, as said below
Outputs:
- field_out: float32 [2, 16, 5, 32, 512], P('group', 'blk')
Inputs may be any that keep to these rules, and one draw needn't show every extreme that they name: `block_inverse`: the entries of a block diagonal lie in 0.06 to 0.14; other entries are at most 0.05 in magnitude. `donor_weight`: the four weights of a slot are positive and sum to one. `receiver_cell`: within one block all entries below 16384 are distinct cells; for each donor block the used slots come first and the rest hold 16384; in every block some donor block fills all 256 slots.
All inputs are finite; a program needn't handle non-finite values.
Results may differ from a plain program's by a relative error of at most 0.0003.
Values sent between devices are 32-bit elements; how exact they have to be, the bound alone decides.
No kernel may reach another device: no remote copies, remote signals or barrier semaphores. Data moves between devices by JAX's collectives and lax.ppermute only.
A program may use at most 128 MiB of HBM per device.

v0:
```python
from functools import partial

import jax
import jax.numpy as jnp
from jax import lax
from jax.sharding import PartitionSpec as P

ITERS = 4


upwind_offsets = (-3, -2, -1, 0, 1, 2)
upwind_weights = (-2.0 / 60.0, 15.0 / 60.0, -60.0 / 60.0, 20.0 / 60.0, 30.0 / 60.0, -3.0 / 60.0)


def padded_2(block, sides, width):
    for axis, dim in sides:
        count = lax.axis_size(axis)
        forward = [(i, i + 1) for i in range(count - 1)]
        backward = [(target, source) for source, target in forward]
        low = lax.ppermute(
            lax.slice_in_dim(block, block.shape[dim] - width, None, axis=dim), axis, forward
        )
        high = lax.ppermute(lax.slice_in_dim(block, 0, width, axis=dim), axis, backward)
        block = jnp.concatenate([low, block, high], axis=dim)
    return block


def window(padded, shift_j, shift_k, row_count, column_count):
    return padded[
        :, 3 + shift_j : 3 + shift_j + row_count, 3 + shift_k : 3 + shift_k + column_count
    ]


def near_half(padded, solution, forcing, inverse, coupling, update_mask):
    row_count, column_count = (solution.shape[1], solution.shape[2])
    gathered = coupling[0] * window(padded, -1, 0, row_count, column_count)
    gathered = gathered + coupling[1] * window(padded, 1, 0, row_count, column_count)
    gathered = gathered + coupling[2] * window(padded, 0, -1, row_count, column_count)
    gathered = gathered + coupling[3] * window(padded, 0, 1, row_count, column_count)
    total = forcing + gathered
    updated = jnp.sum(inverse * total[None], axis=1)
    return jnp.where(update_mask[None], updated, solution)


def off_section(padded, solution, forcing, inverse, coupling, update_mask):
    row_count, column_count = (solution.shape[1], solution.shape[2])
    along_j = jnp.zeros_like(solution)
    along_k = jnp.zeros_like(solution)
    for offset, weight in zip(upwind_offsets, upwind_weights):
        along_j = along_j + weight * window(padded, offset, 0, row_count, column_count)
        along_k = along_k + weight * window(padded, 0, offset, row_count, column_count)
    residual_term = forcing - coupling[0] * along_j - coupling[1] * along_k
    updated = solution + jnp.sum(inverse * residual_term[None], axis=1)
    return jnp.where(update_mask[None], updated, solution)


def interpolate(flat_state, row_bases, weights, column_count):
    cell_count = flat_state.shape[1]
    width = flat_state.shape[0]
    cell_major = jnp.pad(flat_state.T, ((0, column_count + 1), (0, 0)))
    corner_table = jnp.concatenate(
        [
            cell_major[0:cell_count],
            cell_major[1 : cell_count + 1],
            cell_major[column_count : column_count + cell_count],
            cell_major[column_count + 1 : column_count + 1 + cell_count],
        ],
        axis=1,
    )
    picked = jnp.take(corner_table, row_bases, axis=0)
    result = jnp.zeros((row_bases.shape[0], width), jnp.float32)
    for corner in range(4):
        result = (
            result
            + weights[corner].reshape(-1)[:, None]
            * picked[:, corner * width : (corner + 1) * width]
        )
    return result.T


def on_device(field, source, block_inverse, coupling, donor_base, donor_weight, receiver_cell):
    solution = field[0, 0]
    forcing = source[0, 0]
    inverse = block_inverse[0, 0]
    factors = coupling[0, 0]
    bases = donor_base[0, 0]
    weights = donor_weight[0, 0]
    targets = receiver_cell[0, 0].reshape(-1)
    width = solution.shape[0]
    row_count = solution.shape[1]
    column_count = solution.shape[2]
    cell_count = row_count * column_count
    block_count = bases.shape[0]
    slot_count = bases.shape[1]
    slot_total = block_count * slot_count
    row_bases = bases.reshape(-1)
    slot_of_cell = (
        jnp.full((cell_count,), slot_total, jnp.int32)
        .at[targets]
        .set(jnp.arange(slot_total, dtype=jnp.int32), mode="drop")
    )
    frozen_flat = slot_of_cell < slot_total
    movable = jnp.logical_not(frozen_flat).reshape(row_count, column_count)
    parity_grid = (
        lax.broadcasted_iota(jnp.int32, (row_count, column_count), 0)
        + lax.broadcasted_iota(jnp.int32, (row_count, column_count), 1)
    ) % 2
    group_index = lax.axis_index("group")
    is_near = group_index == 0
    for iteration in range(ITERS):
        flat_state = solution.reshape(width, cell_count)
        donor_values = interpolate(flat_state, row_bases, weights, column_count).reshape(
            width, block_count, slot_count
        )
        partner_start = (1 - group_index) * block_count
        buffer = jnp.zeros((width, 2 * block_count, slot_count), jnp.float32)
        buffer = lax.dynamic_update_slice_in_dim(buffer, donor_values, partner_start, 1)
        arrived = lax.all_to_all(buffer, ("group", "blk"), split_axis=1, concat_axis=1, tiled=True)
        arrived = lax.dynamic_slice_in_dim(arrived, partner_start, block_count, 1)
        arrived_rows = jnp.pad(arrived.reshape(width, slot_total).T, ((0, 1), (0, 0)))
        placed = jnp.take(arrived_rows, slot_of_cell, axis=0).T
        flat_state = jnp.where(frozen_flat[None], placed, flat_state)
        solution = flat_state.reshape(solution.shape)
        for parity in range(2):
            padded = padded_2(solution, (("blk", 1),), 3)
            padded = jnp.pad(padded, ((0, 0), (0, 0), (3, 3)))
            near_mask = movable & (parity_grid == parity)
            solution = lax.cond(
                is_near,
                partial(near_half, update_mask=near_mask),
                partial(off_section, update_mask=movable),
                padded,
                solution,
                forcing,
                inverse,
                factors,
            )
    return solution[None, None]


def solution(mesh):
    in_specs = (
        P("group", "blk", None, None, None),
        P("group", "blk", None, None, None),
        P("group", "blk", None, None, None, None),
        P("group", "blk", None, None, None),
        P("group", "blk", None, None),
        P("group", "blk", None, None, None),
        P("group", "blk", None, None),
    )
    out_specs = P("group", "blk", None, None, None)
    return jax.shard_map(
        on_device, mesh=mesh, in_specs=in_specs, out_specs=out_specs, check_vma=False
    )
```

profile of v0, /device:TPU:0, one launch (start us, length us, event | category | flops | bytes accessed | tf_op | source)
XLA Modules:
  0.0 699.7 jit_solution(11789145775844393312)
XLA Ops:
  0.8 5.9 copy.118
  6.7 16.9 %pad_slice_fusion.11 = (f32[16384,5]{1,0:T(8,128)}, f32[16384,5]{1,0:T(8,128)}, f32[16384,5]{1,0:T(8,128)}) fusion(f32[16384,5]{1,0:T(8,128)} %bitcast.190), kind=kLoop, calls=%fused_computation.111 | loop fusion | bytes 1310720 | tf_op jit(solution)/shard_map/slice | solution.py:64
  23.6 17.0 %pad_maximum_fusion = f32[16384,20]{1,0:T(8,128)} fusion(f32[16384,5]{1,0:T(8,128)} %get-tuple-element.626, f32[16384,5]{1,0:T(8,128)} %get-tuple-element.625, f32[16384,5]{1,0:T(8,128)} %get-tuple-element.624, f32[16384,5]{1,0:T(8,128)} %bitcast.191), kind=kLoop, calls=%fused_computation.92 | loop fusion | flops 983040 | bytes 2621440 | tf_op jit(solution)/shard_map/concatenate | solution.py:61
  40.6 14.2 %gather_fusion = f32[4096,20]{1,0:T(8,128)S(1)} fusion(f32[16384,20]{1,0:T(8,128)} %pad_maximum_fusion, s32[4096]{0:T(1024)S(1)} %fusion.21), kind=kCustom, calls=%fused_computation.clone | custom fusion | bytes 671744 | tf_op jit(solution)/shard_map/jit(_take)/gather | solution.py:70
  57.0 7.3 %all-to-all-start = ((f32[5,32,256]{2,0,1:T(8,128)}), f32[5,32,256]{2,0,1:T(8,128)S(1)}, u32[]{:S(2)}, u32[]{:S(2)}) async-start(f32[5,32,256]{2,0,1:T(8,128)} %constant_dynamic-update-slice_fusion.3), calls=%async_computation | async-start | bytes 524288 | tf_op jit(solution)/shard_map/all_to_all | solution.py:118
  64.5 15.6 %scatter_custom_fusion = s32[16384]{0:T(1024)S(1)} fusion(s32[4096]{0:T(1024)S(1)} %bitcast.270, s32[4096]{0:T(1024)S(1)} %iota.17, s32[]{:T(128)} %constant.157.clone.1), kind=kCustom, calls=%fused_computation.178 | custom fusion | bytes 65540 | tf_op jit(solution)/shard_map/scatter | solution.py:100
  83.9 54.4 %gather_fusion.1 = f32[16384,5]{1,0:T(8,128)} fusion(f32[4097,5]{1,0:T(8,128)S(1)} %pad.52, s32[16384]{0:T(1024)S(1)} %fusion.18), kind=kCustom, calls=%fused_computation.1.clone | custom fusion | bytes 720896 | tf_op jit(solution)/shard_map/jit(_take)/gather | solution.py:121
  138.3 9.5 %bitcast_select_fusion.3 = f32[5,16384]{0,1:T(8,128)} fusion(f32[1,1,5,32,512]{2,4,3,1,0:T(8,128)} %copy.118, f32[16384,5]{1,0:T(8,128)} %gather_fusion.1, pred[16384]{0:T(1024)(128)(4,1)S(1)} %get-tuple-element.643, pred[16384]{0:T(1024)(128)(4,1)S(1)} %get-tuple-element.566), kind=kLoop, calls=%fused_computation.99 | loop fusion | flops 163840 | bytes 1015808 | tf_op jit(solution)/shard_map/jit(_where)/select_n | solution.py:122
  147.8 5.4 copy.122
  158.6 4.2 collective-permute-done.1
  163.1 6.5 conditional.8
  163.9 5.3 copy.126
  169.7 4.3 collective-permute-start.2
  175.7 4.2 collective-permute-done.3
  182.7 4.8 copy.127
  187.4 16.9 %pad_slice_fusion.8 = (f32[16384,5]{1,0:T(8,128)}, f32[16384,5]{1,0:T(8,128)}, f32[16384,5]{1,0:T(8,128)}) fusion(f32[16384,5]{1,0:T(8,128)} %bitcast.206), kind=kLoop, calls=%fused_computation.108 | loop fusion | bytes 1310720 | tf_op jit(solution)/shard_map/slice | solution.py:64
  204.3 17.0 %pad_maximum_fusion.1 = f32[16384,20]{1,0:T(8,128)} fusion(f32[16384,5]{1,0:T(8,128)} %get-tuple-element.623, f32[16384,5]{1,0:T(8,128)} %get-tuple-element.622, f32[16384,5]{1,0:T(8,128)} %get-tuple-element.621, f32[16384,5]{1,0:T(8,128)} %bitcast.207), kind=kLoop, calls=%fused_computation.93 | loop fusion | flops 983040 | bytes 2621440 | tf_op jit(solution)/shard_map/concatenate | solution.py:61
  221.4 14.2 %gather_fusion.2 = f32[4096,20]{1,0:T(8,128)S(1)} fusion(f32[16384,20]{1,0:T(8,128)} %pad_maximum_fusion.1, s32[4096]{0:T(1024)S(1)} %copy-done.42), kind=kCustom, calls=%fused_computation.2.clone | custom fusion | bytes 671744 | tf_op jit(solution)/shard_map/jit(_take)/gather | solution.py:70
  238.2 16.8 %all_to_all.20 = f32[5,32,256]{2,0,1:T(8,128)S(1)} all-to-all(f32[5,32,256]{2,0,1:T(8,128)S(1)} %constant_dynamic-update-slice_fusion.2), channel_id=1, replica_groups=mesh['group'=2,'blk'=16] {'group','blk'}, dimensions={1} | all-to-all | bytes 327680 | tf_op jit(solution)/shard_map/all_to_all | solution.py:118
  258.7 54.4 %gather_fusion.3 = f32[16384,5]{1,0:T(8,128)} fusion(f32[4097,5]{1,0:T(8,128)S(1)} %pad.56, s32[16384]{0:T(1024)S(1)} %copy-done.7), kind=kCustom, calls=%fused_computation.5.clone | custom fusion | bytes 720896 | tf_op jit(solution)/shard_map/jit(_take)/gather | solution.py:121
  313.1 9.5 %bitcast_select_fusion.2 = f32[5,16384]{0,1:T(8,128)} fusion(f32[5,32,512]{0,2,1:T(8,128)} %copy.127, f32[16384,5]{1,0:T(8,128)} %gather_fusion.3, pred[16384]{0:T(1024)(128)(4,1)S(1)} %copy-done.15, pred[16384]{0:T(1024)(128)(4,1)S(1)} %copy-done.11), kind=kLoop, calls=%fused_computation.98 | loop fusion | flops 163840 | bytes 1015808 | tf_op jit(solution)/shard_map/jit(_where)/select_n | solution.py:122
  322.6 5.4 copy.131
  331.9 4.2 collective-permute-done.5
  336.4 6.2 conditional.10
  337.3 5.3 copy.135
  348.6 4.2 collective-permute-done.7
  355.6 4.8 copy.136
  360.4 16.9 %pad_slice_fusion.5 = (f32[16384,5]{1,0:T(8,128)}, f32[16384,5]{1,0:T(8,128)}, f32[16384,5]{1,0:T(8,128)}) fusion(f32[16384,5]{1,0:T(8,128)} %bitcast.208), kind=kLoop, calls=%fused_computation.105 | loop fusion | bytes 1310720 | tf_op jit(solution)/shard_map/slice | solution.py:64
  377.3 17.0 %pad_maximum_fusion.2 = f32[16384,20]{1,0:T(8,128)} fusion(f32[16384,5]{1,0:T(8,128)} %get-tuple-element.620, f32[16384,5]{1,0:T(8,128)} %get-tuple-element.619, f32[16384,5]{1,0:T(8,128)} %get-tuple-element.618, f32[16384,5]{1,0:T(8,128)} %bitcast.209), kind=kLoop, calls=%fused_computation.94 | loop fusion | flops 983040 | bytes 2621440 | tf_op jit(solution)/shard_map/concatenate | solution.py:61
  394.3 14.2 %gather_fusion.4 = f32[4096,20]{1,0:T(8,128)S(1)} fusion(f32[16384,20]{1,0:T(8,128)} %pad_maximum_fusion.2, s32[4096]{0:T(1024)S(1)} %copy-done.43), kind=kCustom, calls=%fused_computation.3.clone | custom fusion | bytes 671744 | tf_op jit(solution)/shard_map/jit(_take)/gather | solution.py:70
  411.1 15.8 %all_to_all.21 = f32[5,32,256]{2,0,1:T(8,128)S(1)} all-to-all(f32[5,32,256]{2,0,1:T(8,128)S(1)} %constant_dynamic-update-slice_fusion.1), channel_id=1, replica_groups=mesh['group'=2,'blk'=16] {'group','blk'}, dimensions={1} | all-to-all | bytes 327680 | tf_op jit(solution)/shard_map/all_to_all | solution.py:118
  430.6 54.4 %gather_fusion.5 = f32[16384,5]{1,0:T(8,128)} fusion(f32[4097,5]{1,0:T(8,128)S(1)} %pad.60, s32[16384]{0:T(1024)S(1)} %copy-done.8), kind=kCustom, calls=%fused_computation.6.clone | custom fusion | bytes 720896 | tf_op jit(solution)/shard_map/jit(_take)/gather | solution.py:121
  485.0 9.5 %bitcast_select_fusion.1 = f32[5,16384]{0,1:T(8,128)} fusion(f32[5,32,512]{0,2,1:T(8,128)} %copy.136, f32[16384,5]{1,0:T(8,128)} %gather_fusion.5, pred[16384]{0:T(1024)(128)(4,1)S(1)} %copy-done.16, pred[16384]{0:T(1024)(128)(4,1)S(1)} %copy-done.12), kind=kLoop, calls=%fused_computation.97 | loop fusion | flops 163840 | bytes 1015808 | tf_op jit(solution)/shard_map/jit(_where)/select_n | solution.py:122
  494.5 5.4 copy.140
  503.8 4.2 collective-permute-done.9
  508.3 6.2 conditional.12
  509.3 5.3 copy.144
  527.6 4.8 copy.145
  532.3 16.9 %pad_slice_fusion.2 = (f32[16384,5]{1,0:T(8,128)}, f32[16384,5]{1,0:T(8,128)}, f32[16384,5]{1,0:T(8,128)}) fusion(f32[16384,5]{1,0:T(8,128)} %bitcast.204), kind=kLoop, calls=%fused_computation.102 | loop fusion | bytes 1310720 | tf_op jit(solution)/shard_map/slice | solution.py:64
  549.2 17.0 %pad_maximum_fusion.3 = f32[16384,20]{1,0:T(8,128)} fusion(f32[16384,5]{1,0:T(8,128)} %get-tuple-element.617, f32[16384,5]{1,0:T(8,128)} %get-tuple-element.616, f32[16384,5]{1,0:T(8,128)} %get-tuple-element.615, f32[16384,5]{1,0:T(8,128)} %bitcast.205), kind=kLoop, calls=%fused_computation.95 | loop fusion | flops 983040 | bytes 2621440 | tf_op jit(solution)/shard_map/concatenate | solution.py:61
  566.3 14.2 %gather_fusion.6 = f32[4096,20]{1,0:T(8,128)S(1)} fusion(f32[16384,20]{1,0:T(8,128)} %pad_maximum_fusion.3, s32[4096]{0:T(1024)S(1)} %copy-done.44), kind=kCustom, calls=%fused_computation.4.clone | custom fusion | bytes 671744 | tf_op jit(solution)/shard_map/jit(_take)/gather | solution.py:70
  583.1 16.1 %all_to_all.22 = f32[5,32,256]{2,0,1:T(8,128)S(1)} all-to-all(f32[5,32,256]{2,0,1:T(8,128)S(1)} %constant_dynamic-update-slice_fusion), channel_id=1, replica_groups=mesh['group'=2,'blk'=16] {'group','blk'}, dimensions={1} | all-to-all | bytes 327680 | tf_op jit(solution)/shard_map/all_to_all | solution.py:118
  602.9 54.4 %gather_fusion.7 = f32[16384,5]{1,0:T(8,128)} fusion(f32[4097,5]{1,0:T(8,128)S(1)} %pad.64, s32[16384]{0:T(1024)S(1)} %copy-done.9), kind=kCustom, calls=%fused_computation.7.clone | custom fusion | bytes 720896 | tf_op jit(solution)/shard_map/jit(_take)/gather | solution.py:121
  657.2 9.5 %bitcast_select_fusion = f32[5,16384]{0,1:T(8,128)} fusion(f32[5,32,512]{0,2,1:T(8,128)} %copy.145, f32[16384,5]{1,0:T(8,128)} %gather_fusion.7, pred[16384]{0:T(1024)(128)(4,1)S(1)} %copy-done.17, pred[16384]{0:T(1024)(128)(4,1)S(1)} %copy-done.13), kind=kLoop, calls=%fused_computation.96 | loop fusion | flops 163840 | bytes 1015808 | tf_op jit(solution)/shard_map/jit(_where)/select_n | solution.py:122
  666.7 5.4 copy.149
  676.0 4.2 collective-permute-done.13
  680.5 6.0 conditional.14
  681.2 5.3 copy.153
  (228 shorter events, 90.9 us)
Async XLA Ops:
  0.7 39.8 %copy-start.41 = (s32[4096]{0:T(1024)}, s32[4096]{0:T(1024)S(1)}, u32[]{:S(2)}) copy-start(s32[4096]{0:T(1024)S(1)} %fusion.21) | copy-start | bytes 49156
  40.6 23.8 %copy-start.47 = (s32[1,1,16,256]{3,2,1,0:T(8,128)S(1)}, s32[1,1,16,256]{3,2,1,0:T(8,128)}, u32[]{:S(2)}) copy-start(s32[1,1,16,256]{3,2,1,0:T(8,128)} %param.33) | copy-start | bytes 49156
  55.4 26.7 %copy-start.21 = (f32[2,2,8,128]{3,1,2,0:T(2,128)}, f32[2,2,8,128]{3,1,2,0:T(2,128)S(1)}, u32[]{:S(2)}) copy-start(f32[2,2,8,128]{3,1,2,0:T(2,128)S(1)} %copy.155) | copy-start | bytes 49156
  55.5 26.7 %copy-start.25 = (f32[2,2,8,128]{3,1,2,0:T(2,128)}, f32[2,2,8,128]{3,1,2,0:T(2,128)S(1)}, u32[]{:S(2)}) copy-start(f32[2,2,8,128]{3,1,2,0:T(2,128)S(1)} %copy.157) | copy-start | bytes 49156
  55.5 26.7 %copy-start.29 = (f32[2,2,8,128]{3,1,2,0:T(2,128)}, f32[2,2,8,128]{3,1,2,0:T(2,128)S(1)}, u32[]{:S(2)}) copy-start(f32[2,2,8,128]{3,1,2,0:T(2,128)S(1)} %copy.158) | copy-start | bytes 49156
  55.5 26.6 %copy-start.33 = (f32[2,2,8,128]{3,1,2,0:T(2,128)}, f32[2,2,8,128]{3,1,2,0:T(2,128)S(1)}, u32[]{:S(2)}) copy-start(f32[2,2,8,128]{3,1,2,0:T(2,128)S(1)} %copy.159) | copy-start | bytes 49156
  57.0 23.1 %all-to-all-start = ((f32[5,32,256]{2,0,1:T(8,128)}), f32[5,32,256]{2,0,1:T(8,128)S(1)}, u32[]{:S(2)}, u32[]{:S(2)}) async-start(f32[5,32,256]{2,0,1:T(8,128)} %constant_dynamic-update-slice_fusion.3), calls=%async_computation | async-start | bytes 524288 | tf_op jit(solution)/shard_map/all_to_all | solution.py:118
  80.1 58.2 %copy-start.10 = (pred[16384]{0:T(1024)(128)(4,1)}, pred[16384]{0:T(1024)(128)(4,1)S(1)}, u32[]{:S(2)}) copy-start(pred[16384]{0:T(1024)(128)(4,1)S(1)} %get-tuple-element.566) | copy-start | bytes 49156
  80.1 58.2 %copy-start.14 = (pred[16384]{0:T(1024)(128)(4,1)}, pred[16384]{0:T(1024)(128)(4,1)S(1)}, u32[]{:S(2)}) copy-start(pred[16384]{0:T(1024)(128)(4,1)S(1)} %get-tuple-element.643) | copy-start | bytes 49156
  80.1 58.1 %copy-start.6 = (s32[16384]{0:T(1024)}, s32[16384]{0:T(1024)S(1)}, u32[]{:S(2)}) copy-start(s32[16384]{0:T(1024)S(1)} %fusion.18) | copy-start | bytes 196612
  153.2 5.3 collective-permute-start
  156.9 5.9 collective-permute-start.1
  158.3 21.9 %copy-start.18 = (pred[32,512]{1,0:T(8,128)(4,1)}, pred[32,512]{1,0:T(8,128)(4,1)S(1)}, u32[]{:S(2)}) copy-start(pred[32,512]{1,0:T(8,128)(4,1)S(1)} %get-tuple-element.648) | copy-start | bytes 49156
  169.7 5.9 collective-permute-start.2
  174.0 5.9 collective-permute-start.3
  204.3 17.0 %copy-start.42 = (s32[4096]{0:T(1024)S(1)}, s32[4096]{0:T(1024)}, u32[]{:S(2)}) copy-start(s32[4096]{0:T(1024)} %copy-done.41) | copy-start | bytes 49156
  221.4 16.6 %copy-start.26 = (f32[2,2,8,128]{3,1,2,0:T(2,128)S(1)}, f32[2,2,8,128]{3,1,2,0:T(2,128)}, u32[]{:S(2)}) copy-start(f32[2,2,8,128]{3,1,2,0:T(2,128)} %copy-done.25) | copy-start | bytes 49156
  221.4 16.6 %copy-start.30 = (f32[2,2,8,128]{3,1,2,0:T(2,128)S(1)}, f32[2,2,8,128]{3,1,2,0:T(2,128)}, u32[]{:S(2)}) copy-start(f32[2,2,8,128]{3,1,2,0:T(2,128)} %copy-done.29) | copy-start | bytes 49156
  221.4 16.6 %copy-start.34 = (f32[2,2,8,128]{3,1,2,0:T(2,128)S(1)}, f32[2,2,8,128]{3,1,2,0:T(2,128)}, u32[]{:S(2)}) copy-start(f32[2,2,8,128]{3,1,2,0:T(2,128)} %copy-done.33) | copy-start | bytes 49156
  235.6 23.1 %copy-start.7 = (s32[16384]{0:T(1024)S(1)}, s32[16384]{0:T(1024)}, u32[]{:S(2)}) copy-start(s32[16384]{0:T(1024)} %copy-done.6) | copy-start | bytes 196612
  258.7 54.4 %copy-start.11 = (pred[16384]{0:T(1024)(128)(4,1)S(1)}, pred[16384]{0:T(1024)(128)(4,1)}, u32[]{:S(2)}) copy-start(pred[16384]{0:T(1024)(128)(4,1)} %copy-done.10) | copy-start | bytes 49156
  258.7 54.4 %copy-start.15 = (pred[16384]{0:T(1024)(128)(4,1)S(1)}, pred[16384]{0:T(1024)(128)(4,1)}, u32[]{:S(2)}) copy-start(pred[16384]{0:T(1024)(128)(4,1)} %copy-done.14) | copy-start | bytes 49156
  328.0 3.9 collective-permute-start.4
  330.2 5.9 collective-permute-start.5
  336.4 16.7 %copy-start.19 = (pred[32,512]{1,0:T(8,128)(4,1)S(1)}, pred[32,512]{1,0:T(8,128)(4,1)}, u32[]{:S(2)}) copy-start(pred[32,512]{1,0:T(8,128)(4,1)} %copy-done.18) | copy-start | bytes 49156
  342.7 5.9 collective-permute-start.6
  346.9 5.9 collective-permute-start.7
  377.2 17.0 %copy-start.43 = (s32[4096]{0:T(1024)S(1)}, s32[4096]{0:T(1024)}, u32[]{:S(2)}) copy-start(s32[4096]{0:T(1024)} %copy-done.41) | copy-start | bytes 49156
  394.3 16.6 %copy-start.27 = (f32[2,2,8,128]{3,1,2,0:T(2,128)S(1)}, f32[2,2,8,128]{3,1,2,0:T(2,128)}, u32[]{:S(2)}) copy-start(f32[2,2,8,128]{3,1,2,0:T(2,128)} %copy-done.25) | copy-start | bytes 49156
  408.5 22.1 %copy-start.8 = (s32[16384]{0:T(1024)S(1)}, s32[16384]{0:T(1024)}, u32[]{:S(2)}) copy-start(s32[16384]{0:T(1024)} %copy-done.6) | copy-start | bytes 196612
  430.6 54.4 %copy-start.12 = (pred[16384]{0:T(1024)(128)(4,1)S(1)}, pred[16384]{0:T(1024)(128)(4,1)}, u32[]{:S(2)}) copy-start(pred[16384]{0:T(1024)(128)(4,1)} %copy-done.10) | copy-start | bytes 49156
  430.6 54.4 %copy-start.16 = (pred[16384]{0:T(1024)(128)(4,1)S(1)}, pred[16384]{0:T(1024)(128)(4,1)}, u32[]{:S(2)}) copy-start(pred[16384]{0:T(1024)(128)(4,1)} %copy-done.14) | copy-start | bytes 49156
  499.9 3.9 collective-permute-start.8
  502.1 5.9 collective-permute-start.9
  508.3 16.7 %copy-start.20 = (pred[32,512]{1,0:T(8,128)(4,1)S(1)}, pred[32,512]{1,0:T(8,128)(4,1)}, u32[]{:S(2)}) copy-start(pred[32,512]{1,0:T(8,128)(4,1)} %copy-done.18) | copy-start | bytes 49156
  514.7 5.9 collective-permute-start.10
  518.9 5.9 collective-permute-start.11
  549.2 17.0 %copy-start.44 = (s32[4096]{0:T(1024)S(1)}, s32[4096]{0:T(1024)}, u32[]{:S(2)}) copy-start(s32[4096]{0:T(1024)} %copy-done.41) | copy-start | bytes 49156
  566.3 16.6 %copy-start.28 = (f32[2,2,8,128]{3,1,2,0:T(2,128)S(1)}, f32[2,2,8,128]{3,1,2,0:T(2,128)}, u32[]{:S(2)}) copy-start(f32[2,2,8,128]{3,1,2,0:T(2,128)} %copy-done.25) | copy-start | bytes 49156
  566.3 16.6 %copy-start.32 = (f32[2,2,8,128]{3,1,2,0:T(2,128)S(1)}, f32[2,2,8,128]{3,1,2,0:T(2,128)}, u32[]{:S(2)}) copy-start(f32[2,2,8,128]{3,1,2,0:T(2,128)} %copy-done.29) | copy-start | bytes 49156
  566.3 16.6 %copy-start.36 = (f32[2,2,8,128]{3,1,2,0:T(2,128)S(1)}, f32[2,2,8,128]{3,1,2,0:T(2,128)}, u32[]{:S(2)}) copy-start(f32[2,2,8,128]{3,1,2,0:T(2,128)} %copy-done.33) | copy-start | bytes 49156
  580.5 22.4 %copy-start.9 = (s32[16384]{0:T(1024)S(1)}, s32[16384]{0:T(1024)}, u32[]{:S(2)}) copy-start(s32[16384]{0:T(1024)} %copy-done.6) | copy-start | bytes 196612
  602.8 54.4 %copy-start.13 = (pred[16384]{0:T(1024)(128)(4,1)S(1)}, pred[16384]{0:T(1024)(128)(4,1)}, u32[]{:S(2)}) copy-start(pred[16384]{0:T(1024)(128)(4,1)} %copy-done.10) | copy-start | bytes 49156
  602.8 54.4 %copy-start.17 = (pred[16384]{0:T(1024)(128)(4,1)S(1)}, pred[16384]{0:T(1024)(128)(4,1)}, u32[]{:S(2)}) copy-start(pred[16384]{0:T(1024)(128)(4,1)} %copy-done.14) | copy-start | bytes 49156
  672.1 3.8 collective-permute-start.12
  674.3 5.9 collective-permute-start.13
  686.6 5.9 collective-permute-start.14
  690.9 5.9 collective-permute-start.15
  (17 other events, 232.4 us)
where the time goes:
time: 709 us; the launch traced here: 700 us
  local copies, waits for them, and re-layouts  443 us (62%)
  other arithmetic  123 us (17%)
  blocking collectives  48.7 us (7%)
  starting transfers between devices  44.8 us (6%)
  waiting for transfers between devices  36.7 us (5%)
    gather x4, local copies, waits for them, and re-layouts, on_device(): placed = jnp.take(arrived_rows, slot_of_cell, axis=0).T  218 us
    concatenate x4, other arithmetic, interpolate(): jnp.concatenate([cell_major[0:cell_count], cell_major[1:cell_count + 1],...  68.1 us
    slice x4, local copies, waits for them, and re-layouts, interpolate(): cell_major[1:cell_count + 1]  67.6 us
    gather x8, local copies, waits for them, and re-layouts, interpolate(): picked = jnp.take(corner_table, row_bases, axis=0)  61.5 us
    all_to_all x3, blocking collectives, on_device(): lax.all_to_all(buffer, ('group', 'blk'), split_axis=1, concat_axis=1, til...  48.7 us
    select_n x4, other arithmetic, on_device(): flat_state = jnp.where(frozen_flat[None], placed, flat_state)  37.8 us
    ppermute x8, waiting for transfers between devices, padded_2(): lax.ppermute(lax.slice_in_dim(block, 0, width, axis=dim), axis, backward)  33.9 us
    ppermute x8, starting transfers between devices, padded_2(): lax.ppermute(lax.slice_in_dim(block, block.shape[dim] - width, None, axis...  27.1 us
  transfers between devices with their start and end apart: 17, of which 16 were waited for; matrix products, arithmetic and copies ran while one was open for 2% of the time, Pallas kernels for 0%

commit v1 on v0

v1 whole, which is shorter than its diff:
```python
from functools import partial

import jax
import jax.numpy as jnp
from jax import lax
from jax.experimental import pallas as pl
from jax.experimental.pallas import tpu as pltpu
from jax.sharding import PartitionSpec as P

ITERS = 4

upwind_offsets = (-3, -2, -1, 0, 1, 2)
upwind_weights = (-2.0 / 60.0, 15.0 / 60.0, -60.0 / 60.0, 20.0 / 60.0, 30.0 / 60.0, -3.0 / 60.0)

F32 = jnp.float32
BF16 = jnp.bfloat16
ROWS = 8
LOW, HIGH = 6, 4
LOW_DONE, HIGH_DONE = 3, 2
PAD = 2 * ROWS


def vmem(count):
    return [pl.BlockSpec(memory_space=pltpu.VMEM)] * count


def divmod_const(value, size):
    if size & (size - 1) == 0:
        return value >> (size.bit_length() - 1), value & (size - 1)
    quotient = lax.div(value, jnp.int32(size))
    return quotient, value - quotient * size


def one_hot(index, size):
    rows = lax.broadcasted_iota(jnp.int32, (size, index.shape[1]), 0)
    return jnp.where(rows == index, 1.0, 0.0).astype(BF16)


def split(value):
    high = value.astype(BF16)
    low = (value - high.astype(F32)).astype(BF16)
    return high, low


def donor_sums(state, base_ref, weight_ref, out_ref):
    comps, rows, cols = state.shape
    half = cols // 2
    flat = state.reshape(comps * rows, cols)
    stacked = jnp.concatenate(split(flat), axis=0)
    at = lax.broadcasted_iota(jnp.int32, (cols, cols), 0)
    to = lax.broadcasted_iota(jnp.int32, (cols, cols), 1)
    source_col = jnp.where(to < half, 2 * to, 2 * (to - half) + 1)
    order = jnp.where(at == source_col, 1.0, 0.0).astype(BF16)
    ordered = jnp.dot(stacked, order, preferred_element_type=F32).astype(BF16)
    even, odd = ordered[:, :half], ordered[:, half:]
    slots = base_ref.shape[1]
    row_iota = lax.broadcasted_iota(jnp.int32, (rows, slots), 0)

    def one(d, carry):
        base = base_ref[pl.ds(d, 1), :]
        w0 = weight_ref[0, pl.ds(d, 1), :]
        w1 = weight_ref[1, pl.ds(d, 1), :]
        w2 = weight_ref[2, pl.ds(d, 1), :]
        w3 = weight_ref[3, pl.ds(d, 1), :]
        row, col = divmod_const(base, cols)
        is_odd = (col & 1) == 1
        wraps = col == cols - 1
        odd_at = col >> 1
        even_at = jnp.where(wraps, 0, (col + 1) >> 1)
        even_row = row + jnp.where(wraps, 1, 0)
        picked_even = jnp.dot(even, one_hot(even_at, half), preferred_element_type=F32)
        picked_odd = jnp.dot(odd, one_hot(odd_at, half), preferred_element_type=F32)
        count = comps * rows
        picked_even = (picked_even[:count] + picked_even[count:]).reshape(comps, rows, slots)
        picked_odd = (picked_odd[:count] + picked_odd[count:]).reshape(comps, rows, slots)
        even_weight = jnp.where(
            row_iota == even_row,
            jnp.where(is_odd, w1, w0),
            jnp.where(row_iota == even_row + 1, jnp.where(is_odd, w3, w2), 0.0),
        )
        odd_weight = jnp.where(
            row_iota == row,
            jnp.where(is_odd, w0, w1),
            jnp.where(row_iota == row + 1, jnp.where(is_odd, w2, w3), 0.0),
        )
        total = even_weight[None] * picked_even + odd_weight[None] * picked_odd
        out_ref[d, 0:comps, :] = jnp.sum(total, axis=1)
        return carry

    lax.fori_loop(0, base_ref.shape[0], one, 0)


def spread(values_of, target_ref, comps, rows, cols, acc_ref, exact):
    slots = target_ref.shape[1]
    row_iota = lax.broadcasted_iota(jnp.int32, (rows, slots), 0)
    acc_ref[...] = jnp.zeros_like(acc_ref)

    def one(b, carry):
        row, col = divmod_const(target_ref[pl.ds(b, 1), :], cols)
        hit = row_iota == row
        columns = one_hot(col, cols)
        values = values_of(b)
        parts = [values] if exact else [values.astype(BF16).astype(F32)]
        if not exact:
            parts.append(values - parts[0])
        placed = [
            jnp.where(hit[None], part[:, None, :], 0.0).reshape(comps * rows, slots).astype(BF16)
            for part in parts
        ]
        left = jnp.concatenate(placed, axis=1)
        right = jnp.concatenate([columns] * len(parts), axis=1)
        acc_ref[...] += lax.dot_general(
            left, right, (((1,), (1,)), ((), ())), preferred_element_type=F32
        )
        return carry

    lax.fori_loop(0, target_ref.shape[0], one, 0)


def start_kernel(field_ref, base_ref, weight_ref, target_ref, out_ref, movable_ref, acc_ref):
    rows, cols = field_ref.shape[1:]
    donor_sums(field_ref[...], base_ref, weight_ref, out_ref)
    slots = target_ref.shape[1]
    spread(lambda b: jnp.ones((1, slots), F32), target_ref, 1, rows, cols, acc_ref, True)
    movable_ref[...] = jnp.where(acc_ref[...] > 0.5, 0.0, 1.0)


def place_kernel(arrived_ref, target_ref, state_ref, movable_ref, out_ref, top_ref, bottom_ref, acc_ref):
    comps, rows, cols = state_ref.shape
    spread(
        lambda b: arrived_ref[b, 0:comps, :], target_ref, comps, rows, cols, acc_ref, False
    )
    movable = movable_ref[...] > 0.5
    for c in range(comps):
        placed = acc_ref[c * rows : (c + 1) * rows, :]
        new = jnp.where(movable, state_ref[c], placed)
        out_ref[c] = new
        top_ref[c * LOW : (c + 1) * LOW, :] = new[rows - LOW :, :]
        bottom_ref[c * HIGH : (c + 1) * HIGH, :] = new[:HIGH, :]


def sections(u_ref, start, parts, write, is_near, parity, comps, cols):
    source, inverse, coupling, movable = parts
    lanes = lax.broadcasted_iota(jnp.int32, (ROWS, cols), 1)
    sublanes = lax.broadcasted_iota(jnp.int32, (ROWS, cols), 0)

    def rows_at(c, offset):
        return u_ref[c, start + offset : start + offset + ROWS, :]

    def shifted(value, offset):
        return pltpu.roll(value, (-offset) % cols, 1)

    def finish(update, terms, mask):
        for v in range(comps):
            total = update(v)
            for w in range(comps):
                product = inverse(v, w) * terms[w]
                total = product if total is None else total + product
            write(v, jnp.where(mask, total, rows_at(v, 0)))

    @pl.when(is_near)
    def _():
        c0, c1, c2, c3 = (coupling(i) for i in range(4))
        c2 = jnp.where(lanes >= 1, c2, 0.0)
        c3 = jnp.where(lanes < cols - 1, c3, 0.0)
        terms = []
        for w in range(comps):
            here = rows_at(w, 0)
            term = source(w) + c0 * rows_at(w, -1) + c1 * rows_at(w, 1)
            terms.append(term + c2 * shifted(here, -1) + c3 * shifted(here, 1))
        colour = ((lanes + sublanes) & 1) == parity
        finish(lambda v: None, terms, colour & (movable() > 0.5))

    @pl.when(jnp.logical_not(is_near))
    def _():
        c0, c1 = coupling(0), coupling(1)
        factors = []
        for offset, weight in zip(upwind_offsets, upwind_weights):
            inside = (lanes + offset >= 0) & (lanes + offset < cols)
            factors.append(weight if offset == 0 else jnp.where(inside, weight, 0.0))
        terms = []
        for w in range(comps):
            here = rows_at(w, 0)
            along_j = along_k = None
            for offset, weight, factor in zip(upwind_offsets, upwind_weights, factors):
                in_j = weight * rows_at(w, offset)
                in_k = factor * (here if offset == 0 else shifted(here, offset))
                along_j = in_j if along_j is None else along_j + in_j
                along_k = in_k if along_k is None else along_k + in_k
            terms.append(source(w) - c0 * along_j - c1 * along_k)
        finish(lambda v: rows_at(v, 0), terms, movable() > 0.5)


def sweep(
    state_ref, below_ref, above_ref, source_ref, inverse_ref, coupling_ref, movable_ref,
    low_ref, high_ref, u_ref, v_ref, out_ref,
):
    comps, rows, cols = state_ref.shape
    is_near = lax.axis_index("group") == 0
    for c in range(comps):
        u_ref[c, PAD : PAD + rows, :] = state_ref[c]
        u_ref[c, PAD - LOW : PAD, :] = below_ref[c * LOW : (c + 1) * LOW, :]
        u_ref[c, PAD + rows : PAD + rows + HIGH, :] = above_ref[c * HIGH : (c + 1) * HIGH, :]
        v_ref[c, 0:PAD, :] = jnp.zeros((PAD, cols), F32)
        v_ref[c, PAD + rows :, :] = jnp.zeros((PAD, cols), F32)

    def own(r):
        at = slice(r, r + ROWS)
        return (
            lambda w: source_ref[w, at, :],
            lambda v, w: inverse_ref[v, w, at, :],
            lambda i: coupling_ref[i, at, :],
            lambda: movable_ref[at, :],
        )

    def packed(ref):
        first = comps * comps
        second = first + comps
        last = ref.shape[0] - 1
        return (
            lambda w: ref[first + w],
            lambda v, w: ref[v * comps + w],
            lambda i: ref[second + i],
            lambda: ref[last],
        )

    def into(ref, start):
        def write(v, value):
            ref[v, start : start + ROWS, :] = value
        return write

    sections(u_ref, PAD - ROWS, packed(low_ref), into(v_ref, PAD - ROWS), is_near, 0, comps, cols)
    for r in range(0, rows, ROWS):
        sections(u_ref, PAD + r, own(r), into(v_ref, PAD + r), is_near, 0, comps, cols)
    sections(u_ref, PAD + rows, packed(high_ref), into(v_ref, PAD + rows), is_near, 0, comps, cols)
    for r in range(0, rows, ROWS):
        sections(v_ref, PAD + r, own(r), into(out_ref, r), is_near, 1, comps, cols)


def middle_kernel(
    state_ref, below_ref, above_ref, source_ref, inverse_ref, coupling_ref, movable_ref,
    low_ref, high_ref, base_ref, weight_ref, out_ref, sums_ref, u_ref, v_ref,
):
    sweep(
        state_ref, below_ref, above_ref, source_ref, inverse_ref, coupling_ref, movable_ref,
        low_ref, high_ref, u_ref, v_ref, out_ref,
    )
    donor_sums(out_ref[...], base_ref, weight_ref, sums_ref)


def last_kernel(
    state_ref, below_ref, above_ref, source_ref, inverse_ref, coupling_ref, movable_ref,
    low_ref, high_ref, out_ref, u_ref, v_ref,
):
    sweep(
        state_ref, below_ref, above_ref, source_ref, inverse_ref, coupling_ref, movable_ref,
        low_ref, high_ref, u_ref, v_ref, out_ref,
    )


def on_device(field, source, block_inverse, coupling, donor_base, donor_weight, receiver_cell):
    state = field[0, 0]
    source = source[0, 0]
    inverse = block_inverse[0, 0]
    coupling = coupling[0, 0]
    base = donor_base[0, 0]
    weight = donor_weight[0, 0]
    target = receiver_cell[0, 0]
    comps, rows, cols = state.shape
    blocks, slots = base.shape
    groups = lax.axis_size("group")
    swap = [(g * blocks + b, (groups - 1 - g) * blocks + b) for g in range(groups) for b in range(blocks)]
    up = [(b, b + 1) for b in range(blocks - 1)]
    down = [(b + 1, b) for b in range(blocks - 1)]

    def f32(*shape):
        return jax.ShapeDtypeStruct(shape, F32)

    params = pltpu.CompilerParams(vmem_limit_bytes=48 * 1024 * 1024)
    sums_shape = f32(blocks, -(-comps // ROWS) * ROWS, slots)

    sums, movable = pl.pallas_call(
        start_kernel,
        out_shape=(sums_shape, f32(rows, cols)),
        in_specs=vmem(4),
        out_specs=tuple(vmem(2)),
        scratch_shapes=[pltpu.VMEM((rows, cols), F32)],
        compiler_params=params,
        name="start",
    )(state, base, weight, target)

    def fixed_rows(at, count):
        return jnp.concatenate(
            [
                inverse[:, :, at : at + count].reshape(comps * comps, count, cols),
                source[:, at : at + count],
                coupling[:, at : at + count],
                movable[None, at : at + count],
            ],
            axis=0,
        )

    low = lax.ppermute(fixed_rows(rows - LOW_DONE, LOW_DONE), "blk", up)
    high = lax.ppermute(fixed_rows(0, HIGH_DONE), "blk", down)
    low = jnp.pad(low, ((0, 0), (ROWS - LOW_DONE, 0), (0, 0)))
    high = jnp.pad(high, ((0, 0), (0, ROWS - HIGH_DONE), (0, 0)))

    working = [pltpu.VMEM((comps, rows + 2 * PAD, cols), F32)] * 2
    for iteration in range(ITERS):
        arrived = lax.ppermute(sums, ("group", "blk"), swap)
        arrived = lax.all_to_all(arrived, "blk", split_axis=0, concat_axis=0, tiled=True)
        state, top, bottom = pl.pallas_call(
            place_kernel,
            out_shape=(f32(comps, rows, cols), f32(comps * LOW, cols), f32(comps * HIGH, cols)),
            in_specs=vmem(4),
            out_specs=tuple(vmem(3)),
            scratch_shapes=[pltpu.VMEM((comps * rows, cols), F32)],
            compiler_params=params,
            name="place",
        )(arrived, target, state, movable)
        below = lax.ppermute(top, "blk", up)
        above = lax.ppermute(bottom, "blk", down)
        operands = (state, below, above, source, inverse, coupling, movable, low, high)
        if iteration < ITERS - 1:
            state, sums = pl.pallas_call(
                middle_kernel,
                out_shape=(f32(comps, rows, cols), sums_shape),
                in_specs=vmem(11),
                out_specs=tuple(vmem(2)),
                scratch_shapes=working,
                compiler_params=params,
                name="middle",
            )(*operands, base, weight)
        else:
            state = pl.pallas_call(
                last_kernel,
                out_shape=f32(comps, rows, cols),
                in_specs=vmem(9),
                out_specs=vmem(1)[0],
                scratch_shapes=working,
                compiler_params=params,
                name="last",
            )(*operands)
    return state[None, None]


def solution(mesh):
    in_specs = (
        P("group", "blk", None, None, None),
        P("group", "blk", None, None, None),
        P("group", "blk", None, None, None, None),
        P("group", "blk", None, None, None),
        P("group", "blk", None, None),
        P("group", "blk", None, None, None),
        P("group", "blk", None, None),
    )
    out_specs = P("group", "blk", None, None, None)
    return jax.shard_map(
        on_device, mesh=mesh, in_specs=in_specs, out_specs=out_specs, check_vma=False
    )
```

time: 709 us -> 156 us (0.22); the launches traced: 700 us -> 155 us
  local copies, waits for them, and re-layouts: 443 us -> 8.2 us
  other arithmetic: 123 us -> 0.79 us
  Pallas kernels: 0 us -> 48.8 us
  starting transfers between devices: 44.8 us -> 29.7 us
  waiting for transfers between devices: 36.7 us -> 26.6 us
  blocking collectives: 48.7 us -> 41.1 us
    gather x12 -> x0, local copies, waits for them, and re-layouts: 279 us -> none  [the longest x4 218 us: on_device(): placed = jnp.take(arrived_rows, slot_of_cell, axis=0).T]
    concatenate x12 -> x2, other arithmetic: 70.2 us -> 0.79 us  [fixed_rows(): jnp.concatenate([inverse[:, :, at:at + count].reshape(comps * comps, coun...]
    slice x12 -> x6, local copies, waits for them, and re-layouts: 67.8 us -> 3.72 us  [the longest x2 1.79 us: fixed_rows(): source[:, at:at + count]]
    pallas_call x0 -> x9, Pallas kernels: none -> 48.8 us  [the longest x4 21.2 us: on_device(): pl.pallas_call(place_kernel, out_shape=(f32(comps, rows, cols), f32(comps...]
    select_n x16 -> x0, other arithmetic: 44.3 us -> none  [the longest x4 37.8 us: on_device(): flat_state = jnp.where(frozen_flat[None], placed, flat_state)]
    another operation x8 -> x0, local copies, waits for them, and re-layouts: 21.8 us -> none
    reshape x5 -> x0, local copies, waits for them, and re-layouts: 21.6 us -> none  [the longest x4 21.6 us: on_device(): solution = flat_state.reshape(solution.shape)]
    scatter x1 -> x0, local copies, waits for them, and re-layouts: 15.6 us -> none  [on_device(): slot_of_cell = jnp.full((cell_count,), slot_total, jnp.int32).at[targets]...]
  transfers between devices with their start and end apart: 17 -> 15, of which waited for: 16 -> 8; matrix products, arithmetic and copies ran while one was open for 2% -> 4% of each run, Pallas kernels for 0% -> 3%
where the time goes in v1:
time: 156 us; the launch traced here: 155 us
  Pallas kernels  48.8 us (31%)
  blocking collectives  41.1 us (26%)
  starting transfers between devices  29.7 us (19%)
  waiting for transfers between devices  26.6 us (17%)
  local copies, waits for them, and re-layouts  8.2 us (5%)
    all_to_all x3, blocking collectives, on_device(): lax.all_to_all(arrived, 'blk', split_axis=0, concat_axis=0, tiled=True)  41.1 us
    pallas_call x4, Pallas kernels, on_device(): pl.pallas_call(place_kernel, out_shape=(f32(comps, rows, cols), f32(comps...  21.2 us
    pallas_call x3, Pallas kernels, on_device(): pl.pallas_call(middle_kernel, out_shape=(f32(comps, rows, cols), sums_sha...  17.8 us
    ppermute x4, waiting for transfers between devices, on_device(): above = lax.ppermute(bottom, 'blk', down)  17.6 us
    ppermute x4, starting transfers between devices, on_device(): below = lax.ppermute(top, 'blk', up)  12 us
    pallas_call x1, Pallas kernels, on_device(): pl.pallas_call(start_kernel, out_shape=(sums_shape, f32(rows, cols)), in_...  7.73 us
    all_to_all x1, starting transfers between devices, on_device(): lax.all_to_all(arrived, 'blk', split_axis=0, concat_axis=0, tiled=True)  5.93 us
    ppermute x4, starting transfers between devices, on_device(): above = lax.ppermute(bottom, 'blk', down)  5.17 us
  transfers between devices with their start and end apart: 15, of which 8 were waited for; matrix products, arithmetic and copies ran while one was open for 4% of the time, Pallas kernels for 3%

profile of v1, /device:TPU:0, one launch (start us, length us, event | category | flops | bytes accessed | tf_op | source)
XLA Modules:
  0.0 155.4 jit_solution(17671061472169903701)
XLA Ops:
  0.0 1.1 copy-done.3
  1.1 0.8 copy-done.5
  2.0 0.7 copy-done.7
  2.7 0.7 copy-done.9
  3.4 7.7 %start.1 = (f32[16,8,256]{2,1,0:T(8,128)S(1)}, f32[32,512]{1,0:T(8,128)S(1)}) custom-call(f32[5,32,512]{2,1,0:T(8,128)S(1)} %bitcast.32, s32[16,256]{1,0:T(8,128)S(1)} %bitcast.43, f32[4,16,256]{2,1,0:T(8,128)S(1)} %bitcast.34, s32[16,256]{1,0:T(8,128)S(1)} %bitcast.38), custom_call_target="tpu_custom_call" | custom-call | tf_op jit(solution)/shard_map/start/pallas_call | solution.py:282
  11.1 0.6 collective-permute-start
  11.7 0.8 slice.34
  12.5 0.9 slice.33
  13.4 1.1 slice.32
  14.5 0.0 copy-start.10
  14.5 0.1 pad_maximum_fusion
  14.6 4.6 %collective-permute-start.3 = (f32[35,3,512]{2,1,0:T(4,128)S(1)}, f32[35,3,512]{2,1,0:T(4,128)S(1)}, u32[]{:S(2)}, u32[]{:S(2)}) collective-permute-start(f32[35,3,512]{2,1,0:T(4,128)S(1)} %pad_maximum_fusion), channel_id=1, source_target_pairs={{0,1},{1,2},{2,3},{3,4},{4,5},{5,6},{6,7},{7,8},{8,9},{9,10},{10,1... | collective-permute-start | bytes 645128 | tf_op jit(solution)/shard_map/ppermute | solution.py:303
  19.2 5.9 %all-to-all-start = ((f32[16,8,256]{2,1,0:T(8,128)}), f32[16,8,256]{2,1,0:T(8,128)S(1)}, u32[]{:S(2)}, u32[]{:S(2)}) async-start(f32[16,8,256]{2,1,0:T(8,128)} %collective-permute-done), calls=%async_computation | async-start | bytes 262144 | tf_op jit(solution)/shard_map/all_to_all | solution.py:311
  25.2 0.9 slice.36
  26.1 0.7 pad_maximum_fusion.1
  26.8 1.3 collective-permute-start.4
  28.1 4.9 %all-to-all-done.arrived_ref = f32[16,8,256]{2,1,0:T(8,128)S(1)} async-done(((f32[16,8,256]{2,1,0:T(8,128)}), f32[16,8,256]{2,1,0:T(8,128)S(1)}, u32[]{:S(2)}, u32[]{:S(2)}) %all-to-all-start) | async-done | bytes 131104 | tf_op jit(solution)/shard_map/all_to_all | solution.py:311
  33.0 5.3 %place.4 = (f32[5,32,512]{2,1,0:T(8,128)S(1)}, f32[30,512]{1,0:T(8,128)S(1)}, f32[20,512]{1,0:T(8,128)S(1)}) custom-call(f32[16,8,256]{2,1,0:T(8,128)S(1)} %all-to-all-done.arrived_ref, s32[16,256]{1,0:T(8,128)S(1)} %bitcast.39, f32[5,32,512]{2,1,0:T(8,128)S(1)} %bitcast.33, f32[32,512]{1,0:T(8,128)S(1)} %get-tuple-element.26.movable_ref), custom_call_target="tpu_custom_call" | custom-call | tf_op jit(solution)/shard_map/place/pallas_call | solution.py:312
  38.4 3.0 %collective-permute-start.1 = (f32[30,512]{1,0:T(8,128)S(1)}, f32[30,512]{1,0:T(8,128)S(1)}, u32[]{:S(2)}, u32[]{:S(2)}) collective-permute-start(f32[30,512]{1,0:T(8,128)S(1)} %get-tuple-element.28), channel_id=1, source_target_pairs={{0,1},{1,2},{2,3},{3,4},{4,5},{5,6},{6,7},{7,8},{8,9},{9,10},{10,1... | collective-permute-start | bytes 184328 | tf_op jit(solution)/shard_map/ppermute | solution.py:321
  41.3 1.3 collective-permute-start.2
  42.6 1.0 pad.9.high_ref
  43.6 0.1 pad.8.low_ref
  43.7 3.6 %collective-permute-done.2.above_ref = f32[20,512]{1,0:T(8,128)S(1)} collective-permute-done((f32[20,512]{1,0:T(8,128)S(1)}, f32[20,512]{1,0:T(8,128)S(1)}, u32[]{:S(2)}, u32[]{:S(2)}) %collective-permute-start.2) | collective-permute-done | bytes 40992 | tf_op jit(solution)/shard_map/ppermute | solution.py:322
  47.3 5.9 %middle.3 = (f32[5,32,512]{2,1,0:T(8,128)S(1)}, f32[16,8,256]{2,1,0:T(8,128)S(1)}) custom-call(f32[5,32,512]{2,1,0:T(8,128)S(1)} %get-tuple-element.27.state_ref, f32[30,512]{1,0:T(8,128)S(1)} %collective-permute-done.1.below_ref, f32[20,512]{1,0:T(8,128)S(1)} %collective-permute-done.2.above_ref, f32[5,32,512]{2,1,0:T(8,128)S(1)} %bitcast.22, ...), custom_call_target="tpu_custom_call" | custom-call | tf_op jit(solution)/shard_map/middle/pallas_call | solution.py:325
  53.2 0.1 collective-permute-start.5
  53.3 1.3 collective-permute-done.5
  54.6 13.9 %all_to_all.20.arrived_ref = f32[16,8,256]{2,1,0:T(8,128)S(1)} all-to-all(f32[16,8,256]{2,1,0:T(8,128)S(1)} %collective-permute-done.5), channel_id=1, replica_groups=mesh['group'=2,'blk'=16] {'blk'}, dimensions={0} | all-to-all | bytes 262144 | tf_op jit(solution)/shard_map/all_to_all | solution.py:311
  68.5 5.3 %place.5 = (f32[5,32,512]{2,1,0:T(8,128)S(1)}, f32[30,512]{1,0:T(8,128)S(1)}, f32[20,512]{1,0:T(8,128)S(1)}) custom-call(f32[16,8,256]{2,1,0:T(8,128)S(1)} %all_to_all.20.arrived_ref, s32[16,256]{1,0:T(8,128)S(1)} %bitcast.40, f32[5,32,512]{2,1,0:T(8,128)S(1)} %get-tuple-element.31.state_ref, f32[32,512]{1,0:T(8,128)S(1)} %get-tuple-element.26.movable_ref), custom_call_target="tpu_custom_call" | custom-call | tf_op jit(solution)/shard_map/place/pallas_call | solution.py:312
  73.8 3.0 %collective-permute-start.6 = (f32[30,512]{1,0:T(8,128)S(1)}, f32[30,512]{1,0:T(8,128)S(1)}, u32[]{:S(2)}, u32[]{:S(2)}) collective-permute-start(f32[30,512]{1,0:T(8,128)S(1)} %get-tuple-element.33), channel_id=1, source_target_pairs={{0,1},{1,2},{2,3},{3,4},{4,5},{5,6},{6,7},{7,8},{8,9},{9,10},{10,1... | collective-permute-start | bytes 184328 | tf_op jit(solution)/shard_map/ppermute | solution.py:321
  76.8 1.3 collective-permute-start.7
  78.1 4.7 %collective-permute-done.7.above_ref = f32[20,512]{1,0:T(8,128)S(1)} collective-permute-done((f32[20,512]{1,0:T(8,128)S(1)}, f32[20,512]{1,0:T(8,128)S(1)}, u32[]{:S(2)}, u32[]{:S(2)}) %collective-permute-start.7) | collective-permute-done | bytes 40992 | tf_op jit(solution)/shard_map/ppermute | solution.py:322
  82.8 5.9 %middle.4 = (f32[5,32,512]{2,1,0:T(8,128)S(1)}, f32[16,8,256]{2,1,0:T(8,128)S(1)}) custom-call(f32[5,32,512]{2,1,0:T(8,128)S(1)} %get-tuple-element.32.state_ref, f32[30,512]{1,0:T(8,128)S(1)} %collective-permute-done.6.below_ref, f32[20,512]{1,0:T(8,128)S(1)} %collective-permute-done.7.above_ref, f32[5,32,512]{2,1,0:T(8,128)S(1)} %bitcast.23, ...), custom_call_target="tpu_custom_call" | custom-call | tf_op jit(solution)/shard_map/middle/pallas_call | solution.py:325
  88.7 0.1 collective-permute-start.8
  88.8 1.3 collective-permute-done.8
  90.1 13.6 %all_to_all.21.arrived_ref = f32[16,8,256]{2,1,0:T(8,128)S(1)} all-to-all(f32[16,8,256]{2,1,0:T(8,128)S(1)} %collective-permute-done.8), channel_id=1, replica_groups=mesh['group'=2,'blk'=16] {'blk'}, dimensions={0} | all-to-all | bytes 262144 | tf_op jit(solution)/shard_map/all_to_all | solution.py:311
  103.7 5.3 %place.6 = (f32[5,32,512]{2,1,0:T(8,128)S(1)}, f32[30,512]{1,0:T(8,128)S(1)}, f32[20,512]{1,0:T(8,128)S(1)}) custom-call(f32[16,8,256]{2,1,0:T(8,128)S(1)} %all_to_all.21.arrived_ref, s32[16,256]{1,0:T(8,128)S(1)} %bitcast.41, f32[5,32,512]{2,1,0:T(8,128)S(1)} %get-tuple-element.36.state_ref, f32[32,512]{1,0:T(8,128)S(1)} %get-tuple-element.26.movable_ref), custom_call_target="tpu_custom_call" | custom-call | tf_op jit(solution)/shard_map/place/pallas_call | solution.py:312
  109.0 3.0 %collective-permute-start.9 = (f32[30,512]{1,0:T(8,128)S(1)}, f32[30,512]{1,0:T(8,128)S(1)}, u32[]{:S(2)}, u32[]{:S(2)}) collective-permute-start(f32[30,512]{1,0:T(8,128)S(1)} %get-tuple-element.38), channel_id=1, source_target_pairs={{0,1},{1,2},{2,3},{3,4},{4,5},{5,6},{6,7},{7,8},{8,9},{9,10},{10,1... | collective-permute-start | bytes 184328 | tf_op jit(solution)/shard_map/ppermute | solution.py:321
  112.0 1.3 collective-permute-start.10
  113.3 4.7 %collective-permute-done.10.above_ref = f32[20,512]{1,0:T(8,128)S(1)} collective-permute-done((f32[20,512]{1,0:T(8,128)S(1)}, f32[20,512]{1,0:T(8,128)S(1)}, u32[]{:S(2)}, u32[]{:S(2)}) %collective-permute-start.10) | collective-permute-done | bytes 40992 | tf_op jit(solution)/shard_map/ppermute | solution.py:322
  118.0 6.0 %middle.5 = (f32[5,32,512]{2,1,0:T(8,128)S(1)}, f32[16,8,256]{2,1,0:T(8,128)S(1)}) custom-call(f32[5,32,512]{2,1,0:T(8,128)S(1)} %get-tuple-element.37.state_ref, f32[30,512]{1,0:T(8,128)S(1)} %collective-permute-done.9.below_ref, f32[20,512]{1,0:T(8,128)S(1)} %collective-permute-done.10.above_ref, f32[5,32,512]{2,1,0:T(8,128)S(1)} %bitcast.24, ...), custom_call_target="tpu_custom_call" | custom-call | tf_op jit(solution)/shard_map/middle/pallas_call | solution.py:325
  124.1 0.1 collective-permute-start.11
  124.2 1.3 collective-permute-done.11
  125.5 13.6 %all_to_all.22.arrived_ref = f32[16,8,256]{2,1,0:T(8,128)S(1)} all-to-all(f32[16,8,256]{2,1,0:T(8,128)S(1)} %collective-permute-done.11), channel_id=1, replica_groups=mesh['group'=2,'blk'=16] {'blk'}, dimensions={0} | all-to-all | bytes 262144 | tf_op jit(solution)/shard_map/all_to_all | solution.py:311
  139.1 5.3 %place.7 = (f32[5,32,512]{2,1,0:T(8,128)S(1)}, f32[30,512]{1,0:T(8,128)S(1)}, f32[20,512]{1,0:T(8,128)S(1)}) custom-call(f32[16,8,256]{2,1,0:T(8,128)S(1)} %all_to_all.22.arrived_ref, s32[16,256]{1,0:T(8,128)S(1)} %bitcast.42, f32[5,32,512]{2,1,0:T(8,128)S(1)} %get-tuple-element.41.state_ref, f32[32,512]{1,0:T(8,128)S(1)} %get-tuple-element.26.movable_ref), custom_call_target="tpu_custom_call" | custom-call | tf_op jit(solution)/shard_map/place/pallas_call | solution.py:312
  144.4 3.0 %collective-permute-start.12 = (f32[30,512]{1,0:T(8,128)S(1)}, f32[30,512]{1,0:T(8,128)S(1)}, u32[]{:S(2)}, u32[]{:S(2)}) collective-permute-start(f32[30,512]{1,0:T(8,128)S(1)} %get-tuple-element.43), channel_id=1, source_target_pairs={{0,1},{1,2},{2,3},{3,4},{4,5},{5,6},{6,7},{7,8},{8,9},{9,10},{10,1... | collective-permute-start | bytes 184328 | tf_op jit(solution)/shard_map/ppermute | solution.py:321
  147.4 1.3 collective-permute-start.13
  148.7 4.7 %collective-permute-done.13.above_ref = f32[20,512]{1,0:T(8,128)S(1)} collective-permute-done((f32[20,512]{1,0:T(8,128)S(1)}, f32[20,512]{1,0:T(8,128)S(1)}, u32[]{:S(2)}, u32[]{:S(2)}) %collective-permute-start.13) | collective-permute-done | bytes 40992 | tf_op jit(solution)/shard_map/ppermute | solution.py:322
  153.4 2.0 %last.1 = f32[5,32,512]{2,1,0:T(8,128)} custom-call(f32[5,32,512]{2,1,0:T(8,128)S(1)} %get-tuple-element.42.state_ref, f32[30,512]{1,0:T(8,128)S(1)} %collective-permute-done.12.below_ref, f32[20,512]{1,0:T(8,128)S(1)} %collective-permute-done.13.above_ref, f32[5,32,512]{2,1,0:T(8,128)S(1)} %bitcast.25, f32[5,5,32,512]{3,2,1,0:T(8,128)S(1)} %bitcast.19, ...), custom_call_target="tpu_custom_call" | custom-call | tf_op jit(solution)/shard_map/last/pallas_call | solution.py:335
  (28 shorter events, 0.1 us)
Async XLA Ops:
  0.0 25.1 %copy-start.2 = (f32[1,1,4,32,512]{4,3,2,1,0:T(8,128)S(1)}, f32[1,1,4,32,512]{4,3,2,1,0:T(8,128)}, u32[]{:S(2)}) copy-start(f32[1,1,4,32,512]{4,3,2,1,0:T(8,128)} %param.10) | copy-start | bytes 786436
  0.0 26.1 %copy-start = (f32[1,1,5,5,32,512]{5,4,3,2,1,0:T(8,128)S(1)}, f32[1,1,5,5,32,512]{5,4,3,2,1,0:T(8,128)}, u32[]{:S(2)}) copy-start(f32[1,1,5,5,32,512]{5,4,3,2,1,0:T(8,128)} %param.9) | copy-start | bytes 4915204
  0.0 1.1 copy-start.3
  1.1 0.8 copy-start.5
  2.0 0.7 copy-start.7
  2.7 0.7 copy-start.9
  3.4 29.6 %copy-start.4 = (f32[1,1,5,32,512]{4,3,2,1,0:T(8,128)S(1)}, f32[1,1,5,32,512]{4,3,2,1,0:T(8,128)}, u32[]{:S(2)}) copy-start(f32[1,1,5,32,512]{4,3,2,1,0:T(8,128)} %param.7) | copy-start | bytes 983044
  3.4 29.6 %copy-start.8 = (s32[1,1,16,256]{3,2,1,0:T(8,128)S(1)}, s32[1,1,16,256]{3,2,1,0:T(8,128)}, u32[]{:S(2)}) copy-start(s32[1,1,16,256]{3,2,1,0:T(8,128)} %param.13) | copy-start | bytes 49156
  11.1 8.0 %collective-permute-start = (f32[16,8,256]{2,1,0:T(8,128)S(1)}, f32[16,8,256]{2,1,0:T(8,128)}, u32[]{:S(2)}, u32[]{:S(2)}) collective-permute-start(f32[16,8,256]{2,1,0:T(8,128)S(1)} %get-tuple-element.25), channel_id=1, source_target_pairs={{0,16},{1,17},{2,18},{3,19},{4,20},{5,21},{6,22},{7,23},{8,24},{9,... | collective-permute-start | bytes 393224 | tf_op jit(solution)/shard_map/ppermute | solution.py:310
  14.5 32.8 %copy-start.1 = (f32[1,1,5,32,512]{4,3,2,1,0:T(8,128)S(1)}, f32[1,1,5,32,512]{4,3,2,1,0:T(8,128)}, u32[]{:S(2)}) copy-start(f32[1,1,5,32,512]{4,3,2,1,0:T(8,128)} %param.8) | copy-start | bytes 983044
  14.5 32.8 %copy-start.6 = (f32[1,1,4,16,256]{4,3,2,1,0:T(8,128)S(1)}, f32[1,1,4,16,256]{4,3,2,1,0:T(8,128)}, u32[]{:S(2)}) copy-start(f32[1,1,4,16,256]{4,3,2,1,0:T(8,128)} %param.12) | copy-start | bytes 196612
  14.5 32.8 %copy-start.10 = (s32[1,1,16,256]{3,2,1,0:T(8,128)S(1)}, s32[1,1,16,256]{3,2,1,0:T(8,128)}, u32[]{:S(2)}) copy-start(s32[1,1,16,256]{3,2,1,0:T(8,128)} %param.11) | copy-start | bytes 49156
  14.6 29.0 %collective-permute-start.3 = (f32[35,3,512]{2,1,0:T(4,128)S(1)}, f32[35,3,512]{2,1,0:T(4,128)S(1)}, u32[]{:S(2)}, u32[]{:S(2)}) collective-permute-start(f32[35,3,512]{2,1,0:T(4,128)S(1)} %pad_maximum_fusion), channel_id=1, source_target_pairs={{0,1},{1,2},{2,3},{3,4},{4,5},{5,6},{6,7},{7,8},{8,9},{9,10},{10,1... | collective-permute-start | bytes 645128 | tf_op jit(solution)/shard_map/ppermute | solution.py:303
  19.2 13.8 %all-to-all-start = ((f32[16,8,256]{2,1,0:T(8,128)}), f32[16,8,256]{2,1,0:T(8,128)S(1)}, u32[]{:S(2)}, u32[]{:S(2)}) async-start(f32[16,8,256]{2,1,0:T(8,128)} %collective-permute-done), calls=%async_computation | async-start | bytes 262144 | tf_op jit(solution)/shard_map/all_to_all | solution.py:311
  26.8 15.8 %collective-permute-start.4 = (f32[35,2,512]{2,1,0:T(2,128)}, f32[35,2,512]{2,1,0:T(2,128)}, u32[]{:S(2)}, u32[]{:S(2)}) collective-permute-start(f32[35,2,512]{2,1,0:T(2,128)} %pad_maximum_fusion.1), channel_id=1, source_target_pairs={{1,0},{2,1},{3,2},{4,3},{5,4},{6,5},{7,6},{8,7},{9,8},{10,9},{11,1... | collective-permute-start | bytes 430088 | tf_op jit(solution)/shard_map/ppermute | solution.py:304
  38.4 8.9 %collective-permute-start.1 = (f32[30,512]{1,0:T(8,128)S(1)}, f32[30,512]{1,0:T(8,128)S(1)}, u32[]{:S(2)}, u32[]{:S(2)}) collective-permute-start(f32[30,512]{1,0:T(8,128)S(1)} %get-tuple-element.28), channel_id=1, source_target_pairs={{0,1},{1,2},{2,3},{3,4},{4,5},{5,6},{6,7},{7,8},{8,9},{9,10},{10,1... | collective-permute-start | bytes 184328 | tf_op jit(solution)/shard_map/ppermute | solution.py:321
  41.3 6.0 %collective-permute-start.2 = (f32[20,512]{1,0:T(8,128)S(1)}, f32[20,512]{1,0:T(8,128)S(1)}, u32[]{:S(2)}, u32[]{:S(2)}) collective-permute-start(f32[20,512]{1,0:T(8,128)S(1)} %get-tuple-element.29), channel_id=1, source_target_pairs={{1,0},{2,1},{3,2},{4,3},{5,4},{6,5},{7,6},{8,7},{9,8},{10,9},{11,1... | collective-permute-start | bytes 122888 | tf_op jit(solution)/shard_map/ppermute | solution.py:322
  53.2 1.4 collective-permute-start.5
  73.8 9.0 %collective-permute-start.6 = (f32[30,512]{1,0:T(8,128)S(1)}, f32[30,512]{1,0:T(8,128)S(1)}, u32[]{:S(2)}, u32[]{:S(2)}) collective-permute-start(f32[30,512]{1,0:T(8,128)S(1)} %get-tuple-element.33), channel_id=1, source_target_pairs={{0,1},{1,2},{2,3},{3,4},{4,5},{5,6},{6,7},{7,8},{8,9},{9,10},{10,1... | collective-permute-start | bytes 184328 | tf_op jit(solution)/shard_map/ppermute | solution.py:321
  76.8 6.0 %collective-permute-start.7 = (f32[20,512]{1,0:T(8,128)S(1)}, f32[20,512]{1,0:T(8,128)S(1)}, u32[]{:S(2)}, u32[]{:S(2)}) collective-permute-start(f32[20,512]{1,0:T(8,128)S(1)} %get-tuple-element.34), channel_id=1, source_target_pairs={{1,0},{2,1},{3,2},{4,3},{5,4},{6,5},{7,6},{8,7},{9,8},{10,9},{11,1... | collective-permute-start | bytes 122888 | tf_op jit(solution)/shard_map/ppermute | solution.py:322
  88.7 1.4 collective-permute-start.8
  109.0 9.0 %collective-permute-start.9 = (f32[30,512]{1,0:T(8,128)S(1)}, f32[30,512]{1,0:T(8,128)S(1)}, u32[]{:S(2)}, u32[]{:S(2)}) collective-permute-start(f32[30,512]{1,0:T(8,128)S(1)} %get-tuple-element.38), channel_id=1, source_target_pairs={{0,1},{1,2},{2,3},{3,4},{4,5},{5,6},{6,7},{7,8},{8,9},{9,10},{10,1... | collective-permute-start | bytes 184328 | tf_op jit(solution)/shard_map/ppermute | solution.py:321
  112.0 6.0 %collective-permute-start.10 = (f32[20,512]{1,0:T(8,128)S(1)}, f32[20,512]{1,0:T(8,128)S(1)}, u32[]{:S(2)}, u32[]{:S(2)}) collective-permute-start(f32[20,512]{1,0:T(8,128)S(1)} %get-tuple-element.39), channel_id=1, source_target_pairs={{1,0},{2,1},{3,2},{4,3},{5,4},{6,5},{7,6},{8,7},{9,8},{10,9},{11,1... | collective-permute-start | bytes 122888 | tf_op jit(solution)/shard_map/ppermute | solution.py:322
  124.1 1.4 collective-permute-start.11
  144.4 9.0 %collective-permute-start.12 = (f32[30,512]{1,0:T(8,128)S(1)}, f32[30,512]{1,0:T(8,128)S(1)}, u32[]{:S(2)}, u32[]{:S(2)}) collective-permute-start(f32[30,512]{1,0:T(8,128)S(1)} %get-tuple-element.43), channel_id=1, source_target_pairs={{0,1},{1,2},{2,3},{3,4},{4,5},{5,6},{6,7},{7,8},{8,9},{9,10},{10,1... | collective-permute-start | bytes 184328 | tf_op jit(solution)/shard_map/ppermute | solution.py:321
  147.4 6.0 %collective-permute-start.13 = (f32[20,512]{1,0:T(8,128)S(1)}, f32[20,512]{1,0:T(8,128)S(1)}, u32[]{:S(2)}, u32[]{:S(2)}) collective-permute-start(f32[20,512]{1,0:T(8,128)S(1)} %get-tuple-element.44), channel_id=1, source_target_pairs={{1,0},{2,1},{3,2},{4,3},{5,4},{6,5},{7,6},{8,7},{9,8},{10,9},{11,1... | collective-permute-start | bytes 122888 | tf_op jit(solution)/shard_map/ppermute | solution.py:322

commit v2 on v1

v2 whole, which is shorter than its diff:
```python
from functools import partial

import jax
import jax.numpy as jnp
from jax import lax
from jax.experimental import pallas as pl
from jax.experimental.pallas import tpu as pltpu
from jax.sharding import PartitionSpec as P

ITERS = 4

upwind_offsets = (-3, -2, -1, 0, 1, 2)
upwind_weights = (-2.0 / 60.0, 15.0 / 60.0, -60.0 / 60.0, 20.0 / 60.0, 30.0 / 60.0, -3.0 / 60.0)

F32 = jnp.float32
BF16 = jnp.bfloat16
ROWS = 8
LOW, HIGH = 6, 4
LOW_DONE, HIGH_DONE = 3, 2
PAD = 2 * ROWS
LANES, LANE_BITS, GROUP_BITS = 128, 7, 2
UNROLL = 16
VMEM_LIMIT = 16 * 1024 * 1024


def vmem(count):
    return [pl.BlockSpec(memory_space=pltpu.VMEM)] * count


def divmod_const(value, size):
    if size & (size - 1) == 0:
        return value >> (size.bit_length() - 1), value & (size - 1)
    quotient = lax.div(value, jnp.int32(size))
    return quotient, value - quotient * size


def one_hot(index, size):
    rows = lax.broadcasted_iota(jnp.int32, (size, index.shape[1]), 0)
    return jnp.where(rows == index, 1.0, 0.0).astype(BF16)


def split(value):
    high = value.astype(BF16)
    low = (value - high.astype(F32)).astype(BF16)
    return high, low


def repeat(count, step, unroll=UNROLL):
    lax.fori_loop(0, count, lambda i, carry: (step(i), carry)[1], 0, unroll=min(count, unroll))


def donor_sums(state, base_ref, weight_ref, out_ref):
    comps, rows, cols = state.shape
    half = cols // 2
    flat = state.reshape(comps * rows, cols)
    stacked = jnp.concatenate(split(flat), axis=0)
    at = lax.broadcasted_iota(jnp.int32, (cols, cols), 0)
    to = lax.broadcasted_iota(jnp.int32, (cols, cols), 1)
    source_col = jnp.where(to < half, 2 * to, 2 * (to - half) + 1)
    order = jnp.where(at == source_col, 1.0, 0.0).astype(BF16)
    ordered = jnp.dot(stacked, order, preferred_element_type=F32).astype(BF16)
    even, odd = ordered[:, :half], ordered[:, half:]
    blocks, slots = base_ref.shape
    row_iota = lax.broadcasted_iota(jnp.int32, (rows, slots), 0)

    def one(d):
        base = base_ref[pl.ds(d, 1), :]
        w0 = weight_ref[0, pl.ds(d, 1), :]
        w1 = weight_ref[1, pl.ds(d, 1), :]
        w2 = weight_ref[2, pl.ds(d, 1), :]
        w3 = weight_ref[3, pl.ds(d, 1), :]
        row, col = divmod_const(base, cols)
        is_odd = (col & 1) == 1
        wraps = col == cols - 1
        odd_at = col >> 1
        even_at = jnp.where(wraps, 0, (col + 1) >> 1)
        even_row = row + jnp.where(wraps, 1, 0)
        picked_even = jnp.dot(even, one_hot(even_at, half), preferred_element_type=F32)
        picked_odd = jnp.dot(odd, one_hot(odd_at, half), preferred_element_type=F32)
        count = comps * rows
        picked_even = (picked_even[:count] + picked_even[count:]).reshape(comps, rows, slots)
        picked_odd = (picked_odd[:count] + picked_odd[count:]).reshape(comps, rows, slots)
        even_weight = jnp.where(
            row_iota == even_row,
            jnp.where(is_odd, w1, w0),
            jnp.where(row_iota == even_row + 1, jnp.where(is_odd, w3, w2), 0.0),
        )
        odd_weight = jnp.where(
            row_iota == row,
            jnp.where(is_odd, w0, w1),
            jnp.where(row_iota == row + 1, jnp.where(is_odd, w2, w3), 0.0),
        )
        total = even_weight[None] * picked_even + odd_weight[None] * picked_odd
        out_ref[d, 0:comps, :] = jnp.sum(total, axis=1)

    repeat(blocks, one)
    none = jnp.zeros((comps, slots), F32)
    for d in range(blocks):
        out_ref[d, comps : 2 * comps, :] = out_ref[d - 1, 0:comps, :] if d > 0 else none
        out_ref[d, 2 * comps : 3 * comps, :] = out_ref[d + 1, 0:comps, :] if d < blocks - 1 else none


def selected(hit, values):
    count = values.shape[0] * hit.shape[0]
    parts = [
        jnp.where(hit[None], part.astype(F32)[:, None, :], 0.0).reshape(count, -1).astype(BF16)
        for part in split(values)
    ]
    return jnp.concatenate(parts, axis=0)


def add_product(acc_ref, left, right):
    out = lax.dot_general(left, right, (((1,), (1,)), ((), ())), preferred_element_type=F32)
    count = acc_ref.shape[0]
    acc_ref[...] += out if left.shape[0] == count else out[:count] + out[count:]


def frozen_count(target_ref, rows, cols, acc_ref):
    blocks, slots = target_ref.shape
    row_iota = lax.broadcasted_iota(jnp.int32, (rows, slots), 0)
    acc_ref[...] = jnp.zeros_like(acc_ref)

    def one(b):
        row, col = divmod_const(target_ref[pl.ds(b, 1), :], cols)
        add_product(acc_ref, jnp.where(row_iota == row, 1.0, 0.0).astype(BF16), one_hot(col, cols))

    repeat(blocks, one, 4)


def place_own(arrived_ref, target_ref, comps, rows, cols, acc_ref):
    blocks, slots = target_ref.shape
    row_iota = lax.broadcasted_iota(jnp.int32, (rows, slots), 0)
    acc_ref[...] = jnp.zeros_like(acc_ref)

    def one(b):
        row, col = divmod_const(target_ref[pl.ds(b, 1), :], cols)
        left = selected(row_iota == row, arrived_ref[b, 0:comps, :])
        add_product(acc_ref, left, one_hot(col, cols))

    repeat(blocks, one)


def place_halo(arrived_ref, first, target_ref, start, comps, cols, acc_ref, out_ref):
    blocks, slots = target_ref.shape
    tiles = cols // LANES
    group = ROWS // 2
    row_iota = lax.broadcasted_iota(jnp.int32, (tiles * group, slots), 0)
    acc_ref[...] = jnp.zeros_like(acc_ref)

    def one(b):
        row, col = divmod_const(target_ref[pl.ds(b, 1), :], cols)
        row = row - start
        hit = row_iota == (col >> LANE_BITS) * group + (row & (group - 1))
        at = (row >> GROUP_BITS) * LANES + (col & (LANES - 1))
        left = selected(hit, arrived_ref[b, first : first + comps, :])
        add_product(acc_ref, left, one_hot(at, 2 * LANES))

    repeat(blocks, one)
    for c in range(comps):
        for t in range(tiles):
            for h in range(2):
                out_ref[c, h * group : (h + 1) * group, t * LANES : (t + 1) * LANES] = acc_ref[
                    (c * tiles + t) * group : (c * tiles + t + 1) * group,
                    h * LANES : (h + 1) * LANES,
                ]


def border_rows(state_ref, movable_ref, top_ref, bottom_ref):
    comps, rows, _ = state_ref.shape
    upper = movable_ref[rows - ROWS :, :] > 0.5
    lower = movable_ref[:ROWS, :] > 0.5
    for c in range(comps):
        kept = jnp.where(upper, state_ref[c, rows - ROWS :, :], 0.0)
        top_ref[c * LOW : (c + 1) * LOW, :] = kept[ROWS - LOW :, :]
        kept = jnp.where(lower, state_ref[c, :ROWS, :], 0.0)
        bottom_ref[c * HIGH : (c + 1) * HIGH, :] = kept[:HIGH, :]


def start_kernel(
    field_hbm, base_hbm, weight_hbm, target_hbm, source_hbm, inverse_hbm, coupling_hbm,
    sums_ref, movable_ref, top_ref, bottom_ref,
    field_ref, base_ref, weight_ref, target_ref, source_ref, inverse_ref, coupling_ref, acc_ref, sems,
):
    comps, rows, cols = field_ref.shape
    blocks, slots = target_ref.shape
    last = slice(rows - ROWS, rows)
    first = slice(0, ROWS)
    copies = [
        (target_hbm, target_ref),
        (field_hbm, field_ref),
        (base_hbm, base_ref),
        (weight_hbm, weight_ref),
        (source_hbm.at[:, last], source_ref.at[0]),
        (source_hbm.at[:, first], source_ref.at[1]),
        (inverse_hbm.at[:, :, last], inverse_ref.at[0]),
        (inverse_hbm.at[:, :, first], inverse_ref.at[1]),
        (coupling_hbm.at[:, last], coupling_ref.at[0]),
        (coupling_hbm.at[:, first], coupling_ref.at[1]),
    ]
    copies = [pltpu.make_async_copy(a, b, sems.at[i]) for i, (a, b) in enumerate(copies)]
    for copy in copies:
        copy.start()
    copies[0].wait()
    frozen_count(target_ref, rows, cols, acc_ref)
    movable_ref[...] = jnp.where(acc_ref[...] > 0.5, 0.0, 1.0)
    for copy in copies[1:4]:
        copy.wait()
    donor_sums(field_ref[...], base_ref, weight_ref, sums_ref)
    border_rows(field_ref, movable_ref, top_ref, bottom_ref)
    for copy in copies[4:]:
        copy.wait()
    sides = (
        (top_ref, 0, comps * LOW, LOW_DONE, ROWS - LOW_DONE, rows - ROWS),
        (bottom_ref, 1, comps * HIGH, HIGH_DONE, 0, 0),
    )
    for ref, side, offset, count, at, movable_at in sides:
        fixed = [inverse_ref[side, v, w] for v in range(comps) for w in range(comps)]
        fixed += [source_ref[side, w] for w in range(comps)]
        fixed += [coupling_ref[side, i] for i in range(coupling_ref.shape[1])]
        fixed.append(movable_ref[movable_at : movable_at + ROWS, :])
        for value in fixed:
            ref[offset : offset + count, :] = value[at : at + count, :]
            offset += count
        per = cols // slots
        deep = blocks // per
        for i in range(per):
            cells = target_ref[i * deep : (i + 1) * deep, :].astype(F32)
            ref[offset : offset + deep, i * slots : (i + 1) * slots] = cells


def unpack_kernel(
    top_ref, bottom_ref, low_ref, high_ref, low_target_ref, high_target_ref, *, comps
):
    sides = (
        (top_ref, comps * LOW, LOW_DONE, ROWS - LOW_DONE, low_ref, low_target_ref),
        (bottom_ref, comps * HIGH, HIGH_DONE, 0, high_ref, high_target_ref),
    )
    for ref, offset, count, at, out_ref, target_ref in sides:
        cols = ref.shape[1]
        blocks, slots = target_ref.shape
        for i in range(out_ref.shape[0]):
            out_ref[i] = jnp.zeros((ROWS, cols), F32)
            out_ref[i, at : at + count, :] = ref[offset : offset + count, :]
            offset += count
        per = cols // slots
        deep = blocks // per
        for i in range(per):
            cells = ref[offset : offset + deep, i * slots : (i + 1) * slots]
            target_ref[i * deep : (i + 1) * deep, :] = cells.astype(jnp.int32)


def place(
    arrived_ref, target_ref, state_ref, movable_ref, low_target_ref, high_target_ref,
    out_ref, below_ref, above_ref, acc_ref, halo_ref,
):
    comps, rows, cols = state_ref.shape
    place_own(arrived_ref, target_ref, comps, rows, cols, acc_ref)
    movable = movable_ref[...] > 0.5
    for c in range(comps):
        out_ref[c] = jnp.where(movable, state_ref[c], acc_ref[c * rows : (c + 1) * rows, :])
    place_halo(arrived_ref, comps, low_target_ref, rows - ROWS, comps, cols, halo_ref, below_ref)
    place_halo(arrived_ref, 2 * comps, high_target_ref, 0, comps, cols, halo_ref, above_ref)


def sections(u_ref, start, parts, write, is_near, parity, comps, cols):
    source, inverse, coupling, movable = parts
    lanes = lax.broadcasted_iota(jnp.int32, (ROWS, cols), 1)
    sublanes = lax.broadcasted_iota(jnp.int32, (ROWS, cols), 0)

    def rows_at(c, offset):
        return u_ref[c, start + offset : start + offset + ROWS, :]

    def shifted(value, offset):
        return pltpu.roll(value, (-offset) % cols, 1)

    def finish(update, terms, mask):
        for v in range(comps):
            total = update(v)
            for w in range(comps):
                product = inverse(v, w) * terms[w]
                total = product if total is None else total + product
            write(v, jnp.where(mask, total, rows_at(v, 0)))

    @pl.when(is_near)
    def _():
        c0, c1, c2, c3 = (coupling(i) for i in range(4))
        c2 = jnp.where(lanes >= 1, c2, 0.0)
        c3 = jnp.where(lanes < cols - 1, c3, 0.0)
        terms = []
        for w in range(comps):
            here = rows_at(w, 0)
            term = source(w) + c0 * rows_at(w, -1) + c1 * rows_at(w, 1)
            terms.append(term + c2 * shifted(here, -1) + c3 * shifted(here, 1))
        colour = ((lanes + sublanes) & 1) == parity
        finish(lambda v: None, terms, colour & (movable() > 0.5))

    @pl.when(jnp.logical_not(is_near))
    def _():
        c0, c1 = coupling(0), coupling(1)
        factors = []
        for offset, weight in zip(upwind_offsets, upwind_weights):
            inside = (lanes + offset >= 0) & (lanes + offset < cols)
            factors.append(weight if offset == 0 else jnp.where(inside, weight, 0.0))
        terms = []
        for w in range(comps):
            here = rows_at(w, 0)
            along_j = along_k = None
            for offset, weight, factor in zip(upwind_offsets, upwind_weights, factors):
                in_j = weight * rows_at(w, offset)
                in_k = factor * (here if offset == 0 else shifted(here, offset))
                along_j = in_j if along_j is None else along_j + in_j
                along_k = in_k if along_k is None else along_k + in_k
            terms.append(source(w) - c0 * along_j - c1 * along_k)
        finish(lambda v: rows_at(v, 0), terms, movable() > 0.5)


def sweep(state_ref, below_ref, above_ref, placed_below_ref, placed_above_ref, movable_ref, work, out_ref):
    comps, rows, cols = state_ref.shape
    source_ref, inverse_ref, coupling_ref = work["source"], work["inverse"], work["coupling"]
    low_ref, high_ref, u_ref, v_ref = work["low"], work["high"], work["u"], work["v"]
    is_near = lax.axis_index("group") == 0
    for c in range(comps):
        u_ref[c, PAD : PAD + rows, :] = state_ref[c]
        u_ref[c, PAD - LOW : PAD, :] = (
            below_ref[c * LOW : (c + 1) * LOW, :] + placed_below_ref[c, ROWS - LOW :, :]
        )
        u_ref[c, PAD + rows : PAD + rows + HIGH, :] = (
            above_ref[c * HIGH : (c + 1) * HIGH, :] + placed_above_ref[c, :HIGH, :]
        )

    def own(r):
        at = slice(r, r + ROWS)
        return (
            lambda w: source_ref[w, at, :],
            lambda v, w: inverse_ref[v, w, at, :],
            lambda i: coupling_ref[i, at, :],
            lambda: movable_ref[at, :],
        )

    def packed(ref):
        first = comps * comps
        second = first + comps
        last = ref.shape[0] - 1
        return (
            lambda w: ref[first + w],
            lambda v, w: ref[v * comps + w],
            lambda i: ref[second + i],
            lambda: ref[last],
        )

    def into(ref, start):
        def write(v, value):
            ref[v, start : start + ROWS, :] = value

        return write

    wait = work["wait"]
    for r in range(0, rows, ROWS):
        wait(r)
        sections(u_ref, PAD + r, own(r), into(v_ref, PAD + r), is_near, 0, comps, cols)
    wait("low")
    sections(u_ref, PAD - ROWS, packed(low_ref), into(v_ref, PAD - ROWS), is_near, 0, comps, cols)
    wait("high")
    sections(u_ref, PAD + rows, packed(high_ref), into(v_ref, PAD + rows), is_near, 0, comps, cols)
    for r in range(0, rows, ROWS):
        sections(v_ref, PAD + r, own(r), into(out_ref, r), is_near, 1, comps, cols)


def step_kernel(names, is_last, refs):
    refs = list(refs)
    operands, refs = refs[:6], refs[6:]
    held, refs = refs[: len(names)], refs[len(names) :]
    out_ref = refs.pop(0)
    if not is_last:
        sums_ref, top_ref, bottom_ref = refs[:3]
        refs = refs[3:]
    copied, (u_ref, v_ref, sems) = refs[: len(names)], refs[len(names) :]
    rows = out_ref.shape[1]
    work = dict(zip(names, copied))
    work.update(u=u_ref, v=v_ref)
    copies = {}
    count = 0

    def copy(key, source, target):
        nonlocal count
        copies.setdefault(key, []).append(pltpu.make_async_copy(source, target, sems.at[count]))
        count += 1

    whole = dict(zip(names, held))
    for r in range(0, rows, ROWS):
        at = slice(r, r + ROWS)
        copy(r, whole["inverse"].at[:, :, at], work["inverse"].at[:, :, at])
        copy(r, whole["source"].at[:, at], work["source"].at[:, at])
        copy(r, whole["coupling"].at[:, at], work["coupling"].at[:, at])
    for name in names:
        if name not in ("inverse", "source", "coupling"):
            copy(name, whole[name], work[name])
    for group in copies.values():
        for one in group:
            one.start()

    def wait(key):
        for one in copies[key]:
            one.wait()

    work["wait"] = wait
    sweep(*operands, work, out_ref)
    if not is_last:
        movable_ref = operands[5]
        border_rows(out_ref, movable_ref, top_ref, bottom_ref)
        wait("base")
        wait("weight")
        donor_sums(out_ref[...], work["base"], work["weight"], sums_ref)


def on_device(field, source, block_inverse, coupling, donor_base, donor_weight, receiver_cell):
    state = field[0, 0]
    source = source[0, 0]
    inverse = block_inverse[0, 0]
    coupling = coupling[0, 0]
    base = donor_base[0, 0]
    weight = donor_weight[0, 0]
    target = receiver_cell[0, 0]
    comps, rows, cols = state.shape
    faces = coupling.shape[0]
    blocks, slots = base.shape
    groups = lax.axis_size("group")
    swap = [(g * blocks + b, (groups - 1 - g) * blocks + b) for g in range(groups) for b in range(blocks)]
    up = [(b, b + 1) for b in range(blocks - 1)]
    down = [(b + 1, b) for b in range(blocks - 1)]

    def f32(*shape):
        return jax.ShapeDtypeStruct(shape, F32)

    def call(kernel, operands, remote, outs, scratch):
        remote = [pltpu.with_memory_space_constraint(value, pltpu.HBM) for value in remote]
        return pl.pallas_call(
            kernel,
            out_shape=outs,
            in_specs=vmem(len(operands)) + [pl.BlockSpec(memory_space=pltpu.HBM)] * len(remote),
            out_specs=tuple(vmem(len(outs))),
            scratch_shapes=scratch,
            compiler_params=pltpu.CompilerParams(vmem_limit_bytes=VMEM_LIMIT),
        )(*operands, *remote)

    def vmem_like(*shape, dtype=F32):
        return pltpu.VMEM(shape, dtype)

    fixed = comps * comps + comps + faces + 1
    cells = f32(comps, rows, cols)
    sums_shape = f32(blocks, -(-3 * comps // ROWS) * ROWS, slots)
    deep = blocks * slots // cols

    sums, movable, top, bottom = call(
        start_kernel,
        (),
        (state, base, weight, target, source, inverse, coupling),
        (
            sums_shape,
            f32(rows, cols),
            f32(comps * LOW + fixed * LOW_DONE + deep, cols),
            f32(comps * HIGH + fixed * HIGH_DONE + deep, cols),
        ),
        [
            vmem_like(comps, rows, cols),
            vmem_like(blocks, slots, dtype=jnp.int32),
            vmem_like(*weight.shape),
            vmem_like(blocks, slots, dtype=jnp.int32),
            vmem_like(2, comps, ROWS, cols),
            vmem_like(2, comps, comps, ROWS, cols),
            vmem_like(2, faces, ROWS, cols),
            vmem_like(rows, cols),
            pltpu.SemaphoreType.DMA((10,)),
        ],
    )

    placing = [vmem_like(comps * rows, cols), vmem_like(comps * (cols // LANES) * (ROWS // 2), 2 * LANES)]
    working = [vmem_like(comps, rows + 2 * PAD, cols)] * 2
    held = {"source": source, "inverse": inverse, "coupling": coupling, "base": base, "weight": weight}
    border = (f32(comps * LOW, cols), f32(comps * HIGH, cols))
    halo = f32(comps, ROWS, cols)
    for iteration in range(ITERS):
        arrived = lax.ppermute(sums, ("group", "blk"), swap)
        arrived = lax.all_to_all(arrived, "blk", split_axis=0, concat_axis=0, tiled=True)
        below = lax.ppermute(top, "blk", up)
        above = lax.ppermute(bottom, "blk", down)
        is_last = iteration == ITERS - 1
        if iteration == 0:
            cells_of = jax.ShapeDtypeStruct((blocks, slots), jnp.int32)
            held["low"], held["high"], low_target, high_target = call(
                partial(unpack_kernel, comps=comps),
                (below, above),
                (),
                (f32(fixed, ROWS, cols), f32(fixed, ROWS, cols), cells_of, cells_of),
                [],
            )
        state, placed_below, placed_above = call(
            place,
            (arrived, target, state, movable, low_target, high_target),
            (),
            (cells, halo, halo),
            placing,
        )
        names = tuple(name for name in held if not (is_last and name in ("base", "weight")))
        copied = [vmem_like(*held[name].shape, dtype=held[name].dtype) for name in names]
        results = call(
            lambda *refs: step_kernel(names, is_last, refs),
            (state, below, above, placed_below, placed_above, movable),
            tuple(held[name] for name in names),
            (cells,) if is_last else (cells, sums_shape, *border),
            copied + working + [pltpu.SemaphoreType.DMA((3 * (rows // ROWS) + len(names),))],
        )
        state = results[0]
        if not is_last:
            sums, top, bottom = results[1:]
    return state[None, None]


def solution(mesh):
    in_specs = (
        P("group", "blk", None, None, None),
        P("group", "blk", None, None, None),
        P("group", "blk", None, None, None, None),
        P("group", "blk", None, None, None),
        P("group", "blk", None, None),
        P("group", "blk", None, None, None),
        P("group", "blk", None, None),
    )
    out_specs = P("group", "blk", None, None, None)
    return jax.shard_map(
        on_device, mesh=mesh, in_specs=in_specs, out_specs=out_specs, check_vma=False
    )
```

time: 156 us -> 116 us (0.74)
  blocking collectives: 41.1 us -> 0 us
  starting transfers between devices: 29.7 us -> 42.8 us
  Pallas kernels: 48.8 us -> 36.1 us
  waiting for transfers between devices: 26.6 us -> 34.4 us
  local copies, waits for them, and re-layouts: 8.2 us -> 1.62 us
    all_to_all x3 -> x0, blocking collectives: 41.1 us -> none  [on_device(): lax.all_to_all(arrived, 'blk', split_axis=0, concat_axis=0, tiled=True)]
    all_to_all x1 -> x4, starting transfers between devices: 5.93 us -> 21.4 us  [on_device(): lax.all_to_all(arrived, 'blk', split_axis=0, concat_axis=0, tiled=True)]
    pallas_call x9 -> x10, Pallas kernels: 48.8 us -> 36.1 us  [call(): pl.pallas_call(kernel, out_shape=outs, in_specs=vmem(len(operands)) + [pl...]
    all_to_all x1 -> x4, waiting for transfers between devices: 4.93 us -> 15.4 us  [on_device(): lax.all_to_all(arrived, 'blk', split_axis=0, concat_axis=0, tiled=True)]
    ppermute x2 -> x0, starting transfers between devices: 5.83 us -> none  [the longest x1 4.55 us: on_device(): low = lax.ppermute(fixed_rows(rows - LOW_DONE, LOW_DONE), 'blk', up)]
    ppermute x4, waiting for transfers between devices: 17.6 us -> 12.7 us  [on_device(): above = lax.ppermute(bottom, 'blk', down)]
    slice x6 -> x0, local copies, waits for them, and re-layouts: 3.72 us -> none  [the longest x2 1.79 us: fixed_rows(): source[:, at:at + count]]
    ppermute x4, starting transfers between devices: 12 us -> 15.3 us  [on_device(): below = lax.ppermute(top, 'blk', up)]
  transfers between devices with their start and end apart: 15 -> 16, of which waited for: 8 -> 8; matrix products, arithmetic and copies ran while one was open for 4% -> 0% of each run, Pallas kernels for 3% -> 8%
where the time goes in v2:
time: 116 us; the launch traced here: 115 us
  starting transfers between devices  42.8 us (37%)
  Pallas kernels  36.1 us (31%)
  waiting for transfers between devices  34.4 us (30%)
  local copies, waits for them, and re-layouts  1.62 us (1%)
    pallas_call x10, Pallas kernels, call(): pl.pallas_call(kernel, out_shape=outs, in_specs=vmem(len(operands)) + [pl...  36.1 us
    all_to_all x4, starting transfers between devices, on_device(): lax.all_to_all(arrived, 'blk', split_axis=0, concat_axis=0, tiled=True)  21.4 us
    all_to_all x4, waiting for transfers between devices, on_device(): lax.all_to_all(arrived, 'blk', split_axis=0, concat_axis=0, tiled=True)  15.4 us
    ppermute x4, starting transfers between devices, on_device(): below = lax.ppermute(top, 'blk', up)  15.3 us
    ppermute x4, waiting for transfers between devices, on_device(): above = lax.ppermute(bottom, 'blk', down)  12.7 us
    ppermute x4, waiting for transfers between devices, on_device(): arrived = lax.ppermute(sums, ('group', 'blk'), swap)  6.25 us
    ppermute x4, starting transfers between devices, on_device(): above = lax.ppermute(bottom, 'blk', down)  5.35 us
  transfers between devices with their start and end apart: 16, of which 8 were waited for; matrix products, arithmetic and copies ran while one was open for 0% of the time, Pallas kernels for 8%

profile of v2, /device:TPU:0, one launch (start us, length us, event | category | flops | bytes accessed | tf_op | source)
XLA Modules:
  0.0 115.2 jit_solution(16495349036869322825)
XLA Ops:
  0.0 0.0 copy-start.2
  0.0 5.1 %shard_map.73 = (f32[16,16,256]{2,1,0:T(8,128)S(1)}, f32[32,512]{1,0:T(8,128)S(1)}, f32[143,512]{1,0:T(8,128)S(1)}, f32[98,512]{1,0:T(8,128)S(1)}) custom-call(f32[5,32,512]{2,1,0:T(8,128)} %bitcast.8, s32[16,256]{1,0:T(8,128)} %bitcast.34, f32[4,16,256]{2,1,0:T(8,128)} %bitcast.30, s32[16,256]{1,0:T(8,128)} %bitcast.10, f32[5,32,512]{2,1,0:T(8,128)} %bitcast.20, ...), custom_call_target="tpu_custom_call" | custom-call | tf_op jit(solution)/shard_map/pallas_call | solution.py:437
  5.2 0.6 collective-permute-start
  5.7 1.3 %collective-permute-done = f32[16,16,256]{2,1,0:T(8,128)} collective-permute-done((f32[16,16,256]{2,1,0:T(8,128)S(1)}, f32[16,16,256]{2,1,0:T(8,128)}, u32[]{:S(2)}, u32[]{:S(2)}) %collective-permute-start) | collective-permute-done | bytes 262176 | tf_op jit(solution)/shard_map/ppermute | solution.py:483
  7.0 8.2 %all-to-all-start = ((f32[16,16,256]{2,1,0:T(8,128)}), f32[16,16,256]{2,1,0:T(8,128)S(1)}, u32[]{:S(2)}, u32[]{:S(2)}) async-start(f32[16,16,256]{2,1,0:T(8,128)} %collective-permute-done), calls=%async_computation | async-start | bytes 524288 | tf_op jit(solution)/shard_map/all_to_all | solution.py:484
  15.2 3.8 %collective-permute-start.1 = (f32[143,512]{1,0:T(8,128)S(1)}, f32[143,512]{1,0:T(8,128)S(1)}, u32[]{:S(2)}, u32[]{:S(2)}) collective-permute-start(f32[143,512]{1,0:T(8,128)S(1)} %get-tuple-element.39), channel_id=1, source_target_pairs={{0,1},{1,2},{2,3},{3,4},{4,5},{5,6},{6,7},{7,8},{8,9},{9,10},{10,1... | collective-permute-start | bytes 878600 | tf_op jit(solution)/shard_map/ppermute | solution.py:485
  19.1 1.3 %collective-permute-start.2 = (f32[98,512]{1,0:T(8,128)S(1)}, f32[98,512]{1,0:T(8,128)S(1)}, u32[]{:S(2)}, u32[]{:S(2)}) collective-permute-start(f32[98,512]{1,0:T(8,128)S(1)} %get-tuple-element.40), channel_id=1, source_target_pairs={{1,0},{2,1},{3,2},{4,3},{5,4},{6,5},{7,6},{8,7},{9,8},{10,9},{11,1... | collective-permute-start | bytes 602120 | tf_op jit(solution)/shard_map/ppermute | solution.py:486
  20.4 12.7 %collective-permute-done.2.bottom_ref.refs_2_ = f32[98,512]{1,0:T(8,128)S(1)} collective-permute-done((f32[98,512]{1,0:T(8,128)S(1)}, f32[98,512]{1,0:T(8,128)S(1)}, u32[]{:S(2)}, u32[]{:S(2)}) %collective-permute-start.2) | collective-permute-done | bytes 200736 | tf_op jit(solution)/shard_map/ppermute | solution.py:486
  33.1 0.0 collective-permute-done.1.top_ref.refs_1_
  33.1 0.2 shard_map.74
  33.3 0.0 copy-start
  33.3 0.8 copy-done
  34.1 0.8 copy-done.1
  34.9 0.0 all-to-all-done.arrived_ref
  34.9 0.0 copy-done.2
  34.9 0.0 copy-done.3
  35.0 2.9 %shard_map.75 = (f32[5,32,512]{2,1,0:T(8,128)S(1)}, f32[5,8,512]{2,1,0:T(8,128)S(1)}, f32[5,8,512]{2,1,0:T(8,128)S(1)}) custom-call(f32[16,16,256]{2,1,0:T(8,128)S(1)} %all-to-all-done.arrived_ref, s32[16,256]{1,0:T(8,128)S(1)} %bitcast.11, f32[5,32,512]{2,1,0:T(8,128)S(1)} %bitcast.9, f32[32,512]{1,0:T(8,128)S(1)} %get-tuple-element.38.movable_ref.refs_5_, ...), custom_call_target="tpu_custom_call" | custom-call | tf_op jit(solution)/shard_map/pallas_call | solution.py:437
  37.9 5.2 %shard_map.76 = (f32[5,32,512]{2,1,0:T(8,128)S(1)}, f32[16,16,256]{2,1,0:T(8,128)S(1)}, f32[30,512]{1,0:T(8,128)S(1)}, f32[20,512]{1,0:T(8,128)S(1)}) custom-call(f32[5,32,512]{2,1,0:T(8,128)S(1)} %get-tuple-element.43.refs_0_, f32[143,512]{1,0:T(8,128)S(1)} %collective-permute-done.1.top_ref.refs_1_, ...), custom_call_target="tpu_custom_call" | custom-call | tf_op jit(solution)/shard_map/pallas_call | solution.py:437
  43.1 0.1 collective-permute-start.3
  43.1 1.7 %collective-permute-done.3 = f32[16,16,256]{2,1,0:T(8,128)} collective-permute-done((f32[16,16,256]{2,1,0:T(8,128)S(1)}, f32[16,16,256]{2,1,0:T(8,128)}, u32[]{:S(2)}, u32[]{:S(2)}) %collective-permute-start.3) | collective-permute-done | bytes 262176 | tf_op jit(solution)/shard_map/ppermute | solution.py:483
  44.8 5.5 %all-to-all-start.1 = ((f32[16,16,256]{2,1,0:T(8,128)}), f32[16,16,256]{2,1,0:T(8,128)S(1)}, u32[]{:S(2)}, u32[]{:S(2)}) async-start(f32[16,16,256]{2,1,0:T(8,128)} %collective-permute-done.3), calls=%async_computation.1 | async-start | bytes 524288 | tf_op jit(solution)/shard_map/all_to_all | solution.py:484
  50.3 3.8 %collective-permute-start.4 = (f32[30,512]{1,0:T(8,128)S(1)}, f32[30,512]{1,0:T(8,128)S(1)}, u32[]{:S(2)}, u32[]{:S(2)}) collective-permute-start(f32[30,512]{1,0:T(8,128)S(1)} %get-tuple-element.51), channel_id=1, source_target_pairs={{0,1},{1,2},{2,3},{3,4},{4,5},{5,6},{6,7},{7,8},{8,9},{9,10},{10,1... | collective-permute-start | bytes 184328 | tf_op jit(solution)/shard_map/ppermute | solution.py:485
  54.1 1.5 %collective-permute-start.5 = (f32[20,512]{1,0:T(8,128)S(1)}, f32[20,512]{1,0:T(8,128)S(1)}, u32[]{:S(2)}, u32[]{:S(2)}) collective-permute-start(f32[20,512]{1,0:T(8,128)S(1)} %get-tuple-element.52), channel_id=1, source_target_pairs={{1,0},{2,1},{3,2},{4,3},{5,4},{6,5},{7,6},{8,7},{9,8},{10,9},{11,1... | collective-permute-start | bytes 122888 | tf_op jit(solution)/shard_map/ppermute | solution.py:486
  55.6 5.2 %all-to-all-done.1.arrived_ref = f32[16,16,256]{2,1,0:T(8,128)S(1)} async-done(((f32[16,16,256]{2,1,0:T(8,128)}), f32[16,16,256]{2,1,0:T(8,128)S(1)}, u32[]{:S(2)}, u32[]{:S(2)}) %all-to-all-start.1) | async-done | bytes 262176 | tf_op jit(solution)/shard_map/all_to_all | solution.py:484
  60.8 2.9 %shard_map.77 = (f32[5,32,512]{2,1,0:T(8,128)S(1)}, f32[5,8,512]{2,1,0:T(8,128)S(1)}, f32[5,8,512]{2,1,0:T(8,128)S(1)}) custom-call(f32[16,16,256]{2,1,0:T(8,128)S(1)} %all-to-all-done.1.arrived_ref, s32[16,256]{1,0:T(8,128)S(1)} %bitcast.12, f32[5,32,512]{2,1,0:T(8,128)S(1)} %get-tuple-element.49.state_ref, ...), custom_call_target="tpu_custom_call" | custom-call | tf_op jit(solution)/shard_map/pallas_call | solution.py:437
  63.7 0.0 collective-permute-done.5.refs_2_
  63.8 0.0 collective-permute-done.4.refs_1_
  63.8 5.2 %shard_map.78 = (f32[5,32,512]{2,1,0:T(8,128)S(1)}, f32[16,16,256]{2,1,0:T(8,128)S(1)}, f32[30,512]{1,0:T(8,128)S(1)}, f32[20,512]{1,0:T(8,128)S(1)}) custom-call(f32[5,32,512]{2,1,0:T(8,128)S(1)} %get-tuple-element.50.refs_0_, f32[30,512]{1,0:T(8,128)S(1)} %collective-permute-done.4.refs_1_, f32[20,512]{1,0:T(8,128)S(1)} %collective-permute-done.5.refs_2_, ...), custom_call_target="tpu_custom_call" | custom-call | tf_op jit(solution)/shard_map/pallas_call | solution.py:437
  68.9 0.1 collective-permute-start.6
  69.0 1.7 %collective-permute-done.6 = f32[16,16,256]{2,1,0:T(8,128)} collective-permute-done((f32[16,16,256]{2,1,0:T(8,128)S(1)}, f32[16,16,256]{2,1,0:T(8,128)}, u32[]{:S(2)}, u32[]{:S(2)}) %collective-permute-start.6) | collective-permute-done | bytes 262176 | tf_op jit(solution)/shard_map/ppermute | solution.py:483
  70.7 3.7 %all-to-all-start.2 = ((f32[16,16,256]{2,1,0:T(8,128)}), f32[16,16,256]{2,1,0:T(8,128)S(1)}, u32[]{:S(2)}, u32[]{:S(2)}) async-start(f32[16,16,256]{2,1,0:T(8,128)} %collective-permute-done.6), calls=%async_computation.2 | async-start | bytes 524288 | tf_op jit(solution)/shard_map/all_to_all | solution.py:484
  74.4 3.8 %collective-permute-start.7 = (f32[30,512]{1,0:T(8,128)S(1)}, f32[30,512]{1,0:T(8,128)S(1)}, u32[]{:S(2)}, u32[]{:S(2)}) collective-permute-start(f32[30,512]{1,0:T(8,128)S(1)} %get-tuple-element.58), channel_id=1, source_target_pairs={{0,1},{1,2},{2,3},{3,4},{4,5},{5,6},{6,7},{7,8},{8,9},{9,10},{10,1... | collective-permute-start | bytes 184328 | tf_op jit(solution)/shard_map/ppermute | solution.py:485
  78.2 1.3 %collective-permute-start.8 = (f32[20,512]{1,0:T(8,128)S(1)}, f32[20,512]{1,0:T(8,128)S(1)}, u32[]{:S(2)}, u32[]{:S(2)}) collective-permute-start(f32[20,512]{1,0:T(8,128)S(1)} %get-tuple-element.59), channel_id=1, source_target_pairs={{1,0},{2,1},{3,2},{4,3},{5,4},{6,5},{7,6},{8,7},{9,8},{10,9},{11,1... | collective-permute-start | bytes 122888 | tf_op jit(solution)/shard_map/ppermute | solution.py:486
  79.5 5.1 %all-to-all-done.2.arrived_ref = f32[16,16,256]{2,1,0:T(8,128)S(1)} async-done(((f32[16,16,256]{2,1,0:T(8,128)}), f32[16,16,256]{2,1,0:T(8,128)S(1)}, u32[]{:S(2)}, u32[]{:S(2)}) %all-to-all-start.2) | async-done | bytes 262176 | tf_op jit(solution)/shard_map/all_to_all | solution.py:484
  84.6 2.9 %shard_map.79 = (f32[5,32,512]{2,1,0:T(8,128)S(1)}, f32[5,8,512]{2,1,0:T(8,128)S(1)}, f32[5,8,512]{2,1,0:T(8,128)S(1)}) custom-call(f32[16,16,256]{2,1,0:T(8,128)S(1)} %all-to-all-done.2.arrived_ref, s32[16,256]{1,0:T(8,128)S(1)} %bitcast.13, f32[5,32,512]{2,1,0:T(8,128)S(1)} %get-tuple-element.56.state_ref, ...), custom_call_target="tpu_custom_call" | custom-call | tf_op jit(solution)/shard_map/pallas_call | solution.py:437
  87.6 0.0 collective-permute-done.8.refs_2_
  87.6 0.0 collective-permute-done.7.refs_1_
  87.6 5.2 %shard_map.80 = (f32[5,32,512]{2,1,0:T(8,128)S(1)}, f32[16,16,256]{2,1,0:T(8,128)S(1)}, f32[30,512]{1,0:T(8,128)S(1)}, f32[20,512]{1,0:T(8,128)S(1)}) custom-call(f32[5,32,512]{2,1,0:T(8,128)S(1)} %get-tuple-element.57.refs_0_, f32[30,512]{1,0:T(8,128)S(1)} %collective-permute-done.7.refs_1_, f32[20,512]{1,0:T(8,128)S(1)} %collective-permute-done.8.refs_2_, ...), custom_call_target="tpu_custom_call" | custom-call | tf_op jit(solution)/shard_map/pallas_call | solution.py:437
  92.8 0.1 collective-permute-start.9
  92.9 1.7 %collective-permute-done.9 = f32[16,16,256]{2,1,0:T(8,128)} collective-permute-done((f32[16,16,256]{2,1,0:T(8,128)S(1)}, f32[16,16,256]{2,1,0:T(8,128)}, u32[]{:S(2)}, u32[]{:S(2)}) %collective-permute-start.9) | collective-permute-done | bytes 262176 | tf_op jit(solution)/shard_map/ppermute | solution.py:483
  94.5 4.0 %all-to-all-start.3 = ((f32[16,16,256]{2,1,0:T(8,128)}), f32[16,16,256]{2,1,0:T(8,128)S(1)}, u32[]{:S(2)}, u32[]{:S(2)}) async-start(f32[16,16,256]{2,1,0:T(8,128)} %collective-permute-done.9), calls=%async_computation.3 | async-start | bytes 524288 | tf_op jit(solution)/shard_map/all_to_all | solution.py:484
  98.5 3.8 %collective-permute-start.10 = (f32[30,512]{1,0:T(8,128)S(1)}, f32[30,512]{1,0:T(8,128)S(1)}, u32[]{:S(2)}, u32[]{:S(2)}) collective-permute-start(f32[30,512]{1,0:T(8,128)S(1)} %get-tuple-element.65), channel_id=1, source_target_pairs={{0,1},{1,2},{2,3},{3,4},{4,5},{5,6},{6,7},{7,8},{8,9},{9,10},{10,1... | collective-permute-start | bytes 184328 | tf_op jit(solution)/shard_map/ppermute | solution.py:485
  102.3 1.3 %collective-permute-start.11 = (f32[20,512]{1,0:T(8,128)S(1)}, f32[20,512]{1,0:T(8,128)S(1)}, u32[]{:S(2)}, u32[]{:S(2)}) collective-permute-start(f32[20,512]{1,0:T(8,128)S(1)} %get-tuple-element.66), channel_id=1, source_target_pairs={{1,0},{2,1},{3,2},{4,3},{5,4},{6,5},{7,6},{8,7},{9,8},{10,9},{11,1... | collective-permute-start | bytes 122888 | tf_op jit(solution)/shard_map/ppermute | solution.py:486
  103.6 5.0 %all-to-all-done.3.arrived_ref = f32[16,16,256]{2,1,0:T(8,128)S(1)} async-done(((f32[16,16,256]{2,1,0:T(8,128)}), f32[16,16,256]{2,1,0:T(8,128)S(1)}, u32[]{:S(2)}, u32[]{:S(2)}) %all-to-all-start.3) | async-done | bytes 262176 | tf_op jit(solution)/shard_map/all_to_all | solution.py:484
  108.7 2.9 %shard_map.81 = (f32[5,32,512]{2,1,0:T(8,128)S(1)}, f32[5,8,512]{2,1,0:T(8,128)S(1)}, f32[5,8,512]{2,1,0:T(8,128)S(1)}) custom-call(f32[16,16,256]{2,1,0:T(8,128)S(1)} %all-to-all-done.3.arrived_ref, s32[16,256]{1,0:T(8,128)S(1)} %bitcast.14, f32[5,32,512]{2,1,0:T(8,128)S(1)} %get-tuple-element.63.state_ref, ...), custom_call_target="tpu_custom_call" | custom-call | tf_op jit(solution)/shard_map/pallas_call | solution.py:437
  111.6 0.0 collective-permute-done.11.refs_2_
  111.6 0.0 collective-permute-done.10.refs_1_
  111.6 3.4 %shard_map.82 = f32[5,32,512]{2,1,0:T(8,128)} custom-call(f32[5,32,512]{2,1,0:T(8,128)S(1)} %get-tuple-element.64.refs_0_, f32[30,512]{1,0:T(8,128)S(1)} %collective-permute-done.10.refs_1_, f32[20,512]{1,0:T(8,128)S(1)} %collective-permute-done.11.refs_2_, f32[5,8,512]{2,1,0:T(8,128)S(1)} %get-tuple-element.67.refs_3_, ...), custom_call_target="tpu_custom_call" | custom-call | tf_op jit(solution)/shard_map/pallas_call | solution.py:437
  (2 shorter events, 0.0 us)
Async XLA Ops:
  0.0 34.9 %copy-start.2 = (f32[1,1,5,32,512]{4,3,2,1,0:T(8,128)S(1)}, f32[1,1,5,32,512]{4,3,2,1,0:T(8,128)}, u32[]{:S(2)}) copy-start(f32[1,1,5,32,512]{4,3,2,1,0:T(8,128)} %param.7) | copy-start | bytes 983044
  0.0 34.9 %copy-start.3 = (s32[1,1,16,256]{3,2,1,0:T(8,128)S(1)}, s32[1,1,16,256]{3,2,1,0:T(8,128)}, u32[]{:S(2)}) copy-start(s32[1,1,16,256]{3,2,1,0:T(8,128)} %param.13) | copy-start | bytes 49156
  5.2 1.9 %collective-permute-start = (f32[16,16,256]{2,1,0:T(8,128)S(1)}, f32[16,16,256]{2,1,0:T(8,128)}, u32[]{:S(2)}, u32[]{:S(2)}) collective-permute-start(f32[16,16,256]{2,1,0:T(8,128)S(1)} %get-tuple-element.37), channel_id=1, source_target_pairs={{0,16},{1,17},{2,18},{3,19},{4,20},{5,21},{6,22},{7,23},{8,24},{9,... | collective-permute-start | bytes 786440 | tf_op jit(solution)/shard_map/ppermute | solution.py:483
  7.0 27.9 %all-to-all-start = ((f32[16,16,256]{2,1,0:T(8,128)}), f32[16,16,256]{2,1,0:T(8,128)S(1)}, u32[]{:S(2)}, u32[]{:S(2)}) async-start(f32[16,16,256]{2,1,0:T(8,128)} %collective-permute-done), calls=%async_computation | async-start | bytes 524288 | tf_op jit(solution)/shard_map/all_to_all | solution.py:484
  15.2 17.9 %collective-permute-start.1 = (f32[143,512]{1,0:T(8,128)S(1)}, f32[143,512]{1,0:T(8,128)S(1)}, u32[]{:S(2)}, u32[]{:S(2)}) collective-permute-start(f32[143,512]{1,0:T(8,128)S(1)} %get-tuple-element.39), channel_id=1, source_target_pairs={{0,1},{1,2},{2,3},{3,4},{4,5},{5,6},{6,7},{7,8},{8,9},{9,10},{10,1... | collective-permute-start | bytes 878600 | tf_op jit(solution)/shard_map/ppermute | solution.py:485
  19.1 14.0 %collective-permute-start.2 = (f32[98,512]{1,0:T(8,128)S(1)}, f32[98,512]{1,0:T(8,128)S(1)}, u32[]{:S(2)}, u32[]{:S(2)}) collective-permute-start(f32[98,512]{1,0:T(8,128)S(1)} %get-tuple-element.40), channel_id=1, source_target_pairs={{1,0},{2,1},{3,2},{4,3},{5,4},{6,5},{7,6},{8,7},{9,8},{10,9},{11,1... | collective-permute-start | bytes 602120 | tf_op jit(solution)/shard_map/ppermute | solution.py:486
  33.3 0.8 copy-start
  34.1 0.8 copy-start.1
  43.1 1.7 %collective-permute-start.3 = (f32[16,16,256]{2,1,0:T(8,128)S(1)}, f32[16,16,256]{2,1,0:T(8,128)}, u32[]{:S(2)}, u32[]{:S(2)}) collective-permute-start(f32[16,16,256]{2,1,0:T(8,128)S(1)} %get-tuple-element.48), channel_id=1, source_target_pairs={{0,16},{1,17},{2,18},{3,19},{4,20},{5,21},{6,22},{7,23},{8,24},{9,... | collective-permute-start | bytes 786440 | tf_op jit(solution)/shard_map/ppermute | solution.py:483
  44.8 16.0 %all-to-all-start.1 = ((f32[16,16,256]{2,1,0:T(8,128)}), f32[16,16,256]{2,1,0:T(8,128)S(1)}, u32[]{:S(2)}, u32[]{:S(2)}) async-start(f32[16,16,256]{2,1,0:T(8,128)} %collective-permute-done.3), calls=%async_computation.1 | async-start | bytes 524288 | tf_op jit(solution)/shard_map/all_to_all | solution.py:484
  50.3 13.5 %collective-permute-start.4 = (f32[30,512]{1,0:T(8,128)S(1)}, f32[30,512]{1,0:T(8,128)S(1)}, u32[]{:S(2)}, u32[]{:S(2)}) collective-permute-start(f32[30,512]{1,0:T(8,128)S(1)} %get-tuple-element.51), channel_id=1, source_target_pairs={{0,1},{1,2},{2,3},{3,4},{4,5},{5,6},{6,7},{7,8},{8,9},{9,10},{10,1... | collective-permute-start | bytes 184328 | tf_op jit(solution)/shard_map/ppermute | solution.py:485
  54.1 9.6 %collective-permute-start.5 = (f32[20,512]{1,0:T(8,128)S(1)}, f32[20,512]{1,0:T(8,128)S(1)}, u32[]{:S(2)}, u32[]{:S(2)}) collective-permute-start(f32[20,512]{1,0:T(8,128)S(1)} %get-tuple-element.52), channel_id=1, source_target_pairs={{1,0},{2,1},{3,2},{4,3},{5,4},{6,5},{7,6},{8,7},{9,8},{10,9},{11,1... | collective-permute-start | bytes 122888 | tf_op jit(solution)/shard_map/ppermute | solution.py:486
  68.9 1.7 %collective-permute-start.6 = (f32[16,16,256]{2,1,0:T(8,128)S(1)}, f32[16,16,256]{2,1,0:T(8,128)}, u32[]{:S(2)}, u32[]{:S(2)}) collective-permute-start(f32[16,16,256]{2,1,0:T(8,128)S(1)} %get-tuple-element.55), channel_id=1, source_target_pairs={{0,16},{1,17},{2,18},{3,19},{4,20},{5,21},{6,22},{7,23},{8,24},{9,... | collective-permute-start | bytes 786440 | tf_op jit(solution)/shard_map/ppermute | solution.py:483
  70.7 13.9 %all-to-all-start.2 = ((f32[16,16,256]{2,1,0:T(8,128)}), f32[16,16,256]{2,1,0:T(8,128)S(1)}, u32[]{:S(2)}, u32[]{:S(2)}) async-start(f32[16,16,256]{2,1,0:T(8,128)} %collective-permute-done.6), calls=%async_computation.2 | async-start | bytes 524288 | tf_op jit(solution)/shard_map/all_to_all | solution.py:484
  74.4 13.2 %collective-permute-start.7 = (f32[30,512]{1,0:T(8,128)S(1)}, f32[30,512]{1,0:T(8,128)S(1)}, u32[]{:S(2)}, u32[]{:S(2)}) collective-permute-start(f32[30,512]{1,0:T(8,128)S(1)} %get-tuple-element.58), channel_id=1, source_target_pairs={{0,1},{1,2},{2,3},{3,4},{4,5},{5,6},{6,7},{7,8},{8,9},{9,10},{10,1... | collective-permute-start | bytes 184328 | tf_op jit(solution)/shard_map/ppermute | solution.py:485
  78.2 9.4 %collective-permute-start.8 = (f32[20,512]{1,0:T(8,128)S(1)}, f32[20,512]{1,0:T(8,128)S(1)}, u32[]{:S(2)}, u32[]{:S(2)}) collective-permute-start(f32[20,512]{1,0:T(8,128)S(1)} %get-tuple-element.59), channel_id=1, source_target_pairs={{1,0},{2,1},{3,2},{4,3},{5,4},{6,5},{7,6},{8,7},{9,8},{10,9},{11,1... | collective-permute-start | bytes 122888 | tf_op jit(solution)/shard_map/ppermute | solution.py:486
  92.8 1.7 %collective-permute-start.9 = (f32[16,16,256]{2,1,0:T(8,128)S(1)}, f32[16,16,256]{2,1,0:T(8,128)}, u32[]{:S(2)}, u32[]{:S(2)}) collective-permute-start(f32[16,16,256]{2,1,0:T(8,128)S(1)} %get-tuple-element.62), channel_id=1, source_target_pairs={{0,16},{1,17},{2,18},{3,19},{4,20},{5,21},{6,22},{7,23},{8,24},{9,... | collective-permute-start | bytes 786440 | tf_op jit(solution)/shard_map/ppermute | solution.py:483
  94.5 14.1 %all-to-all-start.3 = ((f32[16,16,256]{2,1,0:T(8,128)}), f32[16,16,256]{2,1,0:T(8,128)S(1)}, u32[]{:S(2)}, u32[]{:S(2)}) async-start(f32[16,16,256]{2,1,0:T(8,128)} %collective-permute-done.9), calls=%async_computation.3 | async-start | bytes 524288 | tf_op jit(solution)/shard_map/all_to_all | solution.py:484
  98.5 13.1 %collective-permute-start.10 = (f32[30,512]{1,0:T(8,128)S(1)}, f32[30,512]{1,0:T(8,128)S(1)}, u32[]{:S(2)}, u32[]{:S(2)}) collective-permute-start(f32[30,512]{1,0:T(8,128)S(1)} %get-tuple-element.65), channel_id=1, source_target_pairs={{0,1},{1,2},{2,3},{3,4},{4,5},{5,6},{6,7},{7,8},{8,9},{9,10},{10,1... | collective-permute-start | bytes 184328 | tf_op jit(solution)/shard_map/ppermute | solution.py:485
  102.3 9.3 %collective-permute-start.11 = (f32[20,512]{1,0:T(8,128)S(1)}, f32[20,512]{1,0:T(8,128)S(1)}, u32[]{:S(2)}, u32[]{:S(2)}) collective-permute-start(f32[20,512]{1,0:T(8,128)S(1)} %get-tuple-element.66), channel_id=1, source_target_pairs={{1,0},{2,1},{3,2},{4,3},{5,4},{6,5},{7,6},{8,7},{9,8},{10,9},{11,1... | collective-permute-start | bytes 122888 | tf_op jit(solution)/shard_map/ppermute | solution.py:486

commit v3 on v2

--- a/solution.py
+++ b/solution.py
@@ -6,6 +6,7 @@
 from jax.experimental import pallas as pl
 from jax.experimental.pallas import tpu as pltpu
 from jax.sharding import PartitionSpec as P
+
 
 ITERS = 4
 
@@ -115,7 +116,8 @@
     acc_ref[...] += out if left.shape[0] == count else out[:count] + out[count:]
 
 
-def frozen_count(target_ref, rows, cols, acc_ref):
+def frozen_kernel(target_ref, movable_ref, acc_ref):
+    rows, cols = movable_ref.shape
     blocks, slots = target_ref.shape
     row_iota = lax.broadcasted_iota(jnp.int32, (rows, slots), 0)
     acc_ref[...] = jnp.zeros_like(acc_ref)
@@ -125,6 +127,7 @@
         add_product(acc_ref, jnp.where(row_iota == row, 1.0, 0.0).astype(BF16), one_hot(col, cols))
 
     repeat(blocks, one, 4)
+    movable_ref[...] = jnp.where(acc_ref[...] > 0.5, 0.0, 1.0)
 
 
 def place_own(arrived_ref, target_ref, comps, rows, cols, acc_ref):
@@ -140,7 +143,7 @@
     repeat(blocks, one)
 
 
-def place_halo(arrived_ref, first, target_ref, start, comps, cols, acc_ref, out_ref):
+def place_halo(arrived_ref, first, target_ref, start, comps, cols, acc_ref, out_ref, unroll=UNROLL):
     blocks, slots = target_ref.shape
     tiles = cols // LANES
     group = ROWS // 2
@@ -152,10 +155,13 @@
         row = row - start
         hit = row_iota == (col >> LANE_BITS) * group + (row & (group - 1))
         at = (row >> GROUP_BITS) * LANES + (col & (LANES - 1))
-        left = selected(hit, arrived_ref[b, first : first + comps, :])
+        if arrived_ref is None:
+            left = jnp.where(hit, 1.0, 0.0).astype(BF16)
+        else:
+            left = selected(hit, arrived_ref[b, first : first + comps, :])
         add_product(acc_ref, left, one_hot(at, 2 * LANES))
 
-    repeat(blocks, one)
+    repeat(blocks, one, unroll)
     for c in range(comps):
         for t in range(tiles):
             for h in range(2):
@@ -178,18 +184,18 @@
 
 def start_kernel(
     field_hbm, base_hbm, weight_hbm, target_hbm, source_hbm, inverse_hbm, coupling_hbm,
-    sums_ref, movable_ref, top_ref, bottom_ref,
-    field_ref, base_ref, weight_ref, target_ref, source_ref, inverse_ref, coupling_ref, acc_ref, sems,
+    sums_ref, top_ref, bottom_ref,
+    field_ref, base_ref, weight_ref, target_ref, source_ref, inverse_ref, coupling_ref, sems,
 ):
     comps, rows, cols = field_ref.shape
     blocks, slots = target_ref.shape
     last = slice(rows - ROWS, rows)
     first = slice(0, ROWS)
     copies = [
-        (target_hbm, target_ref),
         (field_hbm, field_ref),
         (base_hbm, base_ref),
         (weight_hbm, weight_ref),
+        (target_hbm, target_ref),
         (source_hbm.at[:, last], source_ref.at[0]),
         (source_hbm.at[:, first], source_ref.at[1]),
         (inverse_hbm.at[:, :, last], inverse_ref.at[0]),
@@ -200,24 +206,22 @@
     copies = [pltpu.make_async_copy(a, b, sems.at[i]) for i, (a, b) in enumerate(copies)]
     for copy in copies:
         copy.start()
-    copies[0].wait()
-    frozen_count(target_ref, rows, cols, acc_ref)
-    movable_ref[...] = jnp.where(acc_ref[...] > 0.5, 0.0, 1.0)
-    for copy in copies[1:4]:
+    for copy in copies[:3]:
         copy.wait()
     donor_sums(field_ref[...], base_ref, weight_ref, sums_ref)
-    border_rows(field_ref, movable_ref, top_ref, bottom_ref)
-    for copy in copies[4:]:
+    for c in range(comps):
+        top_ref[c * LOW : (c + 1) * LOW, :] = field_ref[c, rows - LOW :, :]
+        bottom_ref[c * HIGH : (c + 1) * HIGH, :] = field_ref[c, :HIGH, :]
+    for copy in copies[3:]:
         copy.wait()
     sides = (
-        (top_ref, 0, comps * LOW, LOW_DONE, ROWS - LOW_DONE, rows - ROWS),
-        (bottom_ref, 1, comps * HIGH, HIGH_DONE, 0, 0),
+        (top_ref, 0, comps * LOW, LOW_DONE, ROWS - LOW_DONE),
+        (bottom_ref, 1, comps * HIGH, HIGH_DONE, 0),
     )
-    for ref, side, offset, count, at, movable_at in sides:
+    for ref, side, offset, count, at in sides:
         fixed = [inverse_ref[side, v, w] for v in range(comps) for w in range(comps)]
         fixed += [source_ref[side, w] for w in range(comps)]
         fixed += [coupling_ref[side, i] for i in range(coupling_ref.shape[1])]
-        fixed.append(movable_ref[movable_at : movable_at + ROWS, :])
         for value in fixed:
             ref[offset : offset + count, :] = value[at : at + count, :]
             offset += count
@@ -229,16 +233,20 @@
 
 
 def unpack_kernel(
-    top_ref, bottom_ref, low_ref, high_ref, low_target_ref, high_target_ref, *, comps
+    top_ref, bottom_ref, low_ref, high_ref, low_target_ref, high_target_ref, below_ref, above_ref,
+    acc_ref, count_ref, *, comps, rows,
 ):
+    cols = top_ref.shape[1]
+    sublanes = lax.broadcasted_iota(jnp.int32, (ROWS, cols), 0)
     sides = (
-        (top_ref, comps * LOW, LOW_DONE, ROWS - LOW_DONE, low_ref, low_target_ref),
-        (bottom_ref, comps * HIGH, HIGH_DONE, 0, high_ref, high_target_ref),
+        (top_ref, LOW, LOW_DONE, ROWS - LOW, ROWS - LOW_DONE, rows - ROWS, low_ref, low_target_ref, below_ref),
+        (bottom_ref, HIGH, HIGH_DONE, 0, 0, 0, high_ref, high_target_ref, above_ref),
     )
-    for ref, offset, count, at, out_ref, target_ref in sides:
-        cols = ref.shape[1]
+    for ref, wide, count, wide_at, at, start, out_ref, target_ref, halo_ref in sides:
         blocks, slots = target_ref.shape
-        for i in range(out_ref.shape[0]):
+        offset = comps * wide
+        last = out_ref.shape[0] - 1
+        for i in range(last):
             out_ref[i] = jnp.zeros((ROWS, cols), F32)
             out_ref[i, at : at + count, :] = ref[offset : offset + count, :]
             offset += count
@@ -247,6 +255,15 @@
         for i in range(per):
             cells = ref[offset : offset + deep, i * slots : (i + 1) * slots]
             target_ref[i * deep : (i + 1) * deep, :] = cells.astype(jnp.int32)
+        place_halo(None, 0, target_ref, start, 1, cols, acc_ref, count_ref, 4)
+        movable = count_ref[0] < 0.5
+        done = (sublanes >= at) & (sublanes < at + count)
+        out_ref[last] = jnp.where(movable & done, 1.0, 0.0)
+        movable = count_ref[0, wide_at : wide_at + wide, :] < 0.5
+        for c in range(comps):
+            halo_ref[c * wide : (c + 1) * wide, :] = jnp.where(
+                movable, ref[c * wide : (c + 1) * wide, :], 0.0
+            )
 
 
 def place(
@@ -354,62 +371,40 @@
 
         return write
 
-    wait = work["wait"]
     for r in range(0, rows, ROWS):
-        wait(r)
         sections(u_ref, PAD + r, own(r), into(v_ref, PAD + r), is_near, 0, comps, cols)
-    wait("low")
     sections(u_ref, PAD - ROWS, packed(low_ref), into(v_ref, PAD - ROWS), is_near, 0, comps, cols)
-    wait("high")
     sections(u_ref, PAD + rows, packed(high_ref), into(v_ref, PAD + rows), is_near, 0, comps, cols)
     for r in range(0, rows, ROWS):
         sections(v_ref, PAD + r, own(r), into(out_ref, r), is_near, 1, comps, cols)
 
 
+def place_kernel(count, refs):
+    refs = list(refs)
+    operands, refs = refs[:6], refs[6:]
+    held, refs = refs[:count], refs[count:]
+    results, refs = refs[:3], refs[3:]
+    copied, (acc_ref, halo_ref, sems) = refs[:count], refs[count:]
+    copies = [pltpu.make_async_copy(held[i], copied[i], sems.at[i]) for i in range(count)]
+    for copy in copies:
+        copy.start()
+    place(*operands, *results, acc_ref, halo_ref)
+    for copy in copies:
+        copy.wait()
+
+
 def step_kernel(names, is_last, refs):
     refs = list(refs)
     operands, refs = refs[:6], refs[6:]
-    held, refs = refs[: len(names)], refs[len(names) :]
+    work, refs = dict(zip(names, refs)), refs[len(names) :]
     out_ref = refs.pop(0)
     if not is_last:
         sums_ref, top_ref, bottom_ref = refs[:3]
         refs = refs[3:]
-    copied, (u_ref, v_ref, sems) = refs[: len(names)], refs[len(names) :]
-    rows = out_ref.shape[1]
-    work = dict(zip(names, copied))
-    work.update(u=u_ref, v=v_ref)
-    copies = {}
-    count = 0
-
-    def copy(key, source, target):
-        nonlocal count
-        copies.setdefault(key, []).append(pltpu.make_async_copy(source, target, sems.at[count]))
-        count += 1
-
-    whole = dict(zip(names, held))
-    for r in range(0, rows, ROWS):
-        at = slice(r, r + ROWS)
-        copy(r, whole["inverse"].at[:, :, at], work["inverse"].at[:, :, at])
-        copy(r, whole["source"].at[:, at], work["source"].at[:, at])
-        copy(r, whole["coupling"].at[:, at], work["coupling"].at[:, at])
-    for name in names:
-        if name not in ("inverse", "source", "coupling"):
-            copy(name, whole[name], work[name])
-    for group in copies.values():
-        for one in group:
-            one.start()
-
-    def wait(key):
-        for one in copies[key]:
-            one.wait()
-
-    work["wait"] = wait
+    work["u"], work["v"] = refs
     sweep(*operands, work, out_ref)
     if not is_last:
-        movable_ref = operands[5]
-        border_rows(out_ref, movable_ref, top_ref, bottom_ref)
-        wait("base")
-        wait("weight")
+        border_rows(out_ref, operands[5], top_ref, bottom_ref)
         donor_sums(out_ref[...], work["base"], work["weight"], sums_ref)
 
 
@@ -451,15 +446,14 @@
     sums_shape = f32(blocks, -(-3 * comps // ROWS) * ROWS, slots)
     deep = blocks * slots // cols
 
-    sums, movable, top, bottom = call(
+    sums, top, bottom = call(
         start_kernel,
         (),
         (state, base, weight, target, source, inverse, coupling),
         (
             sums_shape,
-            f32(rows, cols),
-            f32(comps * LOW + fixed * LOW_DONE + deep, cols),
-            f32(comps * HIGH + fixed * HIGH_DONE + deep, cols),
+            f32(comps * LOW + (fixed - 1) * LOW_DONE + deep, cols),
+            f32(comps * HIGH + (fixed - 1) * HIGH_DONE + deep, cols),
         ),
         [
             vmem_like(comps, rows, cols),
@@ -469,7 +463,6 @@
             vmem_like(2, comps, ROWS, cols),
             vmem_like(2, comps, comps, ROWS, cols),
             vmem_like(2, faces, ROWS, cols),
-            vmem_like(rows, cols),
             pltpu.SemaphoreType.DMA((10,)),
         ],
     )
@@ -487,28 +480,31 @@
         is_last = iteration == ITERS - 1
         if iteration == 0:
             cells_of = jax.ShapeDtypeStruct((blocks, slots), jnp.int32)
-            held["low"], held["high"], low_target, high_target = call(
-                partial(unpack_kernel, comps=comps),
+            (movable,) = call(
+                frozen_kernel, (target,), (), (f32(rows, cols),), [vmem_like(rows, cols)]
+            )
+            held["low"], held["high"], low_target, high_target, below, above = call(
+                partial(unpack_kernel, comps=comps, rows=rows),
                 (below, above),
                 (),
-                (f32(fixed, ROWS, cols), f32(fixed, ROWS, cols), cells_of, cells_of),
-                [],
+                (f32(fixed, ROWS, cols), f32(fixed, ROWS, cols), cells_of, cells_of, *border),
+                [vmem_like((cols // LANES) * (ROWS // 2), 2 * LANES), vmem_like(1, ROWS, cols)],
             )
-        state, placed_below, placed_above = call(
-            place,
+        names = tuple(held)
+        near = tuple(pltpu.VMEM(held[name].shape, held[name].dtype) for name in names)
+        state, placed_below, placed_above, *near = call(
+            lambda *refs: place_kernel(len(names), refs),
             (arrived, target, state, movable, low_target, high_target),
-            (),
-            (cells, halo, halo),
-            placing,
-        )
-        names = tuple(name for name in held if not (is_last and name in ("base", "weight")))
-        copied = [vmem_like(*held[name].shape, dtype=held[name].dtype) for name in names]
+            tuple(held[name] for name in names),
+            (cells, halo, halo, *near),
+            placing + [pltpu.SemaphoreType.DMA((len(names),))],
+        )
         results = call(
             lambda *refs: step_kernel(names, is_last, refs),
-            (state, below, above, placed_below, placed_above, movable),
-            tuple(held[name] for name in names),
+            (state, below, above, placed_below, placed_above, movable, *near),
+            (),
             (cells,) if is_last else (cells, sums_shape, *border),
-            copied + working + [pltpu.SemaphoreType.DMA((3 * (rows // ROWS) + len(names),))],
+            working,
         )
         state = results[0]
         if not is_last:

time: 116 us -> 111 us (0.957)
  Pallas kernels: 36.1 us -> 33 us
  waiting for transfers between devices: 34.4 us -> 32.3 us
    pallas_call x10 -> x11, Pallas kernels: 36.1 us -> 33 us  [call(): pl.pallas_call(kernel, out_shape=outs, in_specs=vmem(len(operands)) + [pl...]
    ppermute x4, waiting for transfers between devices: 12.7 us -> 10.7 us  [on_device(): above = lax.ppermute(bottom, 'blk', down)]
  transfers between devices with their start and end apart: 16 -> 16, of which waited for: 8 -> 8; matrix products, arithmetic and copies ran while one was open for 0% -> 0% of each run, Pallas kernels for 8% -> 12%
where the time goes in v3:
time: 111 us; the launch traced here: 110 us
  starting transfers between devices  43 us (39%)
  Pallas kernels  33 us (30%)
  waiting for transfers between devices  32.3 us (29%)
  local copies, waits for them, and re-layouts  1.62 us (1%)
    pallas_call x11, Pallas kernels, call(): pl.pallas_call(kernel, out_shape=outs, in_specs=vmem(len(operands)) + [pl...  33 us
    all_to_all x4, starting transfers between devices, on_device(): lax.all_to_all(arrived, 'blk', split_axis=0, concat_axis=0, tiled=True)  21.5 us
    all_to_all x4, waiting for transfers between devices, on_device(): lax.all_to_all(arrived, 'blk', split_axis=0, concat_axis=0, tiled=True)  15.6 us
    ppermute x4, starting transfers between devices, on_device(): below = lax.ppermute(top, 'blk', up)  15.3 us
    ppermute x4, waiting for transfers between devices, on_device(): above = lax.ppermute(bottom, 'blk', down)  10.7 us
    ppermute x4, waiting for transfers between devices, on_device(): arrived = lax.ppermute(sums, ('group', 'blk'), swap)  6 us
    ppermute x4, starting transfers between devices, on_device(): above = lax.ppermute(bottom, 'blk', down)  5.17 us
  transfers between devices with their start and end apart: 16, of which 8 were waited for; matrix products, arithmetic and copies ran while one was open for 0% of the time, Pallas kernels for 12%

profile of v3, /device:TPU:0, one launch (start us, length us, event | category | flops | bytes accessed | tf_op | source)
XLA Modules:
  0.0 110.2 jit_solution(7216991092175169442)
XLA Ops:
  0.0 3.7 %shard_map.73 = (f32[16,16,256]{2,1,0:T(8,128)S(1)}, f32[140,512]{1,0:T(8,128)S(1)}, f32[96,512]{1,0:T(8,128)S(1)}) custom-call(f32[5,32,512]{2,1,0:T(8,128)} %bitcast.8, s32[16,256]{1,0:T(8,128)} %bitcast.36, f32[4,16,256]{2,1,0:T(8,128)} %bitcast.31, s32[16,256]{1,0:T(8,128)} %bitcast.10, f32[5,32,512]{2,1,0:T(8,128)} %bitcast.21, ...), custom_call_target="tpu_custom_call" | custom-call | tf_op jit(solution)/shard_map/pallas_call | solution.py:432
  3.7 0.6 collective-permute-start
  4.2 1.3 %collective-permute-done = f32[16,16,256]{2,1,0:T(8,128)} collective-permute-done((f32[16,16,256]{2,1,0:T(8,128)S(1)}, f32[16,16,256]{2,1,0:T(8,128)}, u32[]{:S(2)}, u32[]{:S(2)}) %collective-permute-start) | collective-permute-done | bytes 262176 | tf_op jit(solution)/shard_map/ppermute | solution.py:476
  5.5 8.2 %all-to-all-start = ((f32[16,16,256]{2,1,0:T(8,128)}), f32[16,16,256]{2,1,0:T(8,128)S(1)}, u32[]{:S(2)}, u32[]{:S(2)}) async-start(f32[16,16,256]{2,1,0:T(8,128)} %collective-permute-done), calls=%async_computation | async-start | bytes 524288 | tf_op jit(solution)/shard_map/all_to_all | solution.py:477
  13.8 3.8 %collective-permute-start.1 = (f32[140,512]{1,0:T(8,128)S(1)}, f32[140,512]{1,0:T(8,128)S(1)}, u32[]{:S(2)}, u32[]{:S(2)}) collective-permute-start(f32[140,512]{1,0:T(8,128)S(1)} %get-tuple-element.67), channel_id=1, source_target_pairs={{0,1},{1,2},{2,3},{3,4},{4,5},{5,6},{6,7},{7,8},{8,9},{9,10},{10,1... | collective-permute-start | bytes 860168 | tf_op jit(solution)/shard_map/ppermute | solution.py:478
  17.6 1.3 %collective-permute-start.2 = (f32[96,512]{1,0:T(8,128)S(1)}, f32[96,512]{1,0:T(8,128)S(1)}, u32[]{:S(2)}, u32[]{:S(2)}) collective-permute-start(f32[96,512]{1,0:T(8,128)S(1)} %get-tuple-element.68), channel_id=1, source_target_pairs={{1,0},{2,1},{3,2},{4,3},{5,4},{6,5},{7,6},{8,7},{9,8},{10,9},{11,1... | collective-permute-start | bytes 589832 | tf_op jit(solution)/shard_map/ppermute | solution.py:479
  18.9 0.0 copy-done.3
  18.9 1.7 %shard_map.74.refs_3_.refs_5_ = f32[32,512]{1,0:T(8,128)S(1)} custom-call(s32[16,256]{1,0:T(8,128)S(1)} %bitcast.11), custom_call_target="tpu_custom_call" | custom-call | tf_op jit(solution)/shard_map/pallas_call | solution.py:432
  20.6 10.7 %collective-permute-done.2.bottom_ref = f32[96,512]{1,0:T(8,128)S(1)} collective-permute-done((f32[96,512]{1,0:T(8,128)S(1)}, f32[96,512]{1,0:T(8,128)S(1)}, u32[]{:S(2)}, u32[]{:S(2)}) %collective-permute-start.2) | collective-permute-done | bytes 196640 | tf_op jit(solution)/shard_map/ppermute | solution.py:479
  31.3 0.0 collective-permute-done.1.top_ref
  31.3 2.4 %shard_map.75 = (f32[35,8,512]{2,1,0:T(8,128)S(1)}, f32[35,8,512]{2,1,0:T(8,128)S(1)}, s32[16,256]{1,0:T(8,128)S(1)}, s32[16,256]{1,0:T(8,128)S(1)}, f32[30,512]{1,0:T(8,128)S(1)}, /*index=5*/f32[20,512]{1,0:T(8,128)S(1)}) custom-call(f32[140,512]{1,0:T(8,128)S(1)} %collective-permute-done.1.top_ref, f32[96,512]{1,0:T(8,128)S(1)} %collective-permute-done.2.bottom_ref), custom_call_target="tpu_custom_call" | custom-call | tf_op jit(solution)/shard_map/pallas_call | solution.py:432
  33.7 0.0 copy-start
  33.7 0.8 copy-done
  34.5 0.8 copy-done.1
  35.3 0.0 all-to-all-done.refs_0_
  35.3 0.0 copy-done.2
  35.3 3.0 %shard_map.76 = (f32[5,32,512]{2,1,0:T(8,128)S(1)}, f32[5,8,512]{2,1,0:T(8,128)S(1)}, f32[5,8,512]{2,1,0:T(8,128)S(1)}, f32[5,32,512]{2,1,0:T(8,128)S(1)}, f32[5...) custom-call(f32[16,16,256]{2,1,0:T(8,128)S(1)} %all-to-all-done.refs, ...), custom_call_target="tpu_custom_call" | custom-call | tf_op jit(solution)/shard_map/pallas_call | solution.py:432
  38.3 3.7 %shard_map.77 = (f32[5,32,512]{2,1,0:T(8,128)S(1)}, f32[16,16,256]{2,1,0:T(8,128)S(1)}, f32[30,512]{1,0:T(8,128)S(1)}, f32[20,512]{1,0:T(8,128)S(1)}) custom-call(f32[5,32,512]{2,1,0:T(8,128)S(1)} %get-tuple-element.73.refs_0_, f32[30,512]{1,0:T(8,128)S(1)} %get-tuple-element.74.refs_1_, f32[20,512]{1,0:T(8,128)S(1)} %get-tuple-element.75.refs_2_, ...), custom_call_target="tpu_custom_call" | custom-call | tf_op jit(solution)/shard_map/pallas_call | solution.py:432
  42.0 0.3 collective-permute-start.3
  42.3 1.4 %collective-permute-done.3 = f32[16,16,256]{2,1,0:T(8,128)} collective-permute-done((f32[16,16,256]{2,1,0:T(8,128)S(1)}, f32[16,16,256]{2,1,0:T(8,128)}, u32[]{:S(2)}, u32[]{:S(2)}) %collective-permute-start.3) | collective-permute-done | bytes 262176 | tf_op jit(solution)/shard_map/ppermute | solution.py:476
  43.7 5.9 %all-to-all-start.1 = ((f32[16,16,256]{2,1,0:T(8,128)}), f32[16,16,256]{2,1,0:T(8,128)S(1)}, u32[]{:S(2)}, u32[]{:S(2)}) async-start(f32[16,16,256]{2,1,0:T(8,128)} %collective-permute-done.3), calls=%async_computation.1 | async-start | bytes 524288 | tf_op jit(solution)/shard_map/all_to_all | solution.py:477
  49.6 3.8 %collective-permute-start.4 = (f32[30,512]{1,0:T(8,128)S(1)}, f32[30,512]{1,0:T(8,128)S(1)}, u32[]{:S(2)}, u32[]{:S(2)}) collective-permute-start(f32[30,512]{1,0:T(8,128)S(1)} %get-tuple-element.88), channel_id=1, source_target_pairs={{0,1},{1,2},{2,3},{3,4},{4,5},{5,6},{6,7},{7,8},{8,9},{9,10},{10,1... | collective-permute-start | bytes 184328 | tf_op jit(solution)/shard_map/ppermute | solution.py:478
  53.5 1.3 %collective-permute-start.5 = (f32[20,512]{1,0:T(8,128)S(1)}, f32[20,512]{1,0:T(8,128)S(1)}, u32[]{:S(2)}, u32[]{:S(2)}) collective-permute-start(f32[20,512]{1,0:T(8,128)S(1)} %get-tuple-element.89), channel_id=1, source_target_pairs={{1,0},{2,1},{3,2},{4,3},{5,4},{6,5},{7,6},{8,7},{9,8},{10,9},{11,1... | collective-permute-start | bytes 122888 | tf_op jit(solution)/shard_map/ppermute | solution.py:479
  54.8 5.4 %all-to-all-done.1.refs_0_ = f32[16,16,256]{2,1,0:T(8,128)S(1)} async-done(((f32[16,16,256]{2,1,0:T(8,128)}), f32[16,16,256]{2,1,0:T(8,128)S(1)}, u32[]{:S(2)}, u32[]{:S(2)}) %all-to-all-start.1) | async-done | bytes 262176 | tf_op jit(solution)/shard_map/all_to_all | solution.py:477
  60.1 3.0 %shard_map.78 = (f32[5,32,512]{2,1,0:T(8,128)S(1)}, f32[5,8,512]{2,1,0:T(8,128)S(1)}, f32[5,8,512]{2,1,0:T(8,128)S(1)}, f32[5,32,512]{2,1,0:T(8,128)S(1)}, f32[5...) custom-call(f32[16,16,256]{2,1,0:T(8,128)S(1)} %all-to-all-done.1.re, ...), custom_call_target="tpu_custom_call" | custom-call | tf_op jit(solution)/shard_map/pallas_call | solution.py:432
  63.2 0.0 collective-permute-done.5.refs_2_
  63.2 0.0 collective-permute-done.4.refs_1_
  63.2 3.7 %shard_map.79 = (f32[5,32,512]{2,1,0:T(8,128)S(1)}, f32[16,16,256]{2,1,0:T(8,128)S(1)}, f32[30,512]{1,0:T(8,128)S(1)}, f32[20,512]{1,0:T(8,128)S(1)}) custom-call(f32[5,32,512]{2,1,0:T(8,128)S(1)} %get-tuple-element.87.refs_0_, f32[30,512]{1,0:T(8,128)S(1)} %collective-permute-done.4.refs_1_, f32[20,512]{1,0:T(8,128)S(1)} %collective-permute-done.5.refs_2_, ...), custom_call_target="tpu_custom_call" | custom-call | tf_op jit(solution)/shard_map/pallas_call | solution.py:432
  66.8 0.1 collective-permute-start.6
  66.9 1.7 %collective-permute-done.6 = f32[16,16,256]{2,1,0:T(8,128)} collective-permute-done((f32[16,16,256]{2,1,0:T(8,128)S(1)}, f32[16,16,256]{2,1,0:T(8,128)}, u32[]{:S(2)}, u32[]{:S(2)}) %collective-permute-start.6) | collective-permute-done | bytes 262176 | tf_op jit(solution)/shard_map/ppermute | solution.py:476
  68.6 3.6 %all-to-all-start.2 = ((f32[16,16,256]{2,1,0:T(8,128)}), f32[16,16,256]{2,1,0:T(8,128)S(1)}, u32[]{:S(2)}, u32[]{:S(2)}) async-start(f32[16,16,256]{2,1,0:T(8,128)} %collective-permute-done.6), calls=%async_computation.2 | async-start | bytes 524288 | tf_op jit(solution)/shard_map/all_to_all | solution.py:477
  72.2 3.8 %collective-permute-start.7 = (f32[30,512]{1,0:T(8,128)S(1)}, f32[30,512]{1,0:T(8,128)S(1)}, u32[]{:S(2)}, u32[]{:S(2)}) collective-permute-start(f32[30,512]{1,0:T(8,128)S(1)} %get-tuple-element.102), channel_id=1, source_target_pairs={{0,1},{1,2},{2,3},{3,4},{4,5},{5,6},{6,7},{7,8},{8,9},{9,10},{10,1... | collective-permute-start | bytes 184328 | tf_op jit(solution)/shard_map/ppermute | solution.py:478
  76.0 1.3 %collective-permute-start.8 = (f32[20,512]{1,0:T(8,128)S(1)}, f32[20,512]{1,0:T(8,128)S(1)}, u32[]{:S(2)}, u32[]{:S(2)}) collective-permute-start(f32[20,512]{1,0:T(8,128)S(1)} %get-tuple-element.103), channel_id=1, source_target_pairs={{1,0},{2,1},{3,2},{4,3},{5,4},{6,5},{7,6},{8,7},{9,8},{10,9},{11,1... | collective-permute-start | bytes 122888 | tf_op jit(solution)/shard_map/ppermute | solution.py:479
  77.3 5.2 %all-to-all-done.2.refs_0_ = f32[16,16,256]{2,1,0:T(8,128)S(1)} async-done(((f32[16,16,256]{2,1,0:T(8,128)}), f32[16,16,256]{2,1,0:T(8,128)S(1)}, u32[]{:S(2)}, u32[]{:S(2)}) %all-to-all-start.2) | async-done | bytes 262176 | tf_op jit(solution)/shard_map/all_to_all | solution.py:477
  82.5 3.0 %shard_map.80 = (f32[5,32,512]{2,1,0:T(8,128)S(1)}, f32[5,8,512]{2,1,0:T(8,128)S(1)}, f32[5,8,512]{2,1,0:T(8,128)S(1)}, f32[5,32,512]{2,1,0:T(8,128)S(1)}, f32[5...) custom-call(f32[16,16,256]{2,1,0:T(8,128)S(1)} %all-to-all-done.2.re, ...), custom_call_target="tpu_custom_call" | custom-call | tf_op jit(solution)/shard_map/pallas_call | solution.py:432
  85.6 0.0 collective-permute-done.8.refs_2_
  85.6 0.0 collective-permute-done.7.refs_1_
  85.6 3.9 %shard_map.81 = (f32[5,32,512]{2,1,0:T(8,128)S(1)}, f32[16,16,256]{2,1,0:T(8,128)S(1)}, f32[30,512]{1,0:T(8,128)S(1)}, f32[20,512]{1,0:T(8,128)S(1)}) custom-call(f32[5,32,512]{2,1,0:T(8,128)S(1)} %get-tuple-element.101.refs_0_, f32[30,512]{1,0:T(8,128)S(1)} %collective-permute-done.7.refs_1_, f32[20,512]{1,0:T(8,128)S(1)} %collective-permute-done.8.refs_2_, ...), custom_call_target="tpu_custom_call" | custom-call | tf_op jit(solution)/shard_map/pallas_call | solution.py:432
  89.5 0.1 collective-permute-start.9
  89.5 1.7 %collective-permute-done.9 = f32[16,16,256]{2,1,0:T(8,128)} collective-permute-done((f32[16,16,256]{2,1,0:T(8,128)S(1)}, f32[16,16,256]{2,1,0:T(8,128)}, u32[]{:S(2)}, u32[]{:S(2)}) %collective-permute-start.9) | collective-permute-done | bytes 262176 | tf_op jit(solution)/shard_map/ppermute | solution.py:476
  91.2 3.8 %all-to-all-start.3 = ((f32[16,16,256]{2,1,0:T(8,128)}), f32[16,16,256]{2,1,0:T(8,128)S(1)}, u32[]{:S(2)}, u32[]{:S(2)}) async-start(f32[16,16,256]{2,1,0:T(8,128)} %collective-permute-done.9), calls=%async_computation.3 | async-start | bytes 524288 | tf_op jit(solution)/shard_map/all_to_all | solution.py:477
  95.0 3.8 %collective-permute-start.10 = (f32[30,512]{1,0:T(8,128)S(1)}, f32[30,512]{1,0:T(8,128)S(1)}, u32[]{:S(2)}, u32[]{:S(2)}) collective-permute-start(f32[30,512]{1,0:T(8,128)S(1)} %get-tuple-element.116), channel_id=1, source_target_pairs={{0,1},{1,2},{2,3},{3,4},{4,5},{5,6},{6,7},{7,8},{8,9},{9,10},{10,1... | collective-permute-start | bytes 184328 | tf_op jit(solution)/shard_map/ppermute | solution.py:478
  98.8 1.3 %collective-permute-start.11 = (f32[20,512]{1,0:T(8,128)S(1)}, f32[20,512]{1,0:T(8,128)S(1)}, u32[]{:S(2)}, u32[]{:S(2)}) collective-permute-start(f32[20,512]{1,0:T(8,128)S(1)} %get-tuple-element.117), channel_id=1, source_target_pairs={{1,0},{2,1},{3,2},{4,3},{5,4},{6,5},{7,6},{8,7},{9,8},{10,9},{11,1... | collective-permute-start | bytes 122888 | tf_op jit(solution)/shard_map/ppermute | solution.py:479
  100.1 5.0 %all-to-all-done.3.refs_0_ = f32[16,16,256]{2,1,0:T(8,128)S(1)} async-done(((f32[16,16,256]{2,1,0:T(8,128)}), f32[16,16,256]{2,1,0:T(8,128)S(1)}, u32[]{:S(2)}, u32[]{:S(2)}) %all-to-all-start.3) | async-done | bytes 262176 | tf_op jit(solution)/shard_map/all_to_all | solution.py:477
  105.2 3.0 %shard_map.82 = (f32[5,32,512]{2,1,0:T(8,128)S(1)}, f32[5,8,512]{2,1,0:T(8,128)S(1)}, f32[5,8,512]{2,1,0:T(8,128)S(1)}, f32[5,32,512]{2,1,0:T(8,128)S(1)}, f32[5...) custom-call(f32[16,16,256]{2,1,0:T(8,128)S(1)} %all-to-all-done.3.re, ...), custom_call_target="tpu_custom_call" | custom-call | tf_op jit(solution)/shard_map/pallas_call | solution.py:432
  108.2 0.0 collective-permute-done.11.refs_2_
  108.2 0.0 collective-permute-done.10.refs_1_
  108.2 2.0 %shard_map.83 = f32[5,32,512]{2,1,0:T(8,128)} custom-call(f32[5,32,512]{2,1,0:T(8,128)S(1)} %get-tuple-element.115.refs_0_, f32[30,512]{1,0:T(8,128)S(1)} %collective-permute-done.10.refs_1_, f32[20,512]{1,0:T(8,128)S(1)} %collective-permute-done.11.refs_2_, f32[5,8,512]{2,1,0:T(8,128)S(1)} %get-tuple-element.118.refs_3_, ...), custom_call_target="tpu_custom_call" | custom-call | tf_op jit(solution)/shard_map/pallas_call | solution.py:432
  (3 shorter events, 0.0 us)
Async XLA Ops:
  0.0 18.9 %copy-start.3 = (s32[1,1,16,256]{3,2,1,0:T(8,128)S(1)}, s32[1,1,16,256]{3,2,1,0:T(8,128)}, u32[]{:S(2)}) copy-start(s32[1,1,16,256]{3,2,1,0:T(8,128)} %param.13) | copy-start | bytes 49156
  0.0 35.3 %copy-start.2 = (f32[1,1,5,32,512]{4,3,2,1,0:T(8,128)S(1)}, f32[1,1,5,32,512]{4,3,2,1,0:T(8,128)}, u32[]{:S(2)}) copy-start(f32[1,1,5,32,512]{4,3,2,1,0:T(8,128)} %param.7) | copy-start | bytes 983044
  3.7 1.9 %collective-permute-start = (f32[16,16,256]{2,1,0:T(8,128)S(1)}, f32[16,16,256]{2,1,0:T(8,128)}, u32[]{:S(2)}, u32[]{:S(2)}) collective-permute-start(f32[16,16,256]{2,1,0:T(8,128)S(1)} %get-tuple-element.66), channel_id=1, source_target_pairs={{0,16},{1,17},{2,18},{3,19},{4,20},{5,21},{6,22},{7,23},{8,24},{9,... | collective-permute-start | bytes 786440 | tf_op jit(solution)/shard_map/ppermute | solution.py:476
  5.5 29.8 %all-to-all-start = ((f32[16,16,256]{2,1,0:T(8,128)}), f32[16,16,256]{2,1,0:T(8,128)S(1)}, u32[]{:S(2)}, u32[]{:S(2)}) async-start(f32[16,16,256]{2,1,0:T(8,128)} %collective-permute-done), calls=%async_computation | async-start | bytes 524288 | tf_op jit(solution)/shard_map/all_to_all | solution.py:477
  13.8 17.5 %collective-permute-start.1 = (f32[140,512]{1,0:T(8,128)S(1)}, f32[140,512]{1,0:T(8,128)S(1)}, u32[]{:S(2)}, u32[]{:S(2)}) collective-permute-start(f32[140,512]{1,0:T(8,128)S(1)} %get-tuple-element.67), channel_id=1, source_target_pairs={{0,1},{1,2},{2,3},{3,4},{4,5},{5,6},{6,7},{7,8},{8,9},{9,10},{10,1... | collective-permute-start | bytes 860168 | tf_op jit(solution)/shard_map/ppermute | solution.py:478
  17.6 13.7 %collective-permute-start.2 = (f32[96,512]{1,0:T(8,128)S(1)}, f32[96,512]{1,0:T(8,128)S(1)}, u32[]{:S(2)}, u32[]{:S(2)}) collective-permute-start(f32[96,512]{1,0:T(8,128)S(1)} %get-tuple-element.68), channel_id=1, source_target_pairs={{1,0},{2,1},{3,2},{4,3},{5,4},{6,5},{7,6},{8,7},{9,8},{10,9},{11,1... | collective-permute-start | bytes 589832 | tf_op jit(solution)/shard_map/ppermute | solution.py:479
  33.7 0.8 copy-start
  34.5 0.8 copy-start.1
  42.0 1.7 %collective-permute-start.3 = (f32[16,16,256]{2,1,0:T(8,128)S(1)}, f32[16,16,256]{2,1,0:T(8,128)}, u32[]{:S(2)}, u32[]{:S(2)}) collective-permute-start(f32[16,16,256]{2,1,0:T(8,128)S(1)} %get-tuple-element.85), channel_id=1, source_target_pairs={{0,16},{1,17},{2,18},{3,19},{4,20},{5,21},{6,22},{7,23},{8,24},{9,... | collective-permute-start | bytes 786440 | tf_op jit(solution)/shard_map/ppermute | solution.py:476
  43.7 16.4 %all-to-all-start.1 = ((f32[16,16,256]{2,1,0:T(8,128)}), f32[16,16,256]{2,1,0:T(8,128)S(1)}, u32[]{:S(2)}, u32[]{:S(2)}) async-start(f32[16,16,256]{2,1,0:T(8,128)} %collective-permute-done.3), calls=%async_computation.1 | async-start | bytes 524288 | tf_op jit(solution)/shard_map/all_to_all | solution.py:477
  49.6 13.5 %collective-permute-start.4 = (f32[30,512]{1,0:T(8,128)S(1)}, f32[30,512]{1,0:T(8,128)S(1)}, u32[]{:S(2)}, u32[]{:S(2)}) collective-permute-start(f32[30,512]{1,0:T(8,128)S(1)} %get-tuple-element.88), channel_id=1, source_target_pairs={{0,1},{1,2},{2,3},{3,4},{4,5},{5,6},{6,7},{7,8},{8,9},{9,10},{10,1... | collective-permute-start | bytes 184328 | tf_op jit(solution)/shard_map/ppermute | solution.py:478
  53.5 9.7 %collective-permute-start.5 = (f32[20,512]{1,0:T(8,128)S(1)}, f32[20,512]{1,0:T(8,128)S(1)}, u32[]{:S(2)}, u32[]{:S(2)}) collective-permute-start(f32[20,512]{1,0:T(8,128)S(1)} %get-tuple-element.89), channel_id=1, source_target_pairs={{1,0},{2,1},{3,2},{4,3},{5,4},{6,5},{7,6},{8,7},{9,8},{10,9},{11,1... | collective-permute-start | bytes 122888 | tf_op jit(solution)/shard_map/ppermute | solution.py:479
  66.8 1.7 %collective-permute-start.6 = (f32[16,16,256]{2,1,0:T(8,128)S(1)}, f32[16,16,256]{2,1,0:T(8,128)}, u32[]{:S(2)}, u32[]{:S(2)}) collective-permute-start(f32[16,16,256]{2,1,0:T(8,128)S(1)} %get-tuple-element.99), channel_id=1, source_target_pairs={{0,16},{1,17},{2,18},{3,19},{4,20},{5,21},{6,22},{7,23},{8,24},{9,... | collective-permute-start | bytes 786440 | tf_op jit(solution)/shard_map/ppermute | solution.py:476
  68.6 13.9 %all-to-all-start.2 = ((f32[16,16,256]{2,1,0:T(8,128)}), f32[16,16,256]{2,1,0:T(8,128)S(1)}, u32[]{:S(2)}, u32[]{:S(2)}) async-start(f32[16,16,256]{2,1,0:T(8,128)} %collective-permute-done.6), calls=%async_computation.2 | async-start | bytes 524288 | tf_op jit(solution)/shard_map/all_to_all | solution.py:477
  72.2 13.4 %collective-permute-start.7 = (f32[30,512]{1,0:T(8,128)S(1)}, f32[30,512]{1,0:T(8,128)S(1)}, u32[]{:S(2)}, u32[]{:S(2)}) collective-permute-start(f32[30,512]{1,0:T(8,128)S(1)} %get-tuple-element.102), channel_id=1, source_target_pairs={{0,1},{1,2},{2,3},{3,4},{4,5},{5,6},{6,7},{7,8},{8,9},{9,10},{10,1... | collective-permute-start | bytes 184328 | tf_op jit(solution)/shard_map/ppermute | solution.py:478
  76.0 9.5 %collective-permute-start.8 = (f32[20,512]{1,0:T(8,128)S(1)}, f32[20,512]{1,0:T(8,128)S(1)}, u32[]{:S(2)}, u32[]{:S(2)}) collective-permute-start(f32[20,512]{1,0:T(8,128)S(1)} %get-tuple-element.103), channel_id=1, source_target_pairs={{1,0},{2,1},{3,2},{4,3},{5,4},{6,5},{7,6},{8,7},{9,8},{10,9},{11,1... | collective-permute-start | bytes 122888 | tf_op jit(solution)/shard_map/ppermute | solution.py:479
  89.5 1.7 %collective-permute-start.9 = (f32[16,16,256]{2,1,0:T(8,128)S(1)}, f32[16,16,256]{2,1,0:T(8,128)}, u32[]{:S(2)}, u32[]{:S(2)}) collective-permute-start(f32[16,16,256]{2,1,0:T(8,128)S(1)} %get-tuple-element.113), channel_id=1, source_target_pairs={{0,16},{1,17},{2,18},{3,19},{4,20},{5,21},{6,22},{7,23},{8,24},{9,... | collective-permute-start | bytes 786440 | tf_op jit(solution)/shard_map/ppermute | solution.py:476
  91.2 14.0 %all-to-all-start.3 = ((f32[16,16,256]{2,1,0:T(8,128)}), f32[16,16,256]{2,1,0:T(8,128)S(1)}, u32[]{:S(2)}, u32[]{:S(2)}) async-start(f32[16,16,256]{2,1,0:T(8,128)} %collective-permute-done.9), calls=%async_computation.3 | async-start | bytes 524288 | tf_op jit(solution)/shard_map/all_to_all | solution.py:477
  95.0 13.2 %collective-permute-start.10 = (f32[30,512]{1,0:T(8,128)S(1)}, f32[30,512]{1,0:T(8,128)S(1)}, u32[]{:S(2)}, u32[]{:S(2)}) collective-permute-start(f32[30,512]{1,0:T(8,128)S(1)} %get-tuple-element.116), channel_id=1, source_target_pairs={{0,1},{1,2},{2,3},{3,4},{4,5},{5,6},{6,7},{7,8},{8,9},{9,10},{10,1... | collective-permute-start | bytes 184328 | tf_op jit(solution)/shard_map/ppermute | solution.py:478
  98.8 9.4 %collective-permute-start.11 = (f32[20,512]{1,0:T(8,128)S(1)}, f32[20,512]{1,0:T(8,128)S(1)}, u32[]{:S(2)}, u32[]{:S(2)}) collective-permute-start(f32[20,512]{1,0:T(8,128)S(1)} %get-tuple-element.117), channel_id=1, source_target_pairs={{1,0},{2,1},{3,2},{4,3},{5,4},{6,5},{7,6},{8,7},{9,8},{10,9},{11,1... | collective-permute-start | bytes 122888 | tf_op jit(solution)/shard_map/ppermute | solution.py:479

commit v4 on v3

--- a/solution.py
+++ b/solution.py
@@ -35,9 +35,14 @@
     return quotient, value - quotient * size
 
 
-def one_hot(index, size):
+def one_hot(index, size, packed=False):
     rows = lax.broadcasted_iota(jnp.int32, (size, index.shape[1]), 0)
-    return jnp.where(rows == index, 1.0, 0.0).astype(BF16)
+    if size > 512 or not packed:
+        return jnp.where(rows == index, 1.0, 0.0).astype(BF16)
+    middle = size // 2
+    rows = (rows - middle).astype(F32).astype(BF16)
+    index = (index - middle).astype(F32).astype(BF16)
+    return jnp.where(rows == index, jnp.array(1.0, BF16), jnp.array(0.0, BF16))
 
 
 def split(value):
@@ -76,8 +81,8 @@
         odd_at = col >> 1
         even_at = jnp.where(wraps, 0, (col + 1) >> 1)
         even_row = row + jnp.where(wraps, 1, 0)
-        picked_even = jnp.dot(even, one_hot(even_at, half), preferred_element_type=F32)
-        picked_odd = jnp.dot(odd, one_hot(odd_at, half), preferred_element_type=F32)
+        picked_even = jnp.dot(even, one_hot(even_at, half, True), preferred_element_type=F32)
+        picked_odd = jnp.dot(odd, one_hot(odd_at, half, True), preferred_element_type=F32)
         count = comps * rows
         picked_even = (picked_even[:count] + picked_even[count:]).reshape(comps, rows, slots)
         picked_odd = (picked_odd[:count] + picked_odd[count:]).reshape(comps, rows, slots)
@@ -279,13 +284,24 @@
     place_halo(arrived_ref, 2 * comps, high_target_ref, 0, comps, cols, halo_ref, above_ref)
 
 
+def load(ref, c, start, count):
+    return jnp.concatenate(
+        [ref[c, t, start : start + count, :] for t in range(ref.shape[1])], axis=1
+    )
+
+
+def store(ref, c, start, value):
+    for t in range(ref.shape[1]):
+        ref[c, t, start : start + value.shape[0], :] = value[:, t * LANES : (t + 1) * LANES]
+
+
 def sections(u_ref, start, parts, write, is_near, parity, comps, cols):
     source, inverse, coupling, movable = parts
     lanes = lax.broadcasted_iota(jnp.int32, (ROWS, cols), 1)
     sublanes = lax.broadcasted_iota(jnp.int32, (ROWS, cols), 0)
 
     def rows_at(c, offset):
-        return u_ref[c, start + offset : start + offset + ROWS, :]
+        return load(u_ref, c, start + offset, ROWS)
 
     def shifted(value, offset):
         return pltpu.roll(value, (-offset) % cols, 1)
@@ -337,13 +353,11 @@
     low_ref, high_ref, u_ref, v_ref = work["low"], work["high"], work["u"], work["v"]
     is_near = lax.axis_index("group") == 0
     for c in range(comps):
-        u_ref[c, PAD : PAD + rows, :] = state_ref[c]
-        u_ref[c, PAD - LOW : PAD, :] = (
-            below_ref[c * LOW : (c + 1) * LOW, :] + placed_below_ref[c, ROWS - LOW :, :]
-        )
-        u_ref[c, PAD + rows : PAD + rows + HIGH, :] = (
-            above_ref[c * HIGH : (c + 1) * HIGH, :] + placed_above_ref[c, :HIGH, :]
-        )
+        store(u_ref, c, PAD, state_ref[c])
+        below = below_ref[c * LOW : (c + 1) * LOW, :] + placed_below_ref[c, ROWS - LOW :, :]
+        store(u_ref, c, PAD - LOW, below)
+        above = above_ref[c * HIGH : (c + 1) * HIGH, :] + placed_above_ref[c, :HIGH, :]
+        store(u_ref, c, PAD + rows, above)
 
     def own(r):
         at = slice(r, r + ROWS)
@@ -365,18 +379,21 @@
             lambda: ref[last],
         )
 
-    def into(ref, start):
+    def into(start):
+        return lambda v, value: store(v_ref, v, start, value)
+
+    def out_of(start):
         def write(v, value):
-            ref[v, start : start + ROWS, :] = value
+            out_ref[v, start : start + ROWS, :] = value
 
         return write
 
     for r in range(0, rows, ROWS):
-        sections(u_ref, PAD + r, own(r), into(v_ref, PAD + r), is_near, 0, comps, cols)
-    sections(u_ref, PAD - ROWS, packed(low_ref), into(v_ref, PAD - ROWS), is_near, 0, comps, cols)
-    sections(u_ref, PAD + rows, packed(high_ref), into(v_ref, PAD + rows), is_near, 0, comps, cols)
+        sections(u_ref, PAD + r, own(r), into(PAD + r), is_near, 0, comps, cols)
+    sections(u_ref, PAD - ROWS, packed(low_ref), into(PAD - ROWS), is_near, 0, comps, cols)
+    sections(u_ref, PAD + rows, packed(high_ref), into(PAD + rows), is_near, 0, comps, cols)
     for r in range(0, rows, ROWS):
-        sections(v_ref, PAD + r, own(r), into(out_ref, r), is_near, 1, comps, cols)
+        sections(v_ref, PAD + r, own(r), out_of(r), is_near, 1, comps, cols)
 
 
 def place_kernel(count, refs):
@@ -468,7 +485,7 @@
     )
 
     placing = [vmem_like(comps * rows, cols), vmem_like(comps * (cols // LANES) * (ROWS // 2), 2 * LANES)]
-    working = [vmem_like(comps, rows + 2 * PAD, cols)] * 2
+    working = [vmem_like(comps, cols // LANES, rows + 2 * PAD, LANES)] * 2
     held = {"source": source, "inverse": inverse, "coupling": coupling, "base": base, "weight": weight}
     border = (f32(comps * LOW, cols), f32(comps * HIGH, cols))
     halo = f32(comps, ROWS, cols)

time: 111 us -> 109 us (0.982)
  Pallas kernels: 33 us -> 31.1 us
    pallas_call x11, Pallas kernels: 33 us -> 31.1 us  [call(): pl.pallas_call(kernel, out_shape=outs, in_specs=vmem(len(operands)) + [pl...]
where the time goes in v4:
time: 109 us; the launch traced here: 108 us
  starting transfers between devices  43 us (39%)
  waiting for transfers between devices  32.2 us (30%)
  Pallas kernels  31.1 us (29%)
  local copies, waits for them, and re-layouts  1.62 us (1%)
    pallas_call x11, Pallas kernels, call(): pl.pallas_call(kernel, out_shape=outs, in_specs=vmem(len(operands)) + [pl...  31.1 us
    all_to_all x4, starting transfers between devices, on_device(): lax.all_to_all(arrived, 'blk', split_axis=0, concat_axis=0, tiled=True)  21.4 us
    all_to_all x4, waiting for transfers between devices, on_device(): lax.all_to_all(arrived, 'blk', split_axis=0, concat_axis=0, tiled=True)  15.4 us
    ppermute x4, starting transfers between devices, on_device(): below = lax.ppermute(top, 'blk', up)  15.3 us
    ppermute x4, waiting for transfers between devices, on_device(): above = lax.ppermute(bottom, 'blk', down)  10.7 us
    ppermute x4, waiting for transfers between devices, on_device(): arrived = lax.ppermute(sums, ('group', 'blk'), swap)  6.12 us
    ppermute x4, starting transfers between devices, on_device(): above = lax.ppermute(bottom, 'blk', down)  5.35 us
  transfers between devices with their start and end apart: 16, of which 8 were waited for; matrix products, arithmetic and copies ran while one was open for 0% of the time, Pallas kernels for 12%

profile of v4, /device:TPU:0, one launch (start us, length us, event | category | flops | bytes accessed | tf_op | source)
XLA Modules:
  0.0 108.1 jit_solution(8848540716187981133)
XLA Ops:
  0.0 3.1 %shard_map.73 = (f32[16,16,256]{2,1,0:T(8,128)S(1)}, f32[140,512]{1,0:T(8,128)S(1)}, f32[96,512]{1,0:T(8,128)S(1)}) custom-call(f32[5,32,512]{2,1,0:T(8,128)} %bitcast.8, s32[16,256]{1,0:T(8,128)} %bitcast.36, f32[4,16,256]{2,1,0:T(8,128)} %bitcast.31, s32[16,256]{1,0:T(8,128)} %bitcast.10, f32[5,32,512]{2,1,0:T(8,128)} %bitcast.21, ...), custom_call_target="tpu_custom_call" | custom-call | tf_op jit(solution)/shard_map/pallas_call | solution.py:449
  3.1 0.6 collective-permute-start
  3.6 1.3 %collective-permute-done = f32[16,16,256]{2,1,0:T(8,128)} collective-permute-done((f32[16,16,256]{2,1,0:T(8,128)S(1)}, f32[16,16,256]{2,1,0:T(8,128)}, u32[]{:S(2)}, u32[]{:S(2)}) %collective-permute-start) | collective-permute-done | bytes 262176 | tf_op jit(solution)/shard_map/ppermute | solution.py:493
  4.9 8.2 %all-to-all-start = ((f32[16,16,256]{2,1,0:T(8,128)}), f32[16,16,256]{2,1,0:T(8,128)S(1)}, u32[]{:S(2)}, u32[]{:S(2)}) async-start(f32[16,16,256]{2,1,0:T(8,128)} %collective-permute-done), calls=%async_computation | async-start | bytes 524288 | tf_op jit(solution)/shard_map/all_to_all | solution.py:494
  13.2 3.8 %collective-permute-start.1 = (f32[140,512]{1,0:T(8,128)S(1)}, f32[140,512]{1,0:T(8,128)S(1)}, u32[]{:S(2)}, u32[]{:S(2)}) collective-permute-start(f32[140,512]{1,0:T(8,128)S(1)} %get-tuple-element.67), channel_id=1, source_target_pairs={{0,1},{1,2},{2,3},{3,4},{4,5},{5,6},{6,7},{7,8},{8,9},{9,10},{10,1... | collective-permute-start | bytes 860168 | tf_op jit(solution)/shard_map/ppermute | solution.py:495
  17.0 1.3 %collective-permute-start.2 = (f32[96,512]{1,0:T(8,128)S(1)}, f32[96,512]{1,0:T(8,128)S(1)}, u32[]{:S(2)}, u32[]{:S(2)}) collective-permute-start(f32[96,512]{1,0:T(8,128)S(1)} %get-tuple-element.68), channel_id=1, source_target_pairs={{1,0},{2,1},{3,2},{4,3},{5,4},{6,5},{7,6},{8,7},{9,8},{10,9},{11,1... | collective-permute-start | bytes 589832 | tf_op jit(solution)/shard_map/ppermute | solution.py:496
  18.3 0.0 copy-done.3
  18.3 1.7 %shard_map.74.refs_3_.refs_5_ = f32[32,512]{1,0:T(8,128)S(1)} custom-call(s32[16,256]{1,0:T(8,128)S(1)} %bitcast.11), custom_call_target="tpu_custom_call" | custom-call | tf_op jit(solution)/shard_map/pallas_call | solution.py:449
  20.0 10.7 %collective-permute-done.2.bottom_ref = f32[96,512]{1,0:T(8,128)S(1)} collective-permute-done((f32[96,512]{1,0:T(8,128)S(1)}, f32[96,512]{1,0:T(8,128)S(1)}, u32[]{:S(2)}, u32[]{:S(2)}) %collective-permute-start.2) | collective-permute-done | bytes 196640 | tf_op jit(solution)/shard_map/ppermute | solution.py:496
  30.7 0.0 collective-permute-done.1.top_ref
  30.7 2.4 %shard_map.75 = (f32[35,8,512]{2,1,0:T(8,128)S(1)}, f32[35,8,512]{2,1,0:T(8,128)S(1)}, s32[16,256]{1,0:T(8,128)S(1)}, s32[16,256]{1,0:T(8,128)S(1)}, f32[30,512]{1,0:T(8,128)S(1)}, /*index=5*/f32[20,512]{1,0:T(8,128)S(1)}) custom-call(f32[140,512]{1,0:T(8,128)S(1)} %collective-permute-done.1.top_ref, f32[96,512]{1,0:T(8,128)S(1)} %collective-permute-done.2.bottom_ref), custom_call_target="tpu_custom_call" | custom-call | tf_op jit(solution)/shard_map/pallas_call | solution.py:449
  33.1 0.0 copy-start
  33.1 0.8 copy-done
  33.9 0.8 copy-done.1
  34.7 0.0 all-to-all-done.refs_0_
  34.7 0.0 copy-done.2
  34.7 3.0 %shard_map.76 = (f32[5,32,512]{2,1,0:T(8,128)S(1)}, f32[5,8,512]{2,1,0:T(8,128)S(1)}, f32[5,8,512]{2,1,0:T(8,128)S(1)}, f32[5,32,512]{2,1,0:T(8,128)S(1)}, f32[5...) custom-call(f32[16,16,256]{2,1,0:T(8,128)S(1)} %all-to-all-done.refs, ...), custom_call_target="tpu_custom_call" | custom-call | tf_op jit(solution)/shard_map/pallas_call | solution.py:449
  37.8 3.2 %shard_map.77 = (f32[5,32,512]{2,1,0:T(8,128)S(1)}, f32[16,16,256]{2,1,0:T(8,128)S(1)}, f32[30,512]{1,0:T(8,128)S(1)}, f32[20,512]{1,0:T(8,128)S(1)}) custom-call(f32[5,32,512]{2,1,0:T(8,128)S(1)} %get-tuple-element.73.refs_0_, f32[30,512]{1,0:T(8,128)S(1)} %get-tuple-element.74.refs_1_, f32[20,512]{1,0:T(8,128)S(1)} %get-tuple-element.75.refs_2_, ...), custom_call_target="tpu_custom_call" | custom-call | tf_op jit(solution)/shard_map/pallas_call | solution.py:449
  40.9 0.2 collective-permute-start.3
  41.1 1.5 %collective-permute-done.3 = f32[16,16,256]{2,1,0:T(8,128)} collective-permute-done((f32[16,16,256]{2,1,0:T(8,128)S(1)}, f32[16,16,256]{2,1,0:T(8,128)}, u32[]{:S(2)}, u32[]{:S(2)}) %collective-permute-start.3) | collective-permute-done | bytes 262176 | tf_op jit(solution)/shard_map/ppermute | solution.py:493
  42.7 5.8 %all-to-all-start.1 = ((f32[16,16,256]{2,1,0:T(8,128)}), f32[16,16,256]{2,1,0:T(8,128)S(1)}, u32[]{:S(2)}, u32[]{:S(2)}) async-start(f32[16,16,256]{2,1,0:T(8,128)} %collective-permute-done.3), calls=%async_computation.1 | async-start | bytes 524288 | tf_op jit(solution)/shard_map/all_to_all | solution.py:494
  48.5 3.8 %collective-permute-start.4 = (f32[30,512]{1,0:T(8,128)S(1)}, f32[30,512]{1,0:T(8,128)S(1)}, u32[]{:S(2)}, u32[]{:S(2)}) collective-permute-start(f32[30,512]{1,0:T(8,128)S(1)} %get-tuple-element.88), channel_id=1, source_target_pairs={{0,1},{1,2},{2,3},{3,4},{4,5},{5,6},{6,7},{7,8},{8,9},{9,10},{10,1... | collective-permute-start | bytes 184328 | tf_op jit(solution)/shard_map/ppermute | solution.py:495
  52.3 1.5 %collective-permute-start.5 = (f32[20,512]{1,0:T(8,128)S(1)}, f32[20,512]{1,0:T(8,128)S(1)}, u32[]{:S(2)}, u32[]{:S(2)}) collective-permute-start(f32[20,512]{1,0:T(8,128)S(1)} %get-tuple-element.89), channel_id=1, source_target_pairs={{1,0},{2,1},{3,2},{4,3},{5,4},{6,5},{7,6},{8,7},{9,8},{10,9},{11,1... | collective-permute-start | bytes 122888 | tf_op jit(solution)/shard_map/ppermute | solution.py:496
  53.8 5.2 %all-to-all-done.1.refs_0_ = f32[16,16,256]{2,1,0:T(8,128)S(1)} async-done(((f32[16,16,256]{2,1,0:T(8,128)}), f32[16,16,256]{2,1,0:T(8,128)S(1)}, u32[]{:S(2)}, u32[]{:S(2)}) %all-to-all-start.1) | async-done | bytes 262176 | tf_op jit(solution)/shard_map/all_to_all | solution.py:494
  59.0 3.0 %shard_map.78 = (f32[5,32,512]{2,1,0:T(8,128)S(1)}, f32[5,8,512]{2,1,0:T(8,128)S(1)}, f32[5,8,512]{2,1,0:T(8,128)S(1)}, f32[5,32,512]{2,1,0:T(8,128)S(1)}, f32[5...) custom-call(f32[16,16,256]{2,1,0:T(8,128)S(1)} %all-to-all-done.1.re, ...), custom_call_target="tpu_custom_call" | custom-call | tf_op jit(solution)/shard_map/pallas_call | solution.py:449
  62.0 0.0 collective-permute-done.5.refs_2_
  62.0 0.0 collective-permute-done.4.refs_1_
  62.0 3.2 %shard_map.79 = (f32[5,32,512]{2,1,0:T(8,128)S(1)}, f32[16,16,256]{2,1,0:T(8,128)S(1)}, f32[30,512]{1,0:T(8,128)S(1)}, f32[20,512]{1,0:T(8,128)S(1)}) custom-call(f32[5,32,512]{2,1,0:T(8,128)S(1)} %get-tuple-element.87.refs_0_, f32[30,512]{1,0:T(8,128)S(1)} %collective-permute-done.4.refs_1_, f32[20,512]{1,0:T(8,128)S(1)} %collective-permute-done.5.refs_2_, ...), custom_call_target="tpu_custom_call" | custom-call | tf_op jit(solution)/shard_map/pallas_call | solution.py:449
  65.2 0.1 collective-permute-start.6
  65.3 1.7 %collective-permute-done.6 = f32[16,16,256]{2,1,0:T(8,128)} collective-permute-done((f32[16,16,256]{2,1,0:T(8,128)S(1)}, f32[16,16,256]{2,1,0:T(8,128)}, u32[]{:S(2)}, u32[]{:S(2)}) %collective-permute-start.6) | collective-permute-done | bytes 262176 | tf_op jit(solution)/shard_map/ppermute | solution.py:493
  66.9 3.6 %all-to-all-start.2 = ((f32[16,16,256]{2,1,0:T(8,128)}), f32[16,16,256]{2,1,0:T(8,128)S(1)}, u32[]{:S(2)}, u32[]{:S(2)}) async-start(f32[16,16,256]{2,1,0:T(8,128)} %collective-permute-done.6), calls=%async_computation.2 | async-start | bytes 524288 | tf_op jit(solution)/shard_map/all_to_all | solution.py:494
  70.6 3.8 %collective-permute-start.7 = (f32[30,512]{1,0:T(8,128)S(1)}, f32[30,512]{1,0:T(8,128)S(1)}, u32[]{:S(2)}, u32[]{:S(2)}) collective-permute-start(f32[30,512]{1,0:T(8,128)S(1)} %get-tuple-element.102), channel_id=1, source_target_pairs={{0,1},{1,2},{2,3},{3,4},{4,5},{5,6},{6,7},{7,8},{8,9},{9,10},{10,1... | collective-permute-start | bytes 184328 | tf_op jit(solution)/shard_map/ppermute | solution.py:495
  74.4 1.3 %collective-permute-start.8 = (f32[20,512]{1,0:T(8,128)S(1)}, f32[20,512]{1,0:T(8,128)S(1)}, u32[]{:S(2)}, u32[]{:S(2)}) collective-permute-start(f32[20,512]{1,0:T(8,128)S(1)} %get-tuple-element.103), channel_id=1, source_target_pairs={{1,0},{2,1},{3,2},{4,3},{5,4},{6,5},{7,6},{8,7},{9,8},{10,9},{11,1... | collective-permute-start | bytes 122888 | tf_op jit(solution)/shard_map/ppermute | solution.py:496
  75.7 5.2 %all-to-all-done.2.refs_0_ = f32[16,16,256]{2,1,0:T(8,128)S(1)} async-done(((f32[16,16,256]{2,1,0:T(8,128)}), f32[16,16,256]{2,1,0:T(8,128)S(1)}, u32[]{:S(2)}, u32[]{:S(2)}) %all-to-all-start.2) | async-done | bytes 262176 | tf_op jit(solution)/shard_map/all_to_all | solution.py:494
  80.9 3.0 %shard_map.80 = (f32[5,32,512]{2,1,0:T(8,128)S(1)}, f32[5,8,512]{2,1,0:T(8,128)S(1)}, f32[5,8,512]{2,1,0:T(8,128)S(1)}, f32[5,32,512]{2,1,0:T(8,128)S(1)}, f32[5...) custom-call(f32[16,16,256]{2,1,0:T(8,128)S(1)} %all-to-all-done.2.re, ...), custom_call_target="tpu_custom_call" | custom-call | tf_op jit(solution)/shard_map/pallas_call | solution.py:449
  83.9 0.0 collective-permute-done.8.refs_2_
  83.9 0.0 collective-permute-done.7.refs_1_
  83.9 3.4 %shard_map.81 = (f32[5,32,512]{2,1,0:T(8,128)S(1)}, f32[16,16,256]{2,1,0:T(8,128)S(1)}, f32[30,512]{1,0:T(8,128)S(1)}, f32[20,512]{1,0:T(8,128)S(1)}) custom-call(f32[5,32,512]{2,1,0:T(8,128)S(1)} %get-tuple-element.101.refs_0_, f32[30,512]{1,0:T(8,128)S(1)} %collective-permute-done.7.refs_1_, f32[20,512]{1,0:T(8,128)S(1)} %collective-permute-done.8.refs_2_, ...), custom_call_target="tpu_custom_call" | custom-call | tf_op jit(solution)/shard_map/pallas_call | solution.py:449
  87.3 0.1 collective-permute-start.9
  87.4 1.7 %collective-permute-done.9 = f32[16,16,256]{2,1,0:T(8,128)} collective-permute-done((f32[16,16,256]{2,1,0:T(8,128)S(1)}, f32[16,16,256]{2,1,0:T(8,128)}, u32[]{:S(2)}, u32[]{:S(2)}) %collective-permute-start.9) | collective-permute-done | bytes 262176 | tf_op jit(solution)/shard_map/ppermute | solution.py:493
  89.1 3.8 %all-to-all-start.3 = ((f32[16,16,256]{2,1,0:T(8,128)}), f32[16,16,256]{2,1,0:T(8,128)S(1)}, u32[]{:S(2)}, u32[]{:S(2)}) async-start(f32[16,16,256]{2,1,0:T(8,128)} %collective-permute-done.9), calls=%async_computation.3 | async-start | bytes 524288 | tf_op jit(solution)/shard_map/all_to_all | solution.py:494
  92.9 3.8 %collective-permute-start.10 = (f32[30,512]{1,0:T(8,128)S(1)}, f32[30,512]{1,0:T(8,128)S(1)}, u32[]{:S(2)}, u32[]{:S(2)}) collective-permute-start(f32[30,512]{1,0:T(8,128)S(1)} %get-tuple-element.116), channel_id=1, source_target_pairs={{0,1},{1,2},{2,3},{3,4},{4,5},{5,6},{6,7},{7,8},{8,9},{9,10},{10,1... | collective-permute-start | bytes 184328 | tf_op jit(solution)/shard_map/ppermute | solution.py:495
  96.7 1.3 %collective-permute-start.11 = (f32[20,512]{1,0:T(8,128)S(1)}, f32[20,512]{1,0:T(8,128)S(1)}, u32[]{:S(2)}, u32[]{:S(2)}) collective-permute-start(f32[20,512]{1,0:T(8,128)S(1)} %get-tuple-element.117), channel_id=1, source_target_pairs={{1,0},{2,1},{3,2},{4,3},{5,4},{6,5},{7,6},{8,7},{9,8},{10,9},{11,1... | collective-permute-start | bytes 122888 | tf_op jit(solution)/shard_map/ppermute | solution.py:496
  98.0 5.0 %all-to-all-done.3.refs_0_ = f32[16,16,256]{2,1,0:T(8,128)S(1)} async-done(((f32[16,16,256]{2,1,0:T(8,128)}), f32[16,16,256]{2,1,0:T(8,128)S(1)}, u32[]{:S(2)}, u32[]{:S(2)}) %all-to-all-start.3) | async-done | bytes 262176 | tf_op jit(solution)/shard_map/all_to_all | solution.py:494
  103.0 3.0 %shard_map.82 = (f32[5,32,512]{2,1,0:T(8,128)S(1)}, f32[5,8,512]{2,1,0:T(8,128)S(1)}, f32[5,8,512]{2,1,0:T(8,128)S(1)}, f32[5,32,512]{2,1,0:T(8,128)S(1)}, f32[5...) custom-call(f32[16,16,256]{2,1,0:T(8,128)S(1)} %all-to-all-done.3.re, ...), custom_call_target="tpu_custom_call" | custom-call | tf_op jit(solution)/shard_map/pallas_call | solution.py:449
  106.1 0.0 collective-permute-done.11.refs_2_
  106.1 0.0 collective-permute-done.10.refs_1_
  106.1 2.0 %shard_map.83 = f32[5,32,512]{2,1,0:T(8,128)} custom-call(f32[5,32,512]{2,1,0:T(8,128)S(1)} %get-tuple-element.115.refs_0_, f32[30,512]{1,0:T(8,128)S(1)} %collective-permute-done.10.refs_1_, f32[20,512]{1,0:T(8,128)S(1)} %collective-permute-done.11.refs_2_, f32[5,8,512]{2,1,0:T(8,128)S(1)} %get-tuple-element.118.refs_3_, ...), custom_call_target="tpu_custom_call" | custom-call | tf_op jit(solution)/shard_map/pallas_call | solution.py:449
  (3 shorter events, 0.0 us)
Async XLA Ops:
  0.0 18.3 %copy-start.3 = (s32[1,1,16,256]{3,2,1,0:T(8,128)S(1)}, s32[1,1,16,256]{3,2,1,0:T(8,128)}, u32[]{:S(2)}) copy-start(s32[1,1,16,256]{3,2,1,0:T(8,128)} %param.13) | copy-start | bytes 49156
  0.0 34.7 %copy-start.2 = (f32[1,1,5,32,512]{4,3,2,1,0:T(8,128)S(1)}, f32[1,1,5,32,512]{4,3,2,1,0:T(8,128)}, u32[]{:S(2)}) copy-start(f32[1,1,5,32,512]{4,3,2,1,0:T(8,128)} %param.7) | copy-start | bytes 983044
  3.1 1.9 %collective-permute-start = (f32[16,16,256]{2,1,0:T(8,128)S(1)}, f32[16,16,256]{2,1,0:T(8,128)}, u32[]{:S(2)}, u32[]{:S(2)}) collective-permute-start(f32[16,16,256]{2,1,0:T(8,128)S(1)} %get-tuple-element.66), channel_id=1, source_target_pairs={{0,16},{1,17},{2,18},{3,19},{4,20},{5,21},{6,22},{7,23},{8,24},{9,... | collective-permute-start | bytes 786440 | tf_op jit(solution)/shard_map/ppermute | solution.py:493
  4.9 29.8 %all-to-all-start = ((f32[16,16,256]{2,1,0:T(8,128)}), f32[16,16,256]{2,1,0:T(8,128)S(1)}, u32[]{:S(2)}, u32[]{:S(2)}) async-start(f32[16,16,256]{2,1,0:T(8,128)} %collective-permute-done), calls=%async_computation | async-start | bytes 524288 | tf_op jit(solution)/shard_map/all_to_all | solution.py:494
  13.2 17.5 %collective-permute-start.1 = (f32[140,512]{1,0:T(8,128)S(1)}, f32[140,512]{1,0:T(8,128)S(1)}, u32[]{:S(2)}, u32[]{:S(2)}) collective-permute-start(f32[140,512]{1,0:T(8,128)S(1)} %get-tuple-element.67), channel_id=1, source_target_pairs={{0,1},{1,2},{2,3},{3,4},{4,5},{5,6},{6,7},{7,8},{8,9},{9,10},{10,1... | collective-permute-start | bytes 860168 | tf_op jit(solution)/shard_map/ppermute | solution.py:495
  17.0 13.7 %collective-permute-start.2 = (f32[96,512]{1,0:T(8,128)S(1)}, f32[96,512]{1,0:T(8,128)S(1)}, u32[]{:S(2)}, u32[]{:S(2)}) collective-permute-start(f32[96,512]{1,0:T(8,128)S(1)} %get-tuple-element.68), channel_id=1, source_target_pairs={{1,0},{2,1},{3,2},{4,3},{5,4},{6,5},{7,6},{8,7},{9,8},{10,9},{11,1... | collective-permute-start | bytes 589832 | tf_op jit(solution)/shard_map/ppermute | solution.py:496
  33.1 0.8 copy-start
  33.9 0.8 copy-start.1
  40.9 1.7 %collective-permute-start.3 = (f32[16,16,256]{2,1,0:T(8,128)S(1)}, f32[16,16,256]{2,1,0:T(8,128)}, u32[]{:S(2)}, u32[]{:S(2)}) collective-permute-start(f32[16,16,256]{2,1,0:T(8,128)S(1)} %get-tuple-element.85), channel_id=1, source_target_pairs={{0,16},{1,17},{2,18},{3,19},{4,20},{5,21},{6,22},{7,23},{8,24},{9,... | collective-permute-start | bytes 786440 | tf_op jit(solution)/shard_map/ppermute | solution.py:493
  42.7 16.3 %all-to-all-start.1 = ((f32[16,16,256]{2,1,0:T(8,128)}), f32[16,16,256]{2,1,0:T(8,128)S(1)}, u32[]{:S(2)}, u32[]{:S(2)}) async-start(f32[16,16,256]{2,1,0:T(8,128)} %collective-permute-done.3), calls=%async_computation.1 | async-start | bytes 524288 | tf_op jit(solution)/shard_map/all_to_all | solution.py:494
  48.5 13.6 %collective-permute-start.4 = (f32[30,512]{1,0:T(8,128)S(1)}, f32[30,512]{1,0:T(8,128)S(1)}, u32[]{:S(2)}, u32[]{:S(2)}) collective-permute-start(f32[30,512]{1,0:T(8,128)S(1)} %get-tuple-element.88), channel_id=1, source_target_pairs={{0,1},{1,2},{2,3},{3,4},{4,5},{5,6},{6,7},{7,8},{8,9},{9,10},{10,1... | collective-permute-start | bytes 184328 | tf_op jit(solution)/shard_map/ppermute | solution.py:495
  52.3 9.7 %collective-permute-start.5 = (f32[20,512]{1,0:T(8,128)S(1)}, f32[20,512]{1,0:T(8,128)S(1)}, u32[]{:S(2)}, u32[]{:S(2)}) collective-permute-start(f32[20,512]{1,0:T(8,128)S(1)} %get-tuple-element.89), channel_id=1, source_target_pairs={{1,0},{2,1},{3,2},{4,3},{5,4},{6,5},{7,6},{8,7},{9,8},{10,9},{11,1... | collective-permute-start | bytes 122888 | tf_op jit(solution)/shard_map/ppermute | solution.py:496
  65.2 1.7 %collective-permute-start.6 = (f32[16,16,256]{2,1,0:T(8,128)S(1)}, f32[16,16,256]{2,1,0:T(8,128)}, u32[]{:S(2)}, u32[]{:S(2)}) collective-permute-start(f32[16,16,256]{2,1,0:T(8,128)S(1)} %get-tuple-element.99), channel_id=1, source_target_pairs={{0,16},{1,17},{2,18},{3,19},{4,20},{5,21},{6,22},{7,23},{8,24},{9,... | collective-permute-start | bytes 786440 | tf_op jit(solution)/shard_map/ppermute | solution.py:493
  66.9 13.9 %all-to-all-start.2 = ((f32[16,16,256]{2,1,0:T(8,128)}), f32[16,16,256]{2,1,0:T(8,128)S(1)}, u32[]{:S(2)}, u32[]{:S(2)}) async-start(f32[16,16,256]{2,1,0:T(8,128)} %collective-permute-done.6), calls=%async_computation.2 | async-start | bytes 524288 | tf_op jit(solution)/shard_map/all_to_all | solution.py:494
  70.6 13.4 %collective-permute-start.7 = (f32[30,512]{1,0:T(8,128)S(1)}, f32[30,512]{1,0:T(8,128)S(1)}, u32[]{:S(2)}, u32[]{:S(2)}) collective-permute-start(f32[30,512]{1,0:T(8,128)S(1)} %get-tuple-element.102), channel_id=1, source_target_pairs={{0,1},{1,2},{2,3},{3,4},{4,5},{5,6},{6,7},{7,8},{8,9},{9,10},{10,1... | collective-permute-start | bytes 184328 | tf_op jit(solution)/shard_map/ppermute | solution.py:495
  74.4 9.5 %collective-permute-start.8 = (f32[20,512]{1,0:T(8,128)S(1)}, f32[20,512]{1,0:T(8,128)S(1)}, u32[]{:S(2)}, u32[]{:S(2)}) collective-permute-start(f32[20,512]{1,0:T(8,128)S(1)} %get-tuple-element.103), channel_id=1, source_target_pairs={{1,0},{2,1},{3,2},{4,3},{5,4},{6,5},{7,6},{8,7},{9,8},{10,9},{11,1... | collective-permute-start | bytes 122888 | tf_op jit(solution)/shard_map/ppermute | solution.py:496
  87.3 1.7 %collective-permute-start.9 = (f32[16,16,256]{2,1,0:T(8,128)S(1)}, f32[16,16,256]{2,1,0:T(8,128)}, u32[]{:S(2)}, u32[]{:S(2)}) collective-permute-start(f32[16,16,256]{2,1,0:T(8,128)S(1)} %get-tuple-element.113), channel_id=1, source_target_pairs={{0,16},{1,17},{2,18},{3,19},{4,20},{5,21},{6,22},{7,23},{8,24},{9,... | collective-permute-start | bytes 786440 | tf_op jit(solution)/shard_map/ppermute | solution.py:493
  89.1 14.0 %all-to-all-start.3 = ((f32[16,16,256]{2,1,0:T(8,128)}), f32[16,16,256]{2,1,0:T(8,128)S(1)}, u32[]{:S(2)}, u32[]{:S(2)}) async-start(f32[16,16,256]{2,1,0:T(8,128)} %collective-permute-done.9), calls=%async_computation.3 | async-start | bytes 524288 | tf_op jit(solution)/shard_map/all_to_all | solution.py:494
  92.9 13.2 %collective-permute-start.10 = (f32[30,512]{1,0:T(8,128)S(1)}, f32[30,512]{1,0:T(8,128)S(1)}, u32[]{:S(2)}, u32[]{:S(2)}) collective-permute-start(f32[30,512]{1,0:T(8,128)S(1)} %get-tuple-element.116), channel_id=1, source_target_pairs={{0,1},{1,2},{2,3},{3,4},{4,5},{5,6},{6,7},{7,8},{8,9},{9,10},{10,1... | collective-permute-start | bytes 184328 | tf_op jit(solution)/shard_map/ppermute | solution.py:495
  96.7 9.4 %collective-permute-start.11 = (f32[20,512]{1,0:T(8,128)S(1)}, f32[20,512]{1,0:T(8,128)S(1)}, u32[]{:S(2)}, u32[]{:S(2)}) collective-permute-start(f32[20,512]{1,0:T(8,128)S(1)} %get-tuple-element.117), channel_id=1, source_target_pairs={{1,0},{2,1},{3,2},{4,3},{5,4},{6,5},{7,6},{8,7},{9,8},{10,9},{11,1... | collective-permute-start | bytes 122888 | tf_op jit(solution)/shard_map/ppermute | solution.py:496

commit v5 on v4

--- a/solution.py
+++ b/solution.py
@@ -97,10 +97,22 @@
             jnp.where(row_iota == row + 1, jnp.where(is_odd, w2, w3), 0.0),
         )
         total = even_weight[None] * picked_even + odd_weight[None] * picked_odd
-        out_ref[d, 0:comps, :] = jnp.sum(total, axis=1)
-
+        values = jnp.sum(total, axis=1)
+        out_ref[d, 0:comps, :] = values
+        return values
+
+    none = jnp.zeros((comps, slots), F32)
+    if blocks <= UNROLL:
+        out_ref[0, comps : 2 * comps, :] = none
+        out_ref[blocks - 1, 2 * comps : 3 * comps, :] = none
+        for d in range(blocks):
+            values = one(d)
+            if d < blocks - 1:
+                out_ref[d + 1, comps : 2 * comps, :] = values
+            if d > 0:
+                out_ref[d - 1, 2 * comps : 3 * comps, :] = values
+        return
     repeat(blocks, one)
-    none = jnp.zeros((comps, slots), F32)
     for d in range(blocks):
         out_ref[d, comps : 2 * comps, :] = out_ref[d - 1, 0:comps, :] if d > 0 else none
         out_ref[d, 2 * comps : 3 * comps, :] = out_ref[d + 1, 0:comps, :] if d < blocks - 1 else none

time: 109 us -> 109 us (level)
  no operation moved by 1% of the time
where the time goes in v5:
time: 109 us; the launch traced here: 108 us
  starting transfers between devices  42.9 us (39%)
  waiting for transfers between devices  32.3 us (30%)
  Pallas kernels  31 us (28%)
  local copies, waits for them, and re-layouts  1.62 us (1%)
    pallas_call x11, Pallas kernels, call(): pl.pallas_call(kernel, out_shape=outs, in_specs=vmem(len(operands)) + [pl...  31 us
    all_to_all x4, starting transfers between devices, on_device(): lax.all_to_all(arrived, 'blk', split_axis=0, concat_axis=0, tiled=True)  21.4 us
    all_to_all x4, waiting for transfers between devices, on_device(): lax.all_to_all(arrived, 'blk', split_axis=0, concat_axis=0, tiled=True)  15.5 us
    ppermute x4, starting transfers between devices, on_device(): below = lax.ppermute(top, 'blk', up)  15.3 us
    ppermute x4, waiting for transfers between devices, on_device(): above = lax.ppermute(bottom, 'blk', down)  10.7 us
    ppermute x4, waiting for transfers between devices, on_device(): arrived = lax.ppermute(sums, ('group', 'blk'), swap)  6.12 us
    ppermute x4, starting transfers between devices, on_device(): above = lax.ppermute(bottom, 'blk', down)  5.35 us
  transfers between devices with their start and end apart: 16, of which 8 were waited for; matrix products, arithmetic and copies ran while one was open for 0% of the time, Pallas kernels for 12%

profile of v5, /device:TPU:0, one launch (start us, length us, event | category | flops | bytes accessed | tf_op | source)
XLA Modules:
  0.0 108.1 jit_solution(6031111896617321010)
XLA Ops:
  0.0 3.0 %shard_map.73 = (f32[16,16,256]{2,1,0:T(8,128)S(1)}, f32[140,512]{1,0:T(8,128)S(1)}, f32[96,512]{1,0:T(8,128)S(1)}) custom-call(f32[5,32,512]{2,1,0:T(8,128)} %bitcast.8, s32[16,256]{1,0:T(8,128)} %bitcast.36, f32[4,16,256]{2,1,0:T(8,128)} %bitcast.31, s32[16,256]{1,0:T(8,128)} %bitcast.10, f32[5,32,512]{2,1,0:T(8,128)} %bitcast.21, ...), custom_call_target="tpu_custom_call" | custom-call | tf_op jit(solution)/shard_map/pallas_call | solution.py:461
  3.1 0.6 collective-permute-start
  3.6 1.3 %collective-permute-done = f32[16,16,256]{2,1,0:T(8,128)} collective-permute-done((f32[16,16,256]{2,1,0:T(8,128)S(1)}, f32[16,16,256]{2,1,0:T(8,128)}, u32[]{:S(2)}, u32[]{:S(2)}) %collective-permute-start) | collective-permute-done | bytes 262176 | tf_op jit(solution)/shard_map/ppermute | solution.py:505
  4.9 8.2 %all-to-all-start = ((f32[16,16,256]{2,1,0:T(8,128)}), f32[16,16,256]{2,1,0:T(8,128)S(1)}, u32[]{:S(2)}, u32[]{:S(2)}) async-start(f32[16,16,256]{2,1,0:T(8,128)} %collective-permute-done), calls=%async_computation | async-start | bytes 524288 | tf_op jit(solution)/shard_map/all_to_all | solution.py:506
  13.1 3.8 %collective-permute-start.1 = (f32[140,512]{1,0:T(8,128)S(1)}, f32[140,512]{1,0:T(8,128)S(1)}, u32[]{:S(2)}, u32[]{:S(2)}) collective-permute-start(f32[140,512]{1,0:T(8,128)S(1)} %get-tuple-element.67), channel_id=1, source_target_pairs={{0,1},{1,2},{2,3},{3,4},{4,5},{5,6},{6,7},{7,8},{8,9},{9,10},{10,1... | collective-permute-start | bytes 860168 | tf_op jit(solution)/shard_map/ppermute | solution.py:507
  17.0 1.3 %collective-permute-start.2 = (f32[96,512]{1,0:T(8,128)S(1)}, f32[96,512]{1,0:T(8,128)S(1)}, u32[]{:S(2)}, u32[]{:S(2)}) collective-permute-start(f32[96,512]{1,0:T(8,128)S(1)} %get-tuple-element.68), channel_id=1, source_target_pairs={{1,0},{2,1},{3,2},{4,3},{5,4},{6,5},{7,6},{8,7},{9,8},{10,9},{11,1... | collective-permute-start | bytes 589832 | tf_op jit(solution)/shard_map/ppermute | solution.py:508
  18.3 0.0 copy-done.3
  18.3 1.7 %shard_map.74.refs_3_.refs_5_ = f32[32,512]{1,0:T(8,128)S(1)} custom-call(s32[16,256]{1,0:T(8,128)S(1)} %bitcast.11), custom_call_target="tpu_custom_call" | custom-call | tf_op jit(solution)/shard_map/pallas_call | solution.py:461
  20.0 10.7 %collective-permute-done.2.bottom_ref = f32[96,512]{1,0:T(8,128)S(1)} collective-permute-done((f32[96,512]{1,0:T(8,128)S(1)}, f32[96,512]{1,0:T(8,128)S(1)}, u32[]{:S(2)}, u32[]{:S(2)}) %collective-permute-start.2) | collective-permute-done | bytes 196640 | tf_op jit(solution)/shard_map/ppermute | solution.py:508
  30.7 0.0 collective-permute-done.1.top_ref
  30.7 2.4 %shard_map.75 = (f32[35,8,512]{2,1,0:T(8,128)S(1)}, f32[35,8,512]{2,1,0:T(8,128)S(1)}, s32[16,256]{1,0:T(8,128)S(1)}, s32[16,256]{1,0:T(8,128)S(1)}, f32[30,512]{1,0:T(8,128)S(1)}, /*index=5*/f32[20,512]{1,0:T(8,128)S(1)}) custom-call(f32[140,512]{1,0:T(8,128)S(1)} %collective-permute-done.1.top_ref, f32[96,512]{1,0:T(8,128)S(1)} %collective-permute-done.2.bottom_ref), custom_call_target="tpu_custom_call" | custom-call | tf_op jit(solution)/shard_map/pallas_call | solution.py:461
  33.1 0.0 copy-start
  33.1 0.8 copy-done
  33.9 0.8 copy-done.1
  34.7 0.0 all-to-all-done.refs_0_
  34.7 0.0 copy-done.2
  34.7 3.0 %shard_map.76 = (f32[5,32,512]{2,1,0:T(8,128)S(1)}, f32[5,8,512]{2,1,0:T(8,128)S(1)}, f32[5,8,512]{2,1,0:T(8,128)S(1)}, f32[5,32,512]{2,1,0:T(8,128)S(1)}, f32[5...) custom-call(f32[16,16,256]{2,1,0:T(8,128)S(1)} %all-to-all-done.refs, ...), custom_call_target="tpu_custom_call" | custom-call | tf_op jit(solution)/shard_map/pallas_call | solution.py:461
  37.7 3.2 %shard_map.77 = (f32[5,32,512]{2,1,0:T(8,128)S(1)}, f32[16,16,256]{2,1,0:T(8,128)S(1)}, f32[30,512]{1,0:T(8,128)S(1)}, f32[20,512]{1,0:T(8,128)S(1)}) custom-call(f32[5,32,512]{2,1,0:T(8,128)S(1)} %get-tuple-element.73.refs_0_, f32[30,512]{1,0:T(8,128)S(1)} %get-tuple-element.74.refs_1_, f32[20,512]{1,0:T(8,128)S(1)} %get-tuple-element.75.refs_2_, ...), custom_call_target="tpu_custom_call" | custom-call | tf_op jit(solution)/shard_map/pallas_call | solution.py:461
  40.9 0.2 collective-permute-start.3
  41.1 1.5 %collective-permute-done.3 = f32[16,16,256]{2,1,0:T(8,128)} collective-permute-done((f32[16,16,256]{2,1,0:T(8,128)S(1)}, f32[16,16,256]{2,1,0:T(8,128)}, u32[]{:S(2)}, u32[]{:S(2)}) %collective-permute-start.3) | collective-permute-done | bytes 262176 | tf_op jit(solution)/shard_map/ppermute | solution.py:505
  42.7 5.8 %all-to-all-start.1 = ((f32[16,16,256]{2,1,0:T(8,128)}), f32[16,16,256]{2,1,0:T(8,128)S(1)}, u32[]{:S(2)}, u32[]{:S(2)}) async-start(f32[16,16,256]{2,1,0:T(8,128)} %collective-permute-done.3), calls=%async_computation.1 | async-start | bytes 524288 | tf_op jit(solution)/shard_map/all_to_all | solution.py:506
  48.4 3.8 %collective-permute-start.4 = (f32[30,512]{1,0:T(8,128)S(1)}, f32[30,512]{1,0:T(8,128)S(1)}, u32[]{:S(2)}, u32[]{:S(2)}) collective-permute-start(f32[30,512]{1,0:T(8,128)S(1)} %get-tuple-element.88), channel_id=1, source_target_pairs={{0,1},{1,2},{2,3},{3,4},{4,5},{5,6},{6,7},{7,8},{8,9},{9,10},{10,1... | collective-permute-start | bytes 184328 | tf_op jit(solution)/shard_map/ppermute | solution.py:507
  52.3 1.5 %collective-permute-start.5 = (f32[20,512]{1,0:T(8,128)S(1)}, f32[20,512]{1,0:T(8,128)S(1)}, u32[]{:S(2)}, u32[]{:S(2)}) collective-permute-start(f32[20,512]{1,0:T(8,128)S(1)} %get-tuple-element.89), channel_id=1, source_target_pairs={{1,0},{2,1},{3,2},{4,3},{5,4},{6,5},{7,6},{8,7},{9,8},{10,9},{11,1... | collective-permute-start | bytes 122888 | tf_op jit(solution)/shard_map/ppermute | solution.py:508
  53.8 5.2 %all-to-all-done.1.refs_0_ = f32[16,16,256]{2,1,0:T(8,128)S(1)} async-done(((f32[16,16,256]{2,1,0:T(8,128)}), f32[16,16,256]{2,1,0:T(8,128)S(1)}, u32[]{:S(2)}, u32[]{:S(2)}) %all-to-all-start.1) | async-done | bytes 262176 | tf_op jit(solution)/shard_map/all_to_all | solution.py:506
  59.0 3.0 %shard_map.78 = (f32[5,32,512]{2,1,0:T(8,128)S(1)}, f32[5,8,512]{2,1,0:T(8,128)S(1)}, f32[5,8,512]{2,1,0:T(8,128)S(1)}, f32[5,32,512]{2,1,0:T(8,128)S(1)}, f32[5...) custom-call(f32[16,16,256]{2,1,0:T(8,128)S(1)} %all-to-all-done.1.re, ...), custom_call_target="tpu_custom_call" | custom-call | tf_op jit(solution)/shard_map/pallas_call | solution.py:461
  62.0 0.0 collective-permute-done.5.refs_2_
  62.0 0.0 collective-permute-done.4.refs_1_
  62.0 3.2 %shard_map.79 = (f32[5,32,512]{2,1,0:T(8,128)S(1)}, f32[16,16,256]{2,1,0:T(8,128)S(1)}, f32[30,512]{1,0:T(8,128)S(1)}, f32[20,512]{1,0:T(8,128)S(1)}) custom-call(f32[5,32,512]{2,1,0:T(8,128)S(1)} %get-tuple-element.87.refs_0_, f32[30,512]{1,0:T(8,128)S(1)} %collective-permute-done.4.refs_1_, f32[20,512]{1,0:T(8,128)S(1)} %collective-permute-done.5.refs_2_, ...), custom_call_target="tpu_custom_call" | custom-call | tf_op jit(solution)/shard_map/pallas_call | solution.py:461
  65.2 0.1 collective-permute-start.6
  65.3 1.7 %collective-permute-done.6 = f32[16,16,256]{2,1,0:T(8,128)} collective-permute-done((f32[16,16,256]{2,1,0:T(8,128)S(1)}, f32[16,16,256]{2,1,0:T(8,128)}, u32[]{:S(2)}, u32[]{:S(2)}) %collective-permute-start.6) | collective-permute-done | bytes 262176 | tf_op jit(solution)/shard_map/ppermute | solution.py:505
  66.9 3.6 %all-to-all-start.2 = ((f32[16,16,256]{2,1,0:T(8,128)}), f32[16,16,256]{2,1,0:T(8,128)S(1)}, u32[]{:S(2)}, u32[]{:S(2)}) async-start(f32[16,16,256]{2,1,0:T(8,128)} %collective-permute-done.6), calls=%async_computation.2 | async-start | bytes 524288 | tf_op jit(solution)/shard_map/all_to_all | solution.py:506
  70.5 3.8 %collective-permute-start.7 = (f32[30,512]{1,0:T(8,128)S(1)}, f32[30,512]{1,0:T(8,128)S(1)}, u32[]{:S(2)}, u32[]{:S(2)}) collective-permute-start(f32[30,512]{1,0:T(8,128)S(1)} %get-tuple-element.102), channel_id=1, source_target_pairs={{0,1},{1,2},{2,3},{3,4},{4,5},{5,6},{6,7},{7,8},{8,9},{9,10},{10,1... | collective-permute-start | bytes 184328 | tf_op jit(solution)/shard_map/ppermute | solution.py:507
  74.3 1.3 %collective-permute-start.8 = (f32[20,512]{1,0:T(8,128)S(1)}, f32[20,512]{1,0:T(8,128)S(1)}, u32[]{:S(2)}, u32[]{:S(2)}) collective-permute-start(f32[20,512]{1,0:T(8,128)S(1)} %get-tuple-element.103), channel_id=1, source_target_pairs={{1,0},{2,1},{3,2},{4,3},{5,4},{6,5},{7,6},{8,7},{9,8},{10,9},{11,1... | collective-permute-start | bytes 122888 | tf_op jit(solution)/shard_map/ppermute | solution.py:508
  75.6 5.2 %all-to-all-done.2.refs_0_ = f32[16,16,256]{2,1,0:T(8,128)S(1)} async-done(((f32[16,16,256]{2,1,0:T(8,128)}), f32[16,16,256]{2,1,0:T(8,128)S(1)}, u32[]{:S(2)}, u32[]{:S(2)}) %all-to-all-start.2) | async-done | bytes 262176 | tf_op jit(solution)/shard_map/all_to_all | solution.py:506
  80.9 3.0 %shard_map.80 = (f32[5,32,512]{2,1,0:T(8,128)S(1)}, f32[5,8,512]{2,1,0:T(8,128)S(1)}, f32[5,8,512]{2,1,0:T(8,128)S(1)}, f32[5,32,512]{2,1,0:T(8,128)S(1)}, f32[5...) custom-call(f32[16,16,256]{2,1,0:T(8,128)S(1)} %all-to-all-done.2.re, ...), custom_call_target="tpu_custom_call" | custom-call | tf_op jit(solution)/shard_map/pallas_call | solution.py:461
  83.9 0.0 collective-permute-done.8.refs_2_
  83.9 0.0 collective-permute-done.7.refs_1_
  83.9 3.4 %shard_map.81 = (f32[5,32,512]{2,1,0:T(8,128)S(1)}, f32[16,16,256]{2,1,0:T(8,128)S(1)}, f32[30,512]{1,0:T(8,128)S(1)}, f32[20,512]{1,0:T(8,128)S(1)}) custom-call(f32[5,32,512]{2,1,0:T(8,128)S(1)} %get-tuple-element.101.refs_0_, f32[30,512]{1,0:T(8,128)S(1)} %collective-permute-done.7.refs_1_, f32[20,512]{1,0:T(8,128)S(1)} %collective-permute-done.8.refs_2_, ...), custom_call_target="tpu_custom_call" | custom-call | tf_op jit(solution)/shard_map/pallas_call | solution.py:461
  87.3 0.1 collective-permute-start.9
  87.4 1.7 %collective-permute-done.9 = f32[16,16,256]{2,1,0:T(8,128)} collective-permute-done((f32[16,16,256]{2,1,0:T(8,128)S(1)}, f32[16,16,256]{2,1,0:T(8,128)}, u32[]{:S(2)}, u32[]{:S(2)}) %collective-permute-start.9) | collective-permute-done | bytes 262176 | tf_op jit(solution)/shard_map/ppermute | solution.py:505
  89.0 3.8 %all-to-all-start.3 = ((f32[16,16,256]{2,1,0:T(8,128)}), f32[16,16,256]{2,1,0:T(8,128)S(1)}, u32[]{:S(2)}, u32[]{:S(2)}) async-start(f32[16,16,256]{2,1,0:T(8,128)} %collective-permute-done.9), calls=%async_computation.3 | async-start | bytes 524288 | tf_op jit(solution)/shard_map/all_to_all | solution.py:506
  92.8 3.8 %collective-permute-start.10 = (f32[30,512]{1,0:T(8,128)S(1)}, f32[30,512]{1,0:T(8,128)S(1)}, u32[]{:S(2)}, u32[]{:S(2)}) collective-permute-start(f32[30,512]{1,0:T(8,128)S(1)} %get-tuple-element.116), channel_id=1, source_target_pairs={{0,1},{1,2},{2,3},{3,4},{4,5},{5,6},{6,7},{7,8},{8,9},{9,10},{10,1... | collective-permute-start | bytes 184328 | tf_op jit(solution)/shard_map/ppermute | solution.py:507
  96.7 1.3 %collective-permute-start.11 = (f32[20,512]{1,0:T(8,128)S(1)}, f32[20,512]{1,0:T(8,128)S(1)}, u32[]{:S(2)}, u32[]{:S(2)}) collective-permute-start(f32[20,512]{1,0:T(8,128)S(1)} %get-tuple-element.117), channel_id=1, source_target_pairs={{1,0},{2,1},{3,2},{4,3},{5,4},{6,5},{7,6},{8,7},{9,8},{10,9},{11,1... | collective-permute-start | bytes 122888 | tf_op jit(solution)/shard_map/ppermute | solution.py:508
  98.0 5.0 %all-to-all-done.3.refs_0_ = f32[16,16,256]{2,1,0:T(8,128)S(1)} async-done(((f32[16,16,256]{2,1,0:T(8,128)}), f32[16,16,256]{2,1,0:T(8,128)S(1)}, u32[]{:S(2)}, u32[]{:S(2)}) %all-to-all-start.3) | async-done | bytes 262176 | tf_op jit(solution)/shard_map/all_to_all | solution.py:506
  103.0 3.0 %shard_map.82 = (f32[5,32,512]{2,1,0:T(8,128)S(1)}, f32[5,8,512]{2,1,0:T(8,128)S(1)}, f32[5,8,512]{2,1,0:T(8,128)S(1)}, f32[5,32,512]{2,1,0:T(8,128)S(1)}, f32[5...) custom-call(f32[16,16,256]{2,1,0:T(8,128)S(1)} %all-to-all-done.3.re, ...), custom_call_target="tpu_custom_call" | custom-call | tf_op jit(solution)/shard_map/pallas_call | solution.py:461
  106.0 0.0 collective-permute-done.11.refs_2_
  106.0 0.0 collective-permute-done.10.refs_1_
  106.1 2.0 %shard_map.83 = f32[5,32,512]{2,1,0:T(8,128)} custom-call(f32[5,32,512]{2,1,0:T(8,128)S(1)} %get-tuple-element.115.refs_0_, f32[30,512]{1,0:T(8,128)S(1)} %collective-permute-done.10.refs_1_, f32[20,512]{1,0:T(8,128)S(1)} %collective-permute-done.11.refs_2_, f32[5,8,512]{2,1,0:T(8,128)S(1)} %get-tuple-element.118.refs_3_, ...), custom_call_target="tpu_custom_call" | custom-call | tf_op jit(solution)/shard_map/pallas_call | solution.py:461
  (3 shorter events, 0.0 us)
Async XLA Ops:
  0.0 18.3 %copy-start.3 = (s32[1,1,16,256]{3,2,1,0:T(8,128)S(1)}, s32[1,1,16,256]{3,2,1,0:T(8,128)}, u32[]{:S(2)}) copy-start(s32[1,1,16,256]{3,2,1,0:T(8,128)} %param.13) | copy-start | bytes 49156
  0.0 34.7 %copy-start.2 = (f32[1,1,5,32,512]{4,3,2,1,0:T(8,128)S(1)}, f32[1,1,5,32,512]{4,3,2,1,0:T(8,128)}, u32[]{:S(2)}) copy-start(f32[1,1,5,32,512]{4,3,2,1,0:T(8,128)} %param.7) | copy-start | bytes 983044
  3.1 1.9 %collective-permute-start = (f32[16,16,256]{2,1,0:T(8,128)S(1)}, f32[16,16,256]{2,1,0:T(8,128)}, u32[]{:S(2)}, u32[]{:S(2)}) collective-permute-start(f32[16,16,256]{2,1,0:T(8,128)S(1)} %get-tuple-element.66), channel_id=1, source_target_pairs={{0,16},{1,17},{2,18},{3,19},{4,20},{5,21},{6,22},{7,23},{8,24},{9,... | collective-permute-start | bytes 786440 | tf_op jit(solution)/shard_map/ppermute | solution.py:505
  4.9 29.8 %all-to-all-start = ((f32[16,16,256]{2,1,0:T(8,128)}), f32[16,16,256]{2,1,0:T(8,128)S(1)}, u32[]{:S(2)}, u32[]{:S(2)}) async-start(f32[16,16,256]{2,1,0:T(8,128)} %collective-permute-done), calls=%async_computation | async-start | bytes 524288 | tf_op jit(solution)/shard_map/all_to_all | solution.py:506
  13.1 17.5 %collective-permute-start.1 = (f32[140,512]{1,0:T(8,128)S(1)}, f32[140,512]{1,0:T(8,128)S(1)}, u32[]{:S(2)}, u32[]{:S(2)}) collective-permute-start(f32[140,512]{1,0:T(8,128)S(1)} %get-tuple-element.67), channel_id=1, source_target_pairs={{0,1},{1,2},{2,3},{3,4},{4,5},{5,6},{6,7},{7,8},{8,9},{9,10},{10,1... | collective-permute-start | bytes 860168 | tf_op jit(solution)/shard_map/ppermute | solution.py:507
  17.0 13.7 %collective-permute-start.2 = (f32[96,512]{1,0:T(8,128)S(1)}, f32[96,512]{1,0:T(8,128)S(1)}, u32[]{:S(2)}, u32[]{:S(2)}) collective-permute-start(f32[96,512]{1,0:T(8,128)S(1)} %get-tuple-element.68), channel_id=1, source_target_pairs={{1,0},{2,1},{3,2},{4,3},{5,4},{6,5},{7,6},{8,7},{9,8},{10,9},{11,1... | collective-permute-start | bytes 589832 | tf_op jit(solution)/shard_map/ppermute | solution.py:508
  33.1 0.8 copy-start
  33.9 0.8 copy-start.1
  40.9 1.7 %collective-permute-start.3 = (f32[16,16,256]{2,1,0:T(8,128)S(1)}, f32[16,16,256]{2,1,0:T(8,128)}, u32[]{:S(2)}, u32[]{:S(2)}) collective-permute-start(f32[16,16,256]{2,1,0:T(8,128)S(1)} %get-tuple-element.85), channel_id=1, source_target_pairs={{0,16},{1,17},{2,18},{3,19},{4,20},{5,21},{6,22},{7,23},{8,24},{9,... | collective-permute-start | bytes 786440 | tf_op jit(solution)/shard_map/ppermute | solution.py:505
  42.7 16.3 %all-to-all-start.1 = ((f32[16,16,256]{2,1,0:T(8,128)}), f32[16,16,256]{2,1,0:T(8,128)S(1)}, u32[]{:S(2)}, u32[]{:S(2)}) async-start(f32[16,16,256]{2,1,0:T(8,128)} %collective-permute-done.3), calls=%async_computation.1 | async-start | bytes 524288 | tf_op jit(solution)/shard_map/all_to_all | solution.py:506
  48.4 13.5 %collective-permute-start.4 = (f32[30,512]{1,0:T(8,128)S(1)}, f32[30,512]{1,0:T(8,128)S(1)}, u32[]{:S(2)}, u32[]{:S(2)}) collective-permute-start(f32[30,512]{1,0:T(8,128)S(1)} %get-tuple-element.88), channel_id=1, source_target_pairs={{0,1},{1,2},{2,3},{3,4},{4,5},{5,6},{6,7},{7,8},{8,9},{9,10},{10,1... | collective-permute-start | bytes 184328 | tf_op jit(solution)/shard_map/ppermute | solution.py:507
  52.3 9.7 %collective-permute-start.5 = (f32[20,512]{1,0:T(8,128)S(1)}, f32[20,512]{1,0:T(8,128)S(1)}, u32[]{:S(2)}, u32[]{:S(2)}) collective-permute-start(f32[20,512]{1,0:T(8,128)S(1)} %get-tuple-element.89), channel_id=1, source_target_pairs={{1,0},{2,1},{3,2},{4,3},{5,4},{6,5},{7,6},{8,7},{9,8},{10,9},{11,1... | collective-permute-start | bytes 122888 | tf_op jit(solution)/shard_map/ppermute | solution.py:508
  65.2 1.7 %collective-permute-start.6 = (f32[16,16,256]{2,1,0:T(8,128)S(1)}, f32[16,16,256]{2,1,0:T(8,128)}, u32[]{:S(2)}, u32[]{:S(2)}) collective-permute-start(f32[16,16,256]{2,1,0:T(8,128)S(1)} %get-tuple-element.99), channel_id=1, source_target_pairs={{0,16},{1,17},{2,18},{3,19},{4,20},{5,21},{6,22},{7,23},{8,24},{9,... | collective-permute-start | bytes 786440 | tf_op jit(solution)/shard_map/ppermute | solution.py:505
  66.9 13.9 %all-to-all-start.2 = ((f32[16,16,256]{2,1,0:T(8,128)}), f32[16,16,256]{2,1,0:T(8,128)S(1)}, u32[]{:S(2)}, u32[]{:S(2)}) async-start(f32[16,16,256]{2,1,0:T(8,128)} %collective-permute-done.6), calls=%async_computation.2 | async-start | bytes 524288 | tf_op jit(solution)/shard_map/all_to_all | solution.py:506
  70.5 13.4 %collective-permute-start.7 = (f32[30,512]{1,0:T(8,128)S(1)}, f32[30,512]{1,0:T(8,128)S(1)}, u32[]{:S(2)}, u32[]{:S(2)}) collective-permute-start(f32[30,512]{1,0:T(8,128)S(1)} %get-tuple-element.102), channel_id=1, source_target_pairs={{0,1},{1,2},{2,3},{3,4},{4,5},{5,6},{6,7},{7,8},{8,9},{9,10},{10,1... | collective-permute-start | bytes 184328 | tf_op jit(solution)/shard_map/ppermute | solution.py:507
  74.3 9.6 %collective-permute-start.8 = (f32[20,512]{1,0:T(8,128)S(1)}, f32[20,512]{1,0:T(8,128)S(1)}, u32[]{:S(2)}, u32[]{:S(2)}) collective-permute-start(f32[20,512]{1,0:T(8,128)S(1)} %get-tuple-element.103), channel_id=1, source_target_pairs={{1,0},{2,1},{3,2},{4,3},{5,4},{6,5},{7,6},{8,7},{9,8},{10,9},{11,1... | collective-permute-start | bytes 122888 | tf_op jit(solution)/shard_map/ppermute | solution.py:508
  87.3 1.7 %collective-permute-start.9 = (f32[16,16,256]{2,1,0:T(8,128)S(1)}, f32[16,16,256]{2,1,0:T(8,128)}, u32[]{:S(2)}, u32[]{:S(2)}) collective-permute-start(f32[16,16,256]{2,1,0:T(8,128)S(1)} %get-tuple-element.113), channel_id=1, source_target_pairs={{0,16},{1,17},{2,18},{3,19},{4,20},{5,21},{6,22},{7,23},{8,24},{9,... | collective-permute-start | bytes 786440 | tf_op jit(solution)/shard_map/ppermute | solution.py:505
  89.0 14.0 %all-to-all-start.3 = ((f32[16,16,256]{2,1,0:T(8,128)}), f32[16,16,256]{2,1,0:T(8,128)S(1)}, u32[]{:S(2)}, u32[]{:S(2)}) async-start(f32[16,16,256]{2,1,0:T(8,128)} %collective-permute-done.9), calls=%async_computation.3 | async-start | bytes 524288 | tf_op jit(solution)/shard_map/all_to_all | solution.py:506
  92.8 13.2 %collective-permute-start.10 = (f32[30,512]{1,0:T(8,128)S(1)}, f32[30,512]{1,0:T(8,128)S(1)}, u32[]{:S(2)}, u32[]{:S(2)}) collective-permute-start(f32[30,512]{1,0:T(8,128)S(1)} %get-tuple-element.116), channel_id=1, source_target_pairs={{0,1},{1,2},{2,3},{3,4},{4,5},{5,6},{6,7},{7,8},{8,9},{9,10},{10,1... | collective-permute-start | bytes 184328 | tf_op jit(solution)/shard_map/ppermute | solution.py:507
  96.7 9.4 %collective-permute-start.11 = (f32[20,512]{1,0:T(8,128)S(1)}, f32[20,512]{1,0:T(8,128)S(1)}, u32[]{:S(2)}, u32[]{:S(2)}) collective-permute-start(f32[20,512]{1,0:T(8,128)S(1)} %get-tuple-element.117), channel_id=1, source_target_pairs={{1,0},{2,1},{3,2},{4,3},{5,4},{6,5},{7,6},{8,7},{9,8},{10,9},{11,1... | collective-permute-start | bytes 122888 | tf_op jit(solution)/shard_map/ppermute | solution.py:508
